TPU v7x, 32 devices: a whole 2x2x4 slice. The times are simulated.
32 devices in a mesh: fsdp: 2 (over x), heads: 4 (over y, core), tensor: 4 (over z).
Axes of the slice: x: 2, y: 2, z: 4, core: 2. Of those that a mesh axis runs over, the one named last changes fastest.
Arguments:
- inputs: bfloat16 [16, 1024, 1024], P(('fsdp', 'tensor'), 'heads')
- slot_flag: int32 [16], P(('fsdp', 'tensor')), may hold values from 0 to 1, as said below
- cotangent: bfloat16 [16, 1024, 1024], P(('fsdp', 'tensor'), 'heads'), may hold values from -6 to 6
- first_gain: bfloat16 [1024], P(('fsdp', 'heads', 'tensor')), may hold values from 0.5 to 1.5
- first_shift: bfloat16 [1024], P(('fsdp', 'heads', 'tensor')), may hold values from -1.25 to 1.25
- query_weight: bfloat16 [1024, 1024], P(('fsdp', 'heads', 'tensor')), may hold values from -0.25 to 0.25
- query_bias: bfloat16 [1024], P(('fsdp', 'heads', 'tensor')), may hold values from -1.75 to 1.75
- key_weight: bfloat16 [1024, 1024], P(('fsdp', 'heads', 'tensor')), may hold values from -0.1875 to 0.1875
- value_weight: bfloat16 [1024, 1024], P(('fsdp', 'heads', 'tensor')), may hold values from -0.1875 to 0.1875
- value_bias: bfloat16 [1024], P(('fsdp', 'heads', 'tensor')), may hold values from -0.3125 to 0.3125
- out_weight: bfloat16 [1024, 1024], P(('fsdp', 'heads', 'tensor')), may hold values from -1.5 to 1.5
- out_bias: bfloat16 [1024], P(('fsdp', 'heads', 'tensor')), may hold values from -0.625 to 0.625
- second_gain: bfloat16 [1024], P(('fsdp', 'heads', 'tensor')), may hold values from 0.5 to 1.5
- second_shift: bfloat16 [1024], P(('fsdp', 'heads', 'tensor')), may hold values from -1.25 to 1.25
- gate_weight: bfloat16 [1024, 2736], P(('fsdp', 'heads'), 'tensor'), may hold values from -0.1875 to 0.1875
- gate_bias: bfloat16 [2736], P('tensor'), may hold values from -1.75 to 1.75
- up_weight: bfloat16 [1024, 2736], P(('fsdp', 'heads'), 'tensor'), may hold values from -0.1875 to 0.1875
- up_bias: bfloat16 [2736], P('tensor'), may hold values from -1.75 to 1.75
- inner_gain: bfloat16 [2736], P('tensor'), may hold values from 0.5 to 1.5
- inner_shift: bfloat16 [2736], P('tensor'), may hold values from -1.25 to 1.25
- down_weight: bfloat16 [2736, 1024], P('tensor', ('fsdp', 'heads')), may hold values from -0.109375 to 0.109375
- down_bias: bfloat16 [1024], P(('fsdp', 'heads', 'tensor')), may hold values from -0.625 to 0.625
Outputs:
- output: bfloat16 [16, 1024, 1024], P(('fsdp', 'tensor'), 'heads')
- input_grad: bfloat16 [16, 1024, 1024], P(('fsdp', 'tensor'), 'heads')
- first_gain_grad: float32 [1024], P(('fsdp', 'heads', 'tensor'))
- first_shift_grad: float32 [1024], P(('fsdp', 'heads', 'tensor'))
- query_weight_grad: float32 [1024, 1024], P(('fsdp', 'heads', 'tensor'))
- query_bias_grad: float32 [1024], P(('fsdp', 'heads', 'tensor'))
- key_weight_grad: float32 [1024, 1024], P(('fsdp', 'heads', 'tensor'))
- value_weight_grad: float32 [1024, 1024], P(('fsdp', 'heads', 'tensor'))
- value_bias_grad: float32 [1024], P(('fsdp', 'heads', 'tensor'))
- out_weight_grad: float32 [1024, 1024], P(('fsdp', 'heads', 'tensor'))
- out_bias_grad: float32 [1024], P(('fsdp', 'heads', 'tensor'))
- second_gain_grad: float32 [1024], P(('fsdp', 'heads', 'tensor'))
- second_shift_grad: float32 [1024], P(('fsdp', 'heads', 'tensor'))
- gate_weight_grad: float32 [1024, 2736], P(('fsdp', 'heads'), 'tensor')
- gate_bias_grad: float32 [2736], P('tensor')
- up_weight_grad: float32 [1024, 2736], P(('fsdp', 'heads'), 'tensor')
- up_bias_grad: float32 [2736], P('tensor')
- inner_gain_grad: float32 [2736], P('tensor')
- inner_shift_grad: float32 [2736], P('tensor')
- down_weight_grad: float32 [2736, 1024], P('tensor', ('fsdp', 'heads'))
- down_bias_grad: float32 [1024], P(('fsdp', 'heads', 'tensor'))
Inputs may be any that keep to these rules, and one draw needn't show every extreme that they name: `slot_flag`: exactly one of the 16 image slots has flag 0; all others have flag 1.
All inputs are finite; a program needn't handle non-finite values.
Results may differ from a plain program's by a relative error of at most 0.017.
Values may be sent and summed in bfloat16 or wider, within the bound.
A program may use at most 192 MiB of HBM per device.

v0:
```python
import math

import jax
import jax.numpy as jnp
from jax import lax
from jax.experimental import pallas as pl
from jax.experimental.pallas import tpu as pltpu
from jax.sharding import PartitionSpec as P

HD = 64
PAIR = 2 * HD
FF_REAL = 2730
GRID = 32


norm_eps = 1e-06


def layer_norm(values, gain_vec, shift_vec):
    row_mean = jnp.mean(values, axis=-1, keepdims=True)
    centered = values - row_mean
    row_var = jnp.mean(centered * centered, axis=-1, keepdims=True)
    inv_std = lax.rsqrt(row_var + norm_eps)
    unit_rows = centered * inv_std
    return (unit_rows * gain_vec + shift_vec, unit_rows, inv_std)


def norm_backward(grad_values, unit_rows, inv_std, gain_vec):
    scaled = grad_values * gain_vec
    centered = scaled - jnp.mean(scaled, axis=-1, keepdims=True)
    centered = centered - unit_rows * jnp.mean(scaled * unit_rows, axis=-1, keepdims=True)
    return centered * inv_std


def rope_tables():
    positions = jnp.arange(GRID * GRID, dtype=jnp.int32)
    row_place = (positions // GRID).astype(jnp.float32)
    col_place = (positions % GRID).astype(jnp.float32)
    quarter = HD // 4
    frequency = jnp.power(10000.0, -jnp.arange(quarter, dtype=jnp.float32) / quarter)
    angles = jnp.concatenate(
        [row_place[:, None] * frequency[None, :], col_place[:, None] * frequency[None, :]], axis=1
    )
    angles = jnp.repeat(angles, 2, axis=1)
    return (jnp.cos(angles), jnp.sin(angles))


def pair_swap(values):
    count = values.shape[-1]
    lanes = lax.broadcasted_iota(jnp.int32, values.shape, 1)
    following = pltpu.roll(values, count - 1, 1)
    preceding = pltpu.roll(values, 1, 1)
    return jnp.where(lanes % 2 == 0, -following, preceding)


def rotate(values, cosine_table, sine_table):
    return values * cosine_table + pair_swap(values) * sine_table


def rotate_back(grad_values, cosine_table, sine_table):
    return grad_values * cosine_table - pair_swap(grad_values * sine_table)


def outer_product(left_rows, right_rows):
    return lax.dot_general(
        left_rows, right_rows, (((0,), (0,)), ((), ())), preferred_element_type=jnp.float32
    )


def times_transpose(left_rows, right_rows):
    return lax.dot_general(
        left_rows, right_rows, (((1,), (1,)), ((), ())), preferred_element_type=jnp.float32
    )


def gather_rows(block_values):
    return lax.all_gather(block_values, "tensor", axis=0, tiled=True)


def tensor_sums(first_sum, second_sum):
    both = lax.psum(jnp.stack([first_sum, second_sum]).astype(jnp.bfloat16), "tensor")
    return (both[0].astype(jnp.float32), both[1].astype(jnp.float32))


def scatter_rows(term_fn, row_total):
    return lax.psum_scatter(
        term_fn(jnp.int32(0), row_total * lax.axis_size("tensor")).astype(jnp.bfloat16),
        "tensor",
        scatter_dimension=0,
        tiled=True,
    ).astype(jnp.float32)


def head_masks(axis):
    shape = (1, PAIR) if axis == 1 else (PAIR, 1)
    place = lax.broadcasted_iota(jnp.int32, shape, axis)
    first = (place < HD).astype(jnp.float32)
    return (first, 1.0 - first)


def load_heads(qkv_ref, cosine_ref, sine_ref, query_s, key_s, value_s):
    rows = qkv_ref[...].reshape(query_s.shape[0], 3 * PAIR)
    cosine, sine = cosine_ref[...], sine_ref[...]
    query_rot = rotate(rows[:, :PAIR].astype(jnp.float32), cosine, sine).astype(jnp.bfloat16)
    query_s[...] = (query_rot.astype(jnp.float32) * (1.0 / math.sqrt(HD))).astype(jnp.bfloat16)
    key_rot = rotate(rows[:, PAIR : 2 * PAIR].astype(jnp.float32), cosine, sine)
    key_s[...] = key_rot.astype(jnp.bfloat16)
    value_s[...] = rows[:, 2 * PAIR :]


def forward_kernel(qkv_ref, cosine_ref, sine_ref, mixed_ref, query_s, key_s, value_s):
    load_heads(qkv_ref, cosine_ref, sine_ref, query_s, key_s, value_s)
    pieces, _, piece_len, _ = mixed_ref.shape
    masks = head_masks(1)

    def one_piece(piece, carry):
        start = pl.multiple_of(piece * piece_len, piece_len)
        query_rows = query_s[pl.ds(start, piece_len), :]
        mixed = jnp.zeros((piece_len, PAIR), jnp.float32)
        for mask in masks:
            own_query = query_rows * mask.astype(jnp.bfloat16)
            scores = times_transpose(own_query, key_s[...])
            weights_exp = jnp.exp(scores - jnp.max(scores, axis=-1, keepdims=True))
            inverse = 1.0 / jnp.sum(weights_exp, axis=-1, keepdims=True)
            probs_low = (weights_exp * inverse).astype(jnp.bfloat16)
            part = jnp.dot(probs_low, value_s[...], preferred_element_type=jnp.float32)
            mixed = mixed + part * mask
        mixed_ref[piece, 0] = mixed.astype(jnp.bfloat16)
        return carry

    lax.fori_loop(0, pieces, one_piece, 0)


def backward_kernel(
    qkv_ref, grad_ref, cosine_ref, sine_ref, out_ref,
    query_s, key_s, value_s, turned_s, key_grad_s, value_grad_s,
):
    load_heads(qkv_ref, cosine_ref, sine_ref, query_s, key_s, value_s)
    pieces, _, piece_len, _ = grad_ref.shape
    turned_s[...] = key_s[...].astype(jnp.float32).T.astype(jnp.bfloat16)
    key_grad_s[...] = jnp.zeros_like(key_grad_s)
    value_grad_s[...] = jnp.zeros_like(value_grad_s)
    row_masks = head_masks(1)
    column_masks = head_masks(0)

    def one_piece(piece, carry):
        start = pl.multiple_of(piece * piece_len, piece_len)
        rows = pl.ds(start, piece_len)
        query_rows = query_s[rows, :]
        grad_rows = grad_ref[piece, 0]
        query_grad = jnp.zeros((PAIR, piece_len), jnp.float32)
        for mask, column_mask in zip(row_masks, column_masks):
            own_query = query_rows * mask.astype(jnp.bfloat16)
            own_grad = grad_rows * mask.astype(jnp.bfloat16)
            scores = times_transpose(key_s[...], own_query)
            weights_exp = jnp.exp(scores - jnp.max(scores, axis=0, keepdims=True))
            probs = weights_exp * (1.0 / jnp.sum(weights_exp, axis=0, keepdims=True))
            grad_probs = times_transpose(value_s[...], own_grad)
            row_dot = jnp.sum(grad_probs * probs, axis=0, keepdims=True)
            grad_scores = (probs * (grad_probs - row_dot)).astype(jnp.bfloat16)
            value_grad_s[...] += jnp.dot(
                probs.astype(jnp.bfloat16), own_grad, preferred_element_type=jnp.float32
            )
            key_grad_s[...] += jnp.dot(grad_scores, own_query, preferred_element_type=jnp.float32)
            own_turned = turned_s[...] * column_mask.astype(jnp.bfloat16)
            query_grad = query_grad + jnp.dot(
                own_turned, grad_scores, preferred_element_type=jnp.float32
            )
        query_grad = query_grad.T * (1.0 / math.sqrt(HD))
        turned = rotate_back(query_grad, cosine_ref[rows, :], sine_ref[rows, :])
        out_ref[piece, 0, :, :PAIR] = turned.astype(jnp.bfloat16)
        return carry

    lax.fori_loop(0, pieces, one_piece, 0)
    piece_shape = (pieces, 1, piece_len, PAIR)
    key_grad = rotate_back(key_grad_s[...], cosine_ref[...], sine_ref[...])
    out_ref[:, :, :, PAIR : 2 * PAIR] = key_grad.astype(jnp.bfloat16).reshape(piece_shape)
    out_ref[:, :, :, 2 * PAIR :] = value_grad_s[...].astype(jnp.bfloat16).reshape(piece_shape)


def attention_call(kernel, name, qkv, extra, tables, out_lanes, more_scratch, products):
    pieces, seq_count, piece_len, lanes = qkv.shape
    pair_count = lanes // (3 * PAIR)
    length = pieces * piece_len

    def per_pair(wide):
        return pl.BlockSpec((pieces, 1, piece_len, wide), lambda seq, pair: (0, seq, 0, pair))

    table_spec = pl.BlockSpec((length, PAIR), lambda seq, pair: (0, 0))
    blocks = seq_count * pair_count
    return pl.pallas_call(
        kernel,
        name=name,
        grid=(seq_count, pair_count),
        in_specs=[per_pair(3 * PAIR)] + [per_pair(PAIR)] * len(extra) + [table_spec] * 2,
        out_specs=per_pair(out_lanes),
        out_shape=jax.ShapeDtypeStruct(
            (pieces, seq_count, piece_len, pair_count * out_lanes), jnp.bfloat16
        ),
        scratch_shapes=[pltpu.VMEM((length, PAIR), jnp.bfloat16)] * 3 + more_scratch,
        compiler_params=pltpu.CompilerParams(vmem_limit_bytes=48 << 20),
        cost_estimate=pl.CostEstimate(
            flops=blocks * products * 4 * length * length * PAIR,
            bytes_accessed=blocks * length * PAIR * 16,
            transcendentals=blocks * 2 * length * length,
        ),
    )(qkv, *extra, *tables)


def attend_forward(qkv, tables):
    return attention_call(forward_kernel, "attend_forward", qkv, (), tables, PAIR, [], 2)


def attend_backward(qkv, grad_mixed, tables):
    length = qkv.shape[0] * qkv.shape[2]
    more = [
        pltpu.VMEM((PAIR, length), jnp.bfloat16),
        pltpu.VMEM((length, PAIR), jnp.float32),
        pltpu.VMEM((length, PAIR), jnp.float32),
    ]
    return attention_call(
        backward_kernel, "attend_backward", qkv, (grad_mixed,), tables, 3 * PAIR, more, 5
    )


def hidden_forward(token_rows, gate_part, up_part, gate_shift, up_shift, unit_mask):
    gate_pre = jnp.dot(token_rows, gate_part, preferred_element_type=jnp.float32) + gate_shift
    up_pre = jnp.dot(token_rows, up_part, preferred_element_type=jnp.float32) + up_shift
    return (gate_pre, up_pre, jax.nn.silu(gate_pre) * up_pre * unit_mask)


def inner_normalize(hidden, first_sum, second_sum, inner_scale, inner_offset, unit_mask):
    unit_mean = first_sum[:, None] / FF_REAL
    unit_var = second_sum[:, None] / FF_REAL - unit_mean * unit_mean
    inv_std = lax.rsqrt(unit_var + norm_eps)
    unit_hidden = (hidden - unit_mean) * inv_std
    normed = ((unit_hidden * inner_scale + inner_offset) * unit_mask).astype(jnp.bfloat16)
    return (normed, unit_hidden, inv_std)


def hidden_backward_terms(grad_normed, unit_hidden, inner_scale, unit_mask):
    scaled = grad_normed * unit_mask * inner_scale
    return (scaled, jnp.sum(scaled, axis=-1), jnp.sum(scaled * unit_hidden, axis=-1))


def gate_grads(scaled, scaled_sum, cross_sum, unit_hidden, inv_std, gate_pre, up_pre, unit_mask):
    grad_hidden = (
        unit_mask
        * (scaled - scaled_sum[:, None] / FF_REAL - unit_hidden * cross_sum[:, None] / FF_REAL)
        * inv_std
    )
    sigmoid_gate = jax.nn.sigmoid(gate_pre)
    grad_gate = (
        grad_hidden * up_pre * sigmoid_gate * (1.0 + gate_pre * (1.0 - sigmoid_gate))
    ).astype(jnp.bfloat16)
    grad_up = (grad_hidden * gate_pre * sigmoid_gate).astype(jnp.bfloat16)
    return (grad_gate, grad_up)


def vector_sums(grad_gate, grad_up, grad_normed, unit_hidden, unit_mask):
    return (
        jnp.sum(grad_gate, axis=0, dtype=jnp.float32),
        jnp.sum(grad_up, axis=0, dtype=jnp.float32),
        jnp.sum(grad_normed * unit_mask * unit_hidden, axis=0),
        jnp.sum(grad_normed * unit_mask, axis=0),
    )


def on_device(
    inputs,
    slot_flag,
    cotangent,
    first_gain,
    first_shift,
    query_weight,
    query_bias,
    key_weight,
    value_weight,
    value_bias,
    out_weight,
    out_bias,
    second_gain,
    second_shift,
    gate_weight,
    gate_bias,
    up_weight,
    up_bias,
    inner_gain,
    inner_shift,
    down_weight,
    down_bias,
):
    seq_local, piece_len, width = inputs.shape
    head_ways = lax.axis_size("heads")
    seq_len = piece_len * head_ways
    group_width = width // head_ways
    group_pairs = group_width // PAIR
    token_count = seq_local * piece_len
    fsdp_ways, tensor_ways = lax.axis_size("fsdp"), lax.axis_size("tensor")
    row_part = query_weight.shape[0]
    group_index = lax.axis_index("heads")
    inputs_group = lax.all_gather(inputs, "heads", axis=0, tiled=True)
    stacked = jnp.stack(
        [
            member.reshape(row_part, head_ways, group_pairs, PAIR)
            for member in (query_weight, key_weight, value_weight)
        ],
        axis=3,
    ).reshape(row_part, head_ways, 3 * group_width)
    own_columns = lax.all_to_all(
        stacked.transpose(1, 0, 2), "heads", split_axis=0, concat_axis=0, tiled=True
    )
    qkv_part = lax.all_gather(
        own_columns.reshape(head_ways * row_part, 3 * group_width),
        ("fsdp", "tensor"),
        axis=0,
        tiled=True,
    )
    qkv_part = (
        qkv_part.reshape(fsdp_ways, tensor_ways, head_ways, row_part, 3 * group_width)
        .transpose(0, 2, 1, 3, 4)
        .reshape(width, 3 * group_width)
    )
    out_full = lax.all_gather(out_weight, ("fsdp", "heads", "tensor"), axis=0, tiled=True)
    gathered = tuple(
        lax.all_gather(member, ("fsdp", "heads", "tensor"), axis=0, tiled=True)
        for member in (
            first_gain,
            first_shift,
            query_bias,
            value_bias,
            out_bias,
            second_gain,
            second_shift,
            down_bias,
        )
    )
    gain_one, shift_one, query_shift, value_shift, out_shift, gain_two, shift_two, down_shift = [
        member.astype(jnp.float32) for member in gathered
    ]
    gate_part, up_part, down_part = (
        lax.all_gather(gate_weight, ("fsdp", "heads"), axis=0, tiled=True),
        lax.all_gather(up_weight, ("fsdp", "heads"), axis=0, tiled=True),
        lax.all_gather(down_weight, ("fsdp", "heads"), axis=1, tiled=True),
    )
    inputs_f = inputs.astype(jnp.float32)
    _, unit_one, inv_one = layer_norm(inputs_f, gain_one, shift_one)
    normed_group, _, _ = layer_norm(
        inputs_group.reshape(-1, width).astype(jnp.float32), gain_one, shift_one
    )
    low_one = normed_group.astype(jnp.bfloat16)

    def group_lanes(full_vec):
        own = lax.dynamic_slice_in_dim(full_vec, group_index * group_width, group_width, 0)
        return own.reshape(group_pairs, PAIR)

    query_lanes, value_lanes = group_lanes(query_shift), group_lanes(value_shift)
    qkv_shift = jnp.stack([query_lanes, jnp.zeros_like(query_lanes), value_lanes], axis=1)
    qkv_lin = (
        (jnp.dot(low_one, qkv_part, preferred_element_type=jnp.float32) + qkv_shift.reshape(-1))
        .astype(jnp.bfloat16)
        .reshape(head_ways, seq_local, piece_len, 3 * group_width)
    )
    tables = tuple(jnp.tile(table, (1, PAIR // HD)) for table in rope_tables())
    mixed_heads = attend_forward(qkv_lin, tables)
    mixed_parts = lax.all_to_all(mixed_heads, "heads", split_axis=0, concat_axis=0, tiled=True)
    mixed_flat = mixed_parts.transpose(1, 2, 0, 3).reshape(token_count, width)
    residual = inputs_f + (
        jnp.dot(mixed_flat, out_full, preferred_element_type=jnp.float32) + out_shift
    ).reshape(inputs.shape)
    normed_two, unit_two, inv_two = layer_norm(residual, gain_two, shift_two)
    low_two = normed_two.astype(jnp.bfloat16)
    flag_rows = slot_flag.astype(jnp.float32)[:, None, None]
    grad_total = flag_rows * cotangent.astype(jnp.float32)
    grad_branch = grad_total.astype(jnp.bfloat16)
    down_shift_grad = jnp.sum(grad_branch.reshape(token_count, width), axis=0, dtype=jnp.float32)
    ffn_local = gate_part.shape[1]
    token_rows3 = gather_rows(low_two)
    token_rows = token_rows3.reshape(-1, width)
    col_index = lax.axis_index("tensor") * ffn_local + jnp.arange(ffn_local, dtype=jnp.int32)
    unit_mask = (col_index < FF_REAL).astype(jnp.float32)
    gate_pre, up_pre, hidden = hidden_forward(
        token_rows,
        gate_part,
        up_part,
        gate_bias.astype(jnp.float32),
        up_bias.astype(jnp.float32),
        unit_mask,
    )
    first_sum, second_sum = tensor_sums(jnp.sum(hidden, axis=-1), jnp.sum(hidden * hidden, axis=-1))
    inner_scale = inner_gain.astype(jnp.float32)
    normed_hidden, unit_hidden, inv_hidden = inner_normalize(
        hidden, first_sum, second_sum, inner_scale, inner_shift.astype(jnp.float32), unit_mask
    )
    hidden_seqs = normed_hidden.reshape(token_rows3.shape[0], piece_len, ffn_local)

    def down_term(row_start, row_count):
        picked = hidden_seqs.reshape(-1, ffn_local)
        return jnp.dot(picked, down_part, preferred_element_type=jnp.float32).reshape(
            row_count, piece_len, width
        )

    branch_out = scatter_rows(down_term, seq_local)
    grad_rows = gather_rows(grad_branch).reshape(-1, width)
    down_grad = outer_product(normed_hidden, grad_rows)
    grad_normed = times_transpose(grad_rows, down_part)
    scaled, scaled_sum, cross_sum = hidden_backward_terms(
        grad_normed, unit_hidden, inner_scale, unit_mask
    )
    scaled_sum, cross_sum = tensor_sums(scaled_sum, cross_sum)
    grad_gate, grad_up = gate_grads(
        scaled, scaled_sum, cross_sum, unit_hidden, inv_hidden, gate_pre, up_pre, unit_mask
    )
    gate_grad = outer_product(token_rows, grad_gate)
    up_grad = outer_product(token_rows, grad_up)
    vector_grads = vector_sums(grad_gate, grad_up, grad_normed, unit_hidden, unit_mask)
    gate_seqs = grad_gate.reshape(-1, piece_len, ffn_local)
    up_seqs = grad_up.reshape(-1, piece_len, ffn_local)

    def input_term(row_start, row_count):
        picked_gate = gate_seqs.reshape(-1, ffn_local)
        picked_up = up_seqs.reshape(-1, ffn_local)
        summed = times_transpose(picked_gate, gate_part) + times_transpose(picked_up, up_part)
        return summed.reshape(row_count, piece_len, width)

    grad_normed_two = scatter_rows(input_term, seq_local)
    output = (flag_rows * (residual + branch_out + down_shift)).astype(jnp.bfloat16)
    gate_weight_grad, up_weight_grad, down_weight_grad = (
        lax.psum_scatter(
            gate_grad.astype(jnp.bfloat16), ("fsdp", "heads"), scatter_dimension=0, tiled=True
        ).astype(jnp.float32),
        lax.psum_scatter(
            up_grad.astype(jnp.bfloat16), ("fsdp", "heads"), scatter_dimension=0, tiled=True
        ).astype(jnp.float32),
        lax.psum_scatter(
            down_grad.astype(jnp.bfloat16), ("fsdp", "heads"), scatter_dimension=1, tiled=True
        ).astype(jnp.float32),
    )
    gate_bias_grad, up_bias_grad, inner_gain_grad, inner_shift_grad = lax.psum(
        (vector_grads[0], vector_grads[1], vector_grads[2], vector_grads[3]), ("fsdp", "heads")
    )
    grad_residual = grad_total + norm_backward(grad_normed_two, unit_two, inv_two, gain_two)
    gain_two_grad = jnp.sum((grad_normed_two * unit_two).reshape(token_count, width), axis=0)
    shift_two_grad = jnp.sum(grad_normed_two.reshape(token_count, width), axis=0)
    grad_attn = grad_residual.astype(jnp.bfloat16).reshape(token_count, width)
    out_weight_part = outer_product(mixed_flat, grad_attn)
    out_shift_grad = jnp.sum(grad_attn, axis=0, dtype=jnp.float32)
    grad_mixed = times_transpose(grad_attn, out_full).astype(jnp.bfloat16)
    grad_parts = grad_mixed.reshape(seq_local, piece_len, head_ways, group_width)
    grad_heads = lax.all_to_all(
        grad_parts.transpose(2, 0, 1, 3), "heads", split_axis=0, concat_axis=0, tiled=True
    )
    qkv_grad = attend_backward(qkv_lin, grad_heads, tables)
    qkv_grad = qkv_grad.reshape(head_ways * token_count, 3 * group_width)
    grad_normed_one = (
        lax.psum_scatter(
            times_transpose(qkv_grad, qkv_part).astype(jnp.bfloat16),
            "heads",
            scatter_dimension=0,
            tiled=True,
        )
        .astype(jnp.float32)
        .reshape(inputs.shape)
    )
    qkv_weight_part = (
        outer_product(low_one, qkv_grad)
        .astype(jnp.bfloat16)
        .reshape(fsdp_ways, head_ways, tensor_ways, row_part, 3 * group_width)
        .transpose(0, 2, 1, 3, 4)
        .reshape(width, 3 * group_width)
    )
    qkv_rows = lax.psum_scatter(
        qkv_weight_part, ("fsdp", "tensor"), scatter_dimension=0, tiled=True
    )
    qkv_columns = lax.all_to_all(qkv_rows, "heads", split_axis=0, concat_axis=0, tiled=True)
    qkv_weight_grads = (
        qkv_columns.reshape(head_ways, row_part, group_pairs, 3, PAIR)
        .transpose(3, 1, 0, 2, 4)
        .reshape(3, row_part, width)
        .astype(jnp.float32)
    )
    qkv_shift_grad = jnp.sum(qkv_grad, axis=0, dtype=jnp.float32).reshape(group_pairs, 3, PAIR)

    def place_lanes(own_lanes):
        return lax.dynamic_update_slice_in_dim(
            jnp.zeros((width,), jnp.float32), own_lanes.reshape(-1), group_index * group_width, 0
        )

    query_shift_grad = place_lanes(qkv_shift_grad[:, 0])
    value_shift_grad = place_lanes(qkv_shift_grad[:, 2])
    input_grad = (
        grad_residual + norm_backward(grad_normed_one, unit_one, inv_one, gain_one)
    ).astype(jnp.bfloat16)
    gain_one_grad = jnp.sum((grad_normed_one * unit_one).reshape(token_count, width), axis=0)
    shift_one_grad = jnp.sum(grad_normed_one.reshape(token_count, width), axis=0)
    attn_sums = (
        qkv_weight_grads[0],
        qkv_weight_grads[1],
        qkv_weight_grads[2],
        lax.psum_scatter(
            out_weight_part.astype(jnp.bfloat16),
            ("fsdp", "heads", "tensor"),
            scatter_dimension=0,
            tiled=True,
        ).astype(jnp.float32),
        lax.psum_scatter(
            gain_one_grad, ("fsdp", "heads", "tensor"), scatter_dimension=0, tiled=True
        ),
        lax.psum_scatter(
            shift_one_grad, ("fsdp", "heads", "tensor"), scatter_dimension=0, tiled=True
        ),
        lax.psum_scatter(
            query_shift_grad, ("fsdp", "heads", "tensor"), scatter_dimension=0, tiled=True
        ),
        lax.psum_scatter(
            value_shift_grad, ("fsdp", "heads", "tensor"), scatter_dimension=0, tiled=True
        ),
        lax.psum_scatter(
            out_shift_grad, ("fsdp", "heads", "tensor"), scatter_dimension=0, tiled=True
        ),
        lax.psum_scatter(
            gain_two_grad, ("fsdp", "heads", "tensor"), scatter_dimension=0, tiled=True
        ),
        lax.psum_scatter(
            shift_two_grad, ("fsdp", "heads", "tensor"), scatter_dimension=0, tiled=True
        ),
        lax.psum_scatter(
            down_shift_grad, ("fsdp", "heads", "tensor"), scatter_dimension=0, tiled=True
        ),
    )
    return (
        output,
        input_grad,
        attn_sums[4],
        attn_sums[5],
        attn_sums[0],
        attn_sums[6],
        attn_sums[1],
        attn_sums[2],
        attn_sums[7],
        attn_sums[3],
        attn_sums[8],
        attn_sums[9],
        attn_sums[10],
        gate_weight_grad,
        gate_bias_grad,
        up_weight_grad,
        up_bias_grad,
        inner_gain_grad,
        inner_shift_grad,
        down_weight_grad,
        attn_sums[11],
    )


def solution(mesh):
    return jax.shard_map(
        on_device,
        mesh=mesh,
        in_specs=(
            P(("fsdp", "tensor"), "heads", None),
            P(("fsdp", "tensor")),
            P(("fsdp", "tensor"), "heads", None),
            P(("fsdp", "heads", "tensor")),
            P(("fsdp", "heads", "tensor")),
            P(("fsdp", "heads", "tensor"), None),
            P(("fsdp", "heads", "tensor")),
            P(("fsdp", "heads", "tensor"), None),
            P(("fsdp", "heads", "tensor"), None),
            P(("fsdp", "heads", "tensor")),
            P(("fsdp", "heads", "tensor"), None),
            P(("fsdp", "heads", "tensor")),
            P(("fsdp", "heads", "tensor")),
            P(("fsdp", "heads", "tensor")),
            P(("fsdp", "heads"), "tensor"),
            P("tensor"),
            P(("fsdp", "heads"), "tensor"),
            P("tensor"),
            P("tensor"),
            P("tensor"),
            P("tensor", ("fsdp", "heads")),
            P(("fsdp", "heads", "tensor")),
        ),
        out_specs=(
            P(("fsdp", "tensor"), "heads", None),
            P(("fsdp", "tensor"), "heads", None),
            P(("fsdp", "heads", "tensor")),
            P(("fsdp", "heads", "tensor")),
            P(("fsdp", "heads", "tensor"), None),
            P(("fsdp", "heads", "tensor")),
            P(("fsdp", "heads", "tensor"), None),
            P(("fsdp", "heads", "tensor"), None),
            P(("fsdp", "heads", "tensor")),
            P(("fsdp", "heads", "tensor"), None),
            P(("fsdp", "heads", "tensor")),
            P(("fsdp", "heads", "tensor")),
            P(("fsdp", "heads", "tensor")),
            P(("fsdp", "heads"), "tensor"),
            P("tensor"),
            P(("fsdp", "heads"), "tensor"),
            P("tensor"),
            P("tensor"),
            P("tensor"),
            P("tensor", ("fsdp", "heads")),
            P(("fsdp", "heads", "tensor")),
        ),
        check_vma=False,
    )
```

profile of v0, /device:TPU:0, one launch (start us, length us, event | category | flops | bytes accessed | tf_op | source)
XLA Modules:
  0.0 994.8 jit_solution(8751190608516898587)
XLA Ops:
  10.9 9.5 all_to_all.24
  23.8 40.6 %all-reduce.18 = (bf16[1024]{0:T(1024)(128)(2,1)S(1)}, bf16[1024]{0:T(1024)(128)(2,1)S(1)}, bf16[1024]{0:T(1024)(128)(2,1)S(1)}, bf16[1024]{0:T(1024)(128)(2,1)S...) all-reduce(bf16[1024]{0:T(1024)(128)(2,1)S(1)} %dynamic-update-slic, ...), channel_id=1, replica_groups=mesh['fsdp'=2,'heads'=4,'tensor'=4] {'fsdp','heads','tensor'}, use_global_device_ids=true, to_apply=%add.1 | all-reduce | flops 8192 | bytes 32768
  68.2 31.6 %all-gather.9.cloned.1.call-done = bf16[8,256,1024]{2,1,0:T(8,128)(2,1)} async-done(((bf16[2,256,1024]{2,1,0:T(8,128)(2,1)}), bf16[8,256,1024]{2,1,0:T(8,128)(2,1)}) %all-gather.9.cloned.1.call-update) | async-done | bytes 4194320 | tf_op jit(solution)/shard_map/all_gather | solution.py:302
  99.8 3.0 convert_reduce_fusion
  106.4 3.6 add_convert_fusion.1
  110.1 25.2 %attend_forward.1 = bf16[4,2,256,256]{3,2,1,0:T(8,128)(2,1)} custom-call(bf16[4,2,256,768]{3,2,1,0:T(8,128)(2,1)S(1)} %bitcast.85, f32[1024,128]{1,0:T(8,128)S(1)} %copy.72.cosine_ref, f32[1024,128]{1,0:T(8,128)S(1)} %copy.73.sine_ref), custom_call_target="tpu_custom_call" | custom-call | flops 4294967296 | bytes 8388608 | tf_op jit(solution)/shard_map/attend_forward/pallas_call | solution.py:191
  137.0 3.6 all-to-all-start.1
  141.8 17.0 %all-to-all-done.1 = bf16[4,2,256,256]{3,2,1,0:T(8,128)(2,1)S(1)} async-done(((bf16[4,2,256,256]{3,2,1,0:T(8,128)(2,1)}), bf16[4,2,256,256]{3,2,1,0:T(8,128)(2,1)S(1)}, u32[]{:S(2)}, u32[]{:S(2)}) %all-to-all-start.1) | async-done | bytes 1048608 | tf_op jit(solution)/shard_map/all_to_all | solution.py:366
  159.8 2.0 all-gather.13.cloned.1.call-done
  161.7 2.8 convolution_add_fusion
  168.5 2.0 convert_reduce_fusion.6
  170.7 16.8 %all-gather.17.cloned.1.call-done = bf16[1024,684]{0,1:T(8,128)(2,1)} async-done(((bf16[128,684]{0,1:T(8,128)(2,1)}), bf16[1024,684]{0,1:T(8,128)(2,1)}) %all-gather.17.cloned.1.call-update) | async-done | bytes 1400848 | tf_op jit(solution)/shard_map/all_gather | solution.py:342
  187.4 82.8 %all-gather.15.cloned.1.call-done = bf16[8,256,1024]{2,1,0:T(8,128)(2,1)} async-done(((bf16[2,256,1024]{2,1,0:T(8,128)(2,1)}), bf16[8,256,1024]{2,1,0:T(8,128)(2,1)}) %all-gather.15.cloned.1.call-update) | async-done | bytes 4194320 | tf_op jit(solution)/shard_map/all_gather | solution.py:77
  270.2 8.2 fusion.49
  278.4 17.1 %all-gather.19.cloned.1.call-done = bf16[1024,684]{0,1:T(8,128)(2,1)} async-done(((bf16[128,684]{0,1:T(8,128)(2,1)}), bf16[1024,684]{0,1:T(8,128)(2,1)}) %all-gather.19.cloned.1.call-update) | async-done | bytes 1400848 | tf_op jit(solution)/shard_map/all_gather | solution.py:343
  295.5 10.6 %fusion.43 = (bf16[2048]{0:T(1024)(128)(2,1)S(1)}, bf16[2048]{0:T(1024)(128)(2,1)S(1)}, f32[2048,684]{0,1:T(8,128)}, f32[2048,684]{0,1:T(8,128)}) fusion(f32[684]{0:T(1024)S(1)} %fusion.41, f32[684]{0:T(1024)S(1)} %convert_element_type.245, f32[2048,684]{0,1:T(8,128)} %fusion.49, f32[684]{0:T(1024)S(1)} %convert_element_type.244, ...), kind=kOutput, calls=%fused_computation.115 | convolution fusion | flops 2884308992 | bytes 22421520 | tf_op jit(solution)/shard_map/dot_general | solution.py:228
  306.1 12.3 %psum.42 = bf16[2,2048]{1,0:T(2,128)(2,1)S(1)} all-reduce(bf16[2,2048]{1,0:T(2,128)(2,1)S(1)} %pad_maximum_fusion.2), channel_id=1, replica_groups=mesh['fsdp'=2,'heads'=4,'tensor'=4] {'tensor'}, use_global_device_ids=true, to_apply=%region_6.7 | all-reduce | flops 4096 | bytes 16384 | tf_op jit(solution)/shard_map/psum | solution.py:81
  318.4 4.0 all-gather.21.cloned.1.call-done
  322.5 82.9 %all-gather.23.cloned.1.call-done = bf16[8,256,1024]{2,1,0:T(8,128)(2,1)} async-done(((bf16[2,256,1024]{2,1,0:T(8,128)(2,1)}), bf16[8,256,1024]{2,1,0:T(8,128)(2,1)}) %all-gather.23.cloned.1.call-update) | async-done | bytes 4194320 | tf_op jit(solution)/shard_map/all_gather | solution.py:77
  405.4 10.7 %multiply_reduce_fusion = (f32[684]{0:T(1024)S(1)}, bf16[2048]{0:T(1024)(128)(2,1)S(1)}, bf16[2048]{0:T(1024)(128)(2,1)S(1)}, f32[684]{0:T(1024)S(1)}, f32[2048,684]{0,1:T(8,128)}) fusion(f32[2048,684]{0,1:T(8,128)} %get-tuple-element.63, f32[2048]{0:T(1024)S(1)} %add_rsqrt_fusion, f32[2048]{0:T(1024)S(1)} %bitcast.113, f32[684]{0:T(1024)S(1)} %fusion.41, ...), kind=kOutput, calls=%fused_computation.11 | convolution fusion | flops 2882906624 | bytes 16837312 | tf_op jit(solution)/shard_map/dot_general | solution.py:71
  416.2 9.1 psum.43
  425.3 12.6 %convert_reduce_fusion.2 = (f32[684]{0:T(1024)S(1)}, bf16[2048,684]{0,1:T(8,128)(2,1)S(1)}, f32[684]{0:T(1024)S(1)}, bf16[2048,684]{0,1:T(8,128)(2,1)S(1)}, bf16[2048,684]{0,1:T(8,128)(2,1)}) fusion(f32[2048,684]{0,1:T(8,128)} %fusion.49, f32[684]{0:T(1024)S(1)} %convert_element_type.244, f32[2048]{0:T(1024)S(1)} %bitcast.115, f32[2048]{0:T(1024)S(1)} %add_rsqrt_fusion, ...), kind=kLoop, calls=%fused_computation.12 | loop fusion | flops 46226088 | bytes 30870224 | tf_op jit(solution)/shard_map/reduce_sum | solution.py:263
  437.9 3.5 fusion.50
  441.5 5.3 add_convert_fusion
  447.0 7.3 convolution_convert_fusion.6
  454.3 2.5 copy.82
  456.9 7.3 convolution_convert_fusion.5
  464.2 2.6 copy.84
  466.8 55.9 %reduce-scatter.17.cloned.1.call-done = bf16[2,256,1024]{2,1,0:T(8,128)(2,1)} async-done(((bf16[8,256,1024]{2,1,0:T(8,128)(2,1)}), bf16[2,256,1024]{2,1,0:T(8,128)(2,1)}) %reduce-scatter.17.cloned.1.call-update) | async-done | bytes 1048592 | tf_op jit(solution)/shard_map/reduce_scatter | solution.py:86
  522.7 2.9 fusion.25
  531.6 3.5 all-to-all-start.2
  535.4 6.4 convolution_convert_fusion.4
  543.4 7.3 all-to-all-done.2.grad_ref
  555.0 46.3 %attend_backward.1 = bf16[4,2,256,768]{3,2,1,0:T(8,128)(2,1)S(1)} custom-call(bf16[4,2,256,768]{3,2,1,0:T(8,128)(2,1)} %bitcast.86, bf16[4,2,256,256]{3,2,1,0:T(8,128)(2,1)S(1)} %copy-done.1, f32[1024,128]{1,0:T(8,128)S(1)} %copy-done.3, f32[1024,128]{1,0:T(8,128)S(1)} %copy-done.5), custom_call_target="tpu_custom_call" | custom-call | flops 10737418240 | bytes 8388608 | tf_op jit(solution)/shard_map/attend_backward/pallas_call | solution.py:191
  601.3 3.5 convolution_convert_fusion.3
  606.2 4.2 convolution_convert_fusion.2
  610.5 6.4 convolution_convert_fusion.1
  617.2 7.8 convolution_convert_fusion
  626.2 23.6 %all-reduce.17 = (f32[684]{0:T(1024)}, f32[684]{0:T(1024)}, f32[684]{0:T(1024)}, f32[684]{0:T(1024)}) all-reduce(f32[684]{0:T(1024)S(1)} %get-tuple-element.66, f32[684]{0:T(1024)S(1)} %get-tuple-element.55, f32[684]{0:T(1024)S(1)} %get-tuple-element.21, ...), channel_id=1, replica_groups=mesh['fsdp'=2,'heads'=4,'tensor'=4] {'fsdp','heads'}, use_global_device_ids=true, to_apply=%region_36.37 | all-reduce | flops 2736 | bytes 21888 | tf_op jit(solution)/shard_map/psum | solution.py:439
  655.9 61.6 %reduce-scatter.21.cloned.1.call-done = bf16[128,768]{1,0:T(8,128)(2,1)} async-done(((bf16[1024,768]{1,0:T(8,128)(2,1)}), bf16[128,768]{1,0:T(8,128)(2,1)}) %reduce-scatter.21.cloned.1.call-update) | async-done | bytes 196624 | tf_op jit(solution)/shard_map/reduce_scatter | solution.py:472
  717.5 3.4 all-to-all-start.3
  722.5 3.6 all-to-all-done.3
  729.1 129.4 %reduce-scatter.23.cloned.1.call-done = bf16[32,1024]{1,0:T(8,128)(2,1)} async-done(((bf16[1024,1024]{1,0:T(8,128)(2,1)}), bf16[32,1024]{1,0:T(8,128)(2,1)}) %reduce-scatter.23.cloned.1.call-update) | async-done | bytes 65552 | tf_op jit(solution)/shard_map/reduce_scatter | solution.py:500
  860.0 43.3 %reduce-scatter.19.cloned.1.call-done = bf16[512,1024]{1,0:T(8,128)(2,1)} async-done(((bf16[2048,1024]{1,0:T(8,128)(2,1)}), bf16[512,1024]{1,0:T(8,128)(2,1)}) %reduce-scatter.19.cloned.1.call-update) | async-done | bytes 1048592 | tf_op jit(solution)/shard_map/reduce_scatter | solution.py:456
  905.0 2.4 fusion.19
  907.5 44.4 %all-reduce.16 = (f32[1024]{0:T(1024)S(1)}, f32[1024]{0:T(1024)S(1)}, f32[1024]{0:T(1024)S(1)}, f32[1024]{0:T(1024)S(1)}, f32[1024]{0:T(1024)S(1)}, /*index=5*/f...) all-reduce(f32[1024]{0:T(1024)S(1)} %get-tuple-element.30, ...), channel_id=5, replica_groups=mesh['fsdp'=2,'heads'=4,'tensor'=4] {'fsdp','heads','tensor'}, use_global_device_ids=true, to_apply=%region_20.21.clone | all-reduce | flops 8192 | bytes 65536
  956.6 26.7 %reduce-scatter.15.cloned.1.call-done = bf16[2,256,1024]{2,1,0:T(8,128)(2,1)} async-done(((bf16[8,256,1024]{2,1,0:T(8,128)(2,1)}), bf16[2,256,1024]{2,1,0:T(8,128)(2,1)}) %reduce-scatter.15.cloned.1.call-update) | async-done | bytes 1048592 | tf_op jit(solution)/shard_map/reduce_scatter | solution.py:86
  983.3 4.4 fusion.18
  (242 shorter events, 55.7 us)
Async XLA Ops:
  7.2 14.7 %copy-start.34 = (bf16[32]{0:T(256)(128)(2,1)S(1)}, bf16[32]{0:T(256)(128)(2,1)}, u32[]{:S(2)}) copy-start(bf16[32]{0:T(256)(128)(2,1)} %param.26) | copy-start | bytes 196
  7.2 15.0 %copy-start.35 = (bf16[32]{0:T(256)(128)(2,1)S(1)}, bf16[32]{0:T(256)(128)(2,1)}, u32[]{:S(2)}) copy-start(bf16[32]{0:T(256)(128)(2,1)} %param.25) | copy-start | bytes 196
  7.2 15.2 %copy-start.36 = (bf16[32]{0:T(256)(128)(2,1)S(1)}, bf16[32]{0:T(256)(128)(2,1)}, u32[]{:S(2)}) copy-start(bf16[32]{0:T(256)(128)(2,1)} %param.31) | copy-start | bytes 196
  7.2 15.4 %copy-start.37 = (bf16[32]{0:T(256)(128)(2,1)S(1)}, bf16[32]{0:T(256)(128)(2,1)}, u32[]{:S(2)}) copy-start(bf16[32]{0:T(256)(128)(2,1)} %param.28) | copy-start | bytes 196
  7.2 15.7 %copy-start.38 = (bf16[32]{0:T(256)(128)(2,1)S(1)}, bf16[32]{0:T(256)(128)(2,1)}, u32[]{:S(2)}) copy-start(bf16[32]{0:T(256)(128)(2,1)} %param.33) | copy-start | bytes 196
  7.2 15.9 %copy-start.39 = (bf16[32]{0:T(256)(128)(2,1)S(1)}, bf16[32]{0:T(256)(128)(2,1)}, u32[]{:S(2)}) copy-start(bf16[32]{0:T(256)(128)(2,1)} %param.35) | copy-start | bytes 196
  7.3 16.1 %copy-start.40 = (bf16[32]{0:T(256)(128)(2,1)S(1)}, bf16[32]{0:T(256)(128)(2,1)}, u32[]{:S(2)}) copy-start(bf16[32]{0:T(256)(128)(2,1)} %param.34) | copy-start | bytes 196
  7.3 16.3 %copy-start.41 = (bf16[32]{0:T(256)(128)(2,1)S(1)}, bf16[32]{0:T(256)(128)(2,1)}, u32[]{:S(2)}) copy-start(bf16[32]{0:T(256)(128)(2,1)} %param.43) | copy-start | bytes 196
  7.3 59.2 %all-gather.11.cloned.1.call-start = ((), (), s32[]{:S(2)}) async-start(), calls=%async_computation.13 | async-start | bytes 1769472 | tf_op jit(solution)/shard_map/all_gather | solution.py:313
  20.4 79.4 %all-gather.9.cloned.1.call-start = ((), (), s32[]{:S(2)}) async-start(), calls=%async_computation.12 | async-start | bytes 5242880 | tf_op jit(solution)/shard_map/all_gather | solution.py:302
  21.2 140.6 %all-gather.13.cloned.1.call-start = ((), (), s32[]{:S(2)}) async-start(), calls=%async_computation.14 | async-start | bytes 2162688 | tf_op jit(solution)/shard_map/all_gather | solution.py:324
  65.9 44.2 %copy-start.2 = (f32[1024,128]{1,0:T(8,128)}, f32[1024,128]{1,0:T(8,128)S(1)}, u32[]{:S(2)}) copy-start(f32[1024,128]{1,0:T(8,128)S(1)} %copy.72.cosine_ref) | copy-start | bytes 1572868
  66.5 43.6 %copy-start.4 = (f32[1024,128]{1,0:T(8,128)}, f32[1024,128]{1,0:T(8,128)S(1)}, u32[]{:S(2)}) copy-start(f32[1024,128]{1,0:T(8,128)S(1)} %copy.73.sine_ref) | copy-start | bytes 1572868
  68.2 38.2 %copy-start.18 = (bf16[2,4,4,32,768]{4,3,1,2,0:T(8,128)(2,1)}, bf16[2,4,4,32,768]{4,3,1,2,0:T(8,128)(2,1)S(1)}, u32[]{:S(2)}) copy-start(bf16[2,4,4,32,768]{4,3,1,2,0:T(8,128)(2,1)S(1)} %copy.71) | copy-start | bytes 4718596
  106.4 3.7 copy-start.14
  137.0 4.5 copy-start.10
  137.0 21.7 %all-to-all-start.1 = ((bf16[4,2,256,256]{3,2,1,0:T(8,128)(2,1)}), bf16[4,2,256,256]{3,2,1,0:T(8,128)(2,1)S(1)}, u32[]{:S(2)}, u32[]{:S(2)}) async-start(bf16[4,2,256,256]{3,2,1,0:T(8,128)(2,1)} %attend_forward.1), calls=%async_computation.1 | async-start | bytes 2097152 | tf_op jit(solution)/shard_map/all_to_all | solution.py:366
  140.7 46.8 %all-gather.17.cloned.1.call-start = ((), (), s32[]{:S(2)}) async-start(), calls=%async_computation.16 | async-start | bytes 1585152 | tf_op jit(solution)/shard_map/all_gather | solution.py:342
  141.2 128.9 %all-gather.15.cloned.1.call-start = ((), (), s32[]{:S(2)}) async-start(), calls=%async_computation.15 | async-start | bytes 5242880 | tf_op jit(solution)/shard_map/all_gather | solution.py:77
  141.8 22.9 %copy-start.21 = (f32[2,256]{1,0:T(2,128)}, f32[2,256]{1,0:T(2,128)S(1)}, u32[]{:S(2)}) copy-start(f32[2,256]{1,0:T(2,128)S(1)} %broadcast_multiply_fusion.5) | copy-start | bytes 6148
  159.8 4.8 copy-start.19
  165.3 360.4 %copy-start.7 = (f32[2,256,1024]{2,1,0:T(8,128)}, f32[2,256,1024]{2,1,0:T(8,128)S(1)}, u32[]{:S(2)}) copy-start(f32[2,256,1024]{2,1,0:T(8,128)S(1)} %get-tuple-element.65) | copy-start | bytes 6291460
  167.1 3.5 copy-start.28
  167.1 3.5 copy-start.29
  167.1 3.6 copy-start.30
  167.1 128.4 %all-gather.19.cloned.1.call-start = ((), (), s32[]{:S(2)}) async-start(), calls=%async_computation.17 | async-start | bytes 1585152 | tf_op jit(solution)/shard_map/all_gather | solution.py:343
  167.7 154.8 %all-gather.21.cloned.1.call-start = ((), (), s32[]{:S(2)}) async-start(), calls=%async_computation.18 | async-start | bytes 1585152 | tf_op jit(solution)/shard_map/all_gather | solution.py:344
  168.4 236.9 %all-gather.23.cloned.1.call-start = ((), (), s32[]{:S(2)}) async-start(), calls=%async_computation.20 | async-start | bytes 5242880 | tf_op jit(solution)/shard_map/all_gather | solution.py:77
  168.5 357.2 %copy-start.26 = (f32[2]{0:T(128)}, f32[2]{0:T(128)S(1)}, u32[]{:S(2)}) copy-start(f32[2]{0:T(128)S(1)} %convert_element_type.228) | copy-start | bytes 28
  170.5 352.2 %reduce-scatter.17.cloned.1.call-start = ((), (), s32[]{:S(2)}) async-start(), calls=%async_computation.21 | async-start | bytes 5242880 | tf_op jit(solution)/shard_map/reduce_scatter | solution.py:86
  425.3 12.6 %copy-start.32 = (bf16[1024,684]{0,1:T(8,128)(2,1)S(1)}, bf16[1024,684]{0,1:T(8,128)(2,1)}, u32[]{:S(2)}) copy-start(bf16[1024,684]{0,1:T(8,128)(2,1)} %all-gather.17.cloned.1.call-done) | copy-start | bytes 4202500
  437.9 3.5 copy-start.17
  437.9 3.5 copy-start.16
  437.9 3.5 copy-start.33
  446.8 203.0 %reduce-scatter.25.cloned.1.call-start = ((), (), s32[]{:S(2)}) async-start(), calls=%async_computation.25 | async-start | bytes 1769472
  456.9 194.8 %reduce-scatter.27.cloned.1.call-start = ((), (), s32[]{:S(2)}) async-start(), calls=%async_computation.26 | async-start | bytes 1769472
  525.6 4.0 copy-start.22
  525.7 4.0 copy-start.23
  531.6 19.1 %all-to-all-start.2 = ((bf16[4,2,256,256]{3,2,1,0:T(8,128)(2,1)}), bf16[4,2,256,256]{3,2,1,0:T(8,128)(2,1)S(1)}, u32[]{:S(2)}, u32[]{:S(2)}) async-start(bf16[4,2,256,256]{3,2,1,0:T(8,128)(2,1)} %bitcast.82), calls=%async_computation.4 | async-start | bytes 2097152 | tf_op jit(solution)/shard_map/all_to_all | solution.py:450
  535.1 118.4 %reduce-scatter.29.cloned.1.call-start = ((), (), s32[]{:S(2)}) async-start(), calls=%async_computation.27 | async-start | bytes 1769472
  543.3 174.1 %reduce-scatter.21.cloned.1.call-start = ((), (), s32[]{:S(2)}) async-start(), calls=%async_computation.23 | async-start | bytes 1769472 | tf_op jit(solution)/shard_map/reduce_scatter | solution.py:472
  555.0 46.3 %copy-start.15 = (bf16[8,256,1024]{2,1,0:T(8,128)(2,1)S(1)}, bf16[8,256,1024]{2,1,0:T(8,128)(2,1)}, u32[]{:S(2)}) copy-start(bf16[8,256,1024]{2,1,0:T(8,128)(2,1)} %copy-done.14) | copy-start | bytes 12582916
  606.1 252.4 %reduce-scatter.23.cloned.1.call-start = ((), (), s32[]{:S(2)}) async-start(), calls=%async_computation.24 | async-start | bytes 2162688 | tf_op jit(solution)/shard_map/reduce_scatter | solution.py:500
  610.4 292.9 %reduce-scatter.19.cloned.1.call-start = ((), (), s32[]{:S(2)}) async-start(), calls=%async_computation.22 | async-start | bytes 5242880 | tf_op jit(solution)/shard_map/reduce_scatter | solution.py:456
  616.9 366.4 %reduce-scatter.15.cloned.1.call-start = ((), (), s32[]{:S(2)}) async-start(), calls=%async_computation.19 | async-start | bytes 5242880 | tf_op jit(solution)/shard_map/reduce_scatter | solution.py:86
  655.9 249.2 %copy-start.11 = (bf16[2,256,1024]{2,1,0:T(8,128)(2,1)S(1)}, bf16[2,256,1024]{2,1,0:T(8,128)(2,1)}, u32[]{:S(2)}) copy-start(bf16[2,256,1024]{2,1,0:T(8,128)(2,1)} %param.22) | copy-start | bytes 3145732
  717.5 8.6 all-to-all-start.3
  727.5 255.9 %copy-start.8 = (f32[2,256,1024]{2,1,0:T(8,128)S(1)}, f32[2,256,1024]{2,1,0:T(8,128)}, u32[]{:S(2)}) copy-start(f32[2,256,1024]{2,1,0:T(8,128)} %copy-done.7) | copy-start | bytes 6291460
  (14 other events, 27.1 us)
Sparse Core Ops, SparseCore 0:
  20.5 44.8 all-gather.10
  67.0 32.8 all-gather.8
  102.8 58.8 all-gather.12
  163.5 23.8 all-gather.16
  189.4 80.7 all-gather.14
  271.9 23.5 all-gather.18
  297.4 25.0 all-gather.20
  324.6 80.7 all-gather.22
  446.9 75.7 reduce-scatter.16
  525.8 39.1 reduce-scatter.24
  568.3 38.3 reduce-scatter.26
  609.9 38.5 reduce-scatter.28
  651.9 65.5 reduce-scatter.20
  719.6 138.8 reduce-scatter.22
  860.9 42.3 reduce-scatter.18
  905.5 77.8 reduce-scatter.14
where the time goes:
time: 1000 us; the launch traced here: 995 us
  waiting for transfers between devices  585 us (58%)
  blocking collectives  139 us (14%)
  matrix products  88.9 us (9%)
  Pallas kernels  71.5 us (7%)
  other arithmetic  43.1 us (4%)
  local copies, waits for them, and re-layouts  38.9 us (4%)
  between operations  15.4 us (2%)
  starting transfers between devices  12 us (1%)
    all_gather x2, waiting for transfers between devices, gather_rows(): return lax.all_gather(block_values, 'tensor', axis=0, tiled=True)  166 us
    reduce_scatter x1, waiting for transfers between devices, on_device(): lax.psum_scatter(out_weight_part.astype(jnp.bfloat16), ('fsdp', 'heads',...  129 us
    unnamed x2, blocking collectives  85.1 us
    reduce_scatter x2, waiting for transfers between devices, scatter_rows(): lax.psum_scatter(term_fn(jnp.int32(0), row_total * lax.axis_size('tensor'...  82.7 us
    pallas_call x2, Pallas kernels, attention_call(): pl.pallas_call(kernel, name=name, grid=(seq_count, pair_count), in_specs=...  71.5 us
    reduce_scatter x1, waiting for transfers between devices, on_device(): lax.psum_scatter(qkv_weight_part, ('fsdp', 'tensor'), scatter_dimension=0...  61.6 us
    reduce_scatter x1, waiting for transfers between devices, on_device(): lax.psum_scatter(times_transpose(qkv_grad, qkv_part).astype(jnp.bfloat16)...  43.3 us
    all_gather x1, waiting for transfers between devices, on_device(): inputs_group = lax.all_gather(inputs, 'heads', axis=0, tiled=True)  31.6 us
  transfers between devices with their start and end apart: 19, of which 15 were waited for; matrix products, arithmetic and copies ran while one was open for 12% of the time, Pallas kernels for 7%

commit v1 on v0

--- a/solution.py
+++ b/solution.py
@@ -80,6 +80,78 @@
 def tensor_sums(first_sum, second_sum):
     both = lax.psum(jnp.stack([first_sum, second_sum]).astype(jnp.bfloat16), "tensor")
     return (both[0].astype(jnp.float32), both[1].astype(jnp.float32))
+
+
+def cube_pairs(ways, bit):
+    return [(place, place ^ (1 << bit)) for place in range(ways)]
+
+
+def cube_gather(block, axis_name):
+    ways = lax.axis_size(axis_name)
+    bits = ways.bit_length() - 1
+    index = lax.axis_index(axis_name)
+    held = block.reshape((1,) * bits + block.shape)
+    for bit in reversed(range(bits)):
+        place = bits - 1 - bit
+        other = lax.ppermute(held, axis_name, cube_pairs(ways, bit))
+        held = jnp.where(
+            (index >> bit) % 2 == 0,
+            jnp.concatenate([held, other], axis=place),
+            jnp.concatenate([other, held], axis=place),
+        )
+    return held.reshape((ways * block.shape[0],) + block.shape[1:])
+
+
+def cube_scatter(terms, axis_name):
+    ways = lax.axis_size(axis_name)
+    bits = ways.bit_length() - 1
+    index = lax.axis_index(axis_name)
+    held = terms.reshape((2,) * bits + terms.shape[1:])
+    for bit in range(bits):
+        place = bits - 1 - bit
+        mine = (index >> bit) % 2
+        kept = lax.dynamic_index_in_dim(held, mine, place, keepdims=False)
+        sent = lax.dynamic_index_in_dim(held, 1 - mine, place, keepdims=False)
+        other = lax.ppermute(sent.astype(jnp.bfloat16), axis_name, cube_pairs(ways, bit))
+        held = kept.astype(jnp.float32) + other.astype(jnp.float32)
+    return held
+
+
+def line_pairs(ways):
+    upward = [(place, place + 1) for place in range(ways - 1)]
+    return (upward, [(target, source) for source, target in upward])
+
+
+def line_gather(block, axis_name):
+    ways = lax.axis_size(axis_name)
+    upward, downward = line_pairs(ways)
+    below, above = [block], [block]
+    for _ in range(ways - 1):
+        below.append(lax.ppermute(below[-1], axis_name, upward))
+        above.append(lax.ppermute(above[-1], axis_name, downward))
+    around = jnp.stack(below[:0:-1] + [block] + above[1:])
+    picked = lax.dynamic_slice_in_dim(around, ways - 1 - lax.axis_index(axis_name), ways, 0)
+    return picked.reshape((ways * block.shape[0],) + block.shape[1:])
+
+
+def line_scatter(terms, axis_name):
+    ways = lax.axis_size(axis_name)
+    upward, downward = line_pairs(ways)
+    index = lax.axis_index(axis_name)
+
+    def term(offset):
+        place = jnp.clip(index + offset, 0, ways - 1)
+        return lax.dynamic_index_in_dim(terms, place, 0, keepdims=False).astype(jnp.float32)
+
+    total = term(0)
+    for sign, pairs in ((1, upward), (-1, downward)):
+        running = term(sign * (ways - 1))
+        for distance in range(ways - 1, 0, -1):
+            if distance < ways - 1:
+                running = term(sign * distance) + running.astype(jnp.float32)
+            running = lax.ppermute(running.astype(jnp.bfloat16), axis_name, pairs)
+        total = total + running.astype(jnp.float32)
+    return total
 
 
 def scatter_rows(term_fn, row_total):
@@ -299,7 +371,11 @@
     fsdp_ways, tensor_ways = lax.axis_size("fsdp"), lax.axis_size("tensor")
     row_part = query_weight.shape[0]
     group_index = lax.axis_index("heads")
-    inputs_group = lax.all_gather(inputs, "heads", axis=0, tiled=True)
+    inputs_group = cube_gather(inputs, "heads")
+    grad_flags = slot_flag.astype(jnp.float32)[:, None, None]
+    grad_total = grad_flags * cotangent.astype(jnp.float32)
+    grad_branch = grad_total.astype(jnp.bfloat16)
+    grad_rows = line_gather(grad_branch, "tensor").reshape(-1, width)
     stacked = jnp.stack(
         [
             member.reshape(row_part, head_ways, group_pairs, PAIR)
@@ -307,24 +383,8 @@
         ],
         axis=3,
     ).reshape(row_part, head_ways, 3 * group_width)
-    own_columns = lax.all_to_all(
-        stacked.transpose(1, 0, 2), "heads", split_axis=0, concat_axis=0, tiled=True
-    )
-    qkv_part = lax.all_gather(
-        own_columns.reshape(head_ways * row_part, 3 * group_width),
-        ("fsdp", "tensor"),
-        axis=0,
-        tiled=True,
-    )
-    qkv_part = (
-        qkv_part.reshape(fsdp_ways, tensor_ways, head_ways, row_part, 3 * group_width)
-        .transpose(0, 2, 1, 3, 4)
-        .reshape(width, 3 * group_width)
-    )
-    out_full = lax.all_gather(out_weight, ("fsdp", "heads", "tensor"), axis=0, tiled=True)
-    gathered = tuple(
-        lax.all_gather(member, ("fsdp", "heads", "tensor"), axis=0, tiled=True)
-        for member in (
+    vectors = jnp.concatenate(
+        [
             first_gain,
             first_shift,
             query_bias,
@@ -333,8 +393,33 @@
             second_gain,
             second_shift,
             down_bias,
-        )
-    )
+        ]
+    )
+    vector_row = jnp.pad(vectors, (0, 3 * group_width - vectors.shape[0]))
+    sent_columns = jnp.concatenate(
+        [
+            stacked.transpose(1, 0, 2),
+            jnp.broadcast_to(vector_row, (head_ways, 1, 3 * group_width)),
+        ],
+        axis=1,
+    )
+    own_columns = lax.all_to_all(
+        sent_columns, "heads", split_axis=0, concat_axis=0, tiled=True
+    )
+    columns = lax.all_gather(
+        own_columns.reshape(-1, 3 * group_width), ("fsdp", "tensor"), axis=0, tiled=True
+    )
+    columns = columns.reshape(
+        fsdp_ways, tensor_ways, head_ways, row_part + 1, 3 * group_width
+    ).transpose(0, 2, 1, 3, 4)
+    qkv_part = columns[:, :, :, :row_part].reshape(width, 3 * group_width)
+    gathered = (
+        columns[:, :, :, row_part, : vectors.shape[0]]
+        .reshape(-1, 8, row_part)
+        .transpose(1, 0, 2)
+        .reshape(8, width)
+    )
+    out_full = lax.all_gather(out_weight, ("fsdp", "heads", "tensor"), axis=0, tiled=True)
     gain_one, shift_one, query_shift, value_shift, out_shift, gain_two, shift_two, down_shift = [
         member.astype(jnp.float32) for member in gathered
     ]
@@ -371,8 +456,6 @@
     normed_two, unit_two, inv_two = layer_norm(residual, gain_two, shift_two)
     low_two = normed_two.astype(jnp.bfloat16)
     flag_rows = slot_flag.astype(jnp.float32)[:, None, None]
-    grad_total = flag_rows * cotangent.astype(jnp.float32)
-    grad_branch = grad_total.astype(jnp.bfloat16)
     down_shift_grad = jnp.sum(grad_branch.reshape(token_count, width), axis=0, dtype=jnp.float32)
     ffn_local = gate_part.shape[1]
     token_rows3 = gather_rows(low_two)
@@ -400,8 +483,10 @@
             row_count, piece_len, width
         )
 
-    branch_out = scatter_rows(down_term, seq_local)
-    grad_rows = gather_rows(grad_branch).reshape(-1, width)
+    branch_terms = down_term(0, seq_local * tensor_ways).astype(jnp.bfloat16)
+    branch_out = line_scatter(
+        branch_terms.reshape((tensor_ways,) + inputs.shape), "tensor"
+    )
     down_grad = outer_product(normed_hidden, grad_rows)
     grad_normed = times_transpose(grad_rows, down_part)
     scaled, scaled_sum, cross_sum = hidden_backward_terms(
@@ -452,15 +537,9 @@
     )
     qkv_grad = attend_backward(qkv_lin, grad_heads, tables)
     qkv_grad = qkv_grad.reshape(head_ways * token_count, 3 * group_width)
-    grad_normed_one = (
-        lax.psum_scatter(
-            times_transpose(qkv_grad, qkv_part).astype(jnp.bfloat16),
-            "heads",
-            scatter_dimension=0,
-            tiled=True,
-        )
-        .astype(jnp.float32)
-        .reshape(inputs.shape)
+    group_terms = times_transpose(qkv_grad, qkv_part).astype(jnp.bfloat16)
+    grad_normed_one = cube_scatter(
+        group_terms.reshape((head_ways,) + inputs.shape), "heads"
     )
     qkv_weight_part = (
         outer_product(low_one, qkv_grad)
@@ -498,8 +577,13 @@
         qkv_weight_grads[1],
         qkv_weight_grads[2],
         lax.psum_scatter(
-            out_weight_part.astype(jnp.bfloat16),
-            ("fsdp", "heads", "tensor"),
+            lax.psum_scatter(
+                out_weight_part.astype(jnp.bfloat16),
+                ("fsdp", "heads"),
+                scatter_dimension=0,
+                tiled=True,
+            ),
+            "tensor",
             scatter_dimension=0,
             tiled=True,
         ).astype(jnp.float32),

time: 1000 us -> 900 us (0.900)
  waiting for transfers between devices: 585 us -> 368 us
  starting transfers between devices: 12 us -> 96.1 us
  local copies, waits for them, and re-layouts: 38.9 us -> 73 us
  blocking collectives: 139 us -> 118 us
  other arithmetic: 43.1 us -> 61.6 us
    ppermute x0 -> x16, waiting for transfers between devices: none -> 232 us  [the longest x6 115 us: line_scatter(): running = lax.ppermute(running.astype(jnp.bfloat16), axis_name, pairs)]
    all_gather x2 -> x1, waiting for transfers between devices: 166 us -> 0.01 us  [gather_rows(): return lax.all_gather(block_values, 'tensor', axis=0, tiled=True)]
    reduce_scatter x2, waiting for transfers between devices: 173 us -> 19.3 us  [the longest x1 19.3 us: on_device(): lax.psum_scatter(lax.psum_scatter(out_weight_part.astype(jnp.bfloat16), (...]
    ppermute x0 -> x16, starting transfers between devices: none -> 84.1 us  [the longest x3 41.5 us: line_gather(): below.append(lax.ppermute(below[-1], axis_name, upward))]
    reduce_scatter x2 -> x1, waiting for transfers between devices: 82.7 us -> 0.01 us  [scatter_rows(): lax.psum_scatter(term_fn(jnp.int32(0), row_total * lax.axis_size('tensor'...]
    unnamed x2 -> x1, blocking collectives: 85.1 us -> 40.5 us
    psum x1, blocking collectives: 23.6 us -> 46.4 us  [on_device(): lax.psum((vector_grads[0], vector_grads[1], vector_grads[2], vector_grads...]
    all_gather x1, waiting for transfers between devices: 17.1 us -> 0.01 us  [on_device(): lax.all_gather(up_weight, ('fsdp', 'heads'), axis=0, tiled=True)]
  transfers between devices with their start and end apart: 19 -> 32, of which waited for: 15 -> 17; matrix products, arithmetic and copies ran while one was open for 12% -> 17% of each run, Pallas kernels for 7% -> 8%
where the time goes in v1:
time: 900 us; the launch traced here: 889 us
  waiting for transfers between devices  368 us (41%)
  blocking collectives  118 us (13%)
  starting transfers between devices  96.1 us (11%)
  matrix products  84.9 us (9%)
  local copies, waits for them, and re-layouts  73 us (8%)
  Pallas kernels  71.5 us (8%)
  other arithmetic  61.6 us (7%)
  between operations  15.5 us (2%)
    ppermute x6, waiting for transfers between devices, line_scatter(): running = lax.ppermute(running.astype(jnp.bfloat16), axis_name, pairs)  115 us
    ppermute x3, waiting for transfers between devices, line_gather(): below.append(lax.ppermute(below[-1], axis_name, upward))  73.7 us
    pallas_call x2, Pallas kernels, attention_call(): pl.pallas_call(kernel, name=name, grid=(seq_count, pair_count), in_specs=...  71.5 us
    reduce_scatter x1, waiting for transfers between devices, on_device(): lax.psum_scatter(qkv_weight_part, ('fsdp', 'tensor'), scatter_dimension=0...  65.8 us
    psum x1, blocking collectives, on_device(): lax.psum((vector_grads[0], vector_grads[1], vector_grads[2], vector_grads...  46.4 us
    ppermute x3, starting transfers between devices, line_gather(): below.append(lax.ppermute(below[-1], axis_name, upward))  41.5 us
    unnamed x1, blocking collectives  40.5 us
    ppermute x6, starting transfers between devices, line_scatter(): running = lax.ppermute(running.astype(jnp.bfloat16), axis_name, pairs)  37.9 us
  transfers between devices with their start and end apart: 32, of which 17 were waited for; matrix products, arithmetic and copies ran while one was open for 17% of the time, Pallas kernels for 8%

profile of v1, /device:TPU:0, one launch (start us, length us, event | category | flops | bytes accessed | tf_op | source)
XLA Modules:
  0.0 889.4 jit_solution(6001771417906981674)
XLA Ops:
  10.9 5.4 concatenate.44
  16.4 9.9 %all_to_all.24 = bf16[4,33,768]{2,1,0:T(8,128)(2,1)S(1)} all-to-all(bf16[4,33,768]{2,1,0:T(8,128)(2,1)S(1)} %pad_maximum_fusion.1), channel_id=1, replica_groups=mesh['fsdp'=2,'heads'=4,'tensor'=4] {'heads'}, dimensions={0} | all-to-all | bytes 405504 | tf_op jit(solution)/shard_map/all_to_all | solution.py:406
  27.6 24.3 %collective-permute-done = bf16[1,1,2,256,1024]{4,3,2,1,0:T(8,128)(2,1)} collective-permute-done((bf16[1,1,2,256,1024]{4,3,2,1,0:T(8,128)(2,1)S(1)}, bf16[1,1,2,256,1024]{4,3,2,1,0:T(8,128)(2,1)}, u32[]{:S(2)}, u32[]{:S(2)}) %collective-permute-start) | collective-permute-done | bytes 1048608 | tf_op jit(solution)/shard_map/ppermute | solution.py:96
  57.5 15.2 %all-gather.18.cloned.1.call-done = bf16[8,132,768]{2,1,0:T(8,128)(2,1)} async-done(((bf16[1,132,768]{2,1,0:T(8,128)(2,1)}), bf16[8,132,768]{2,1,0:T(8,128)(2,1)}) %all-gather.18.cloned.1.call-update) | async-done | bytes 1622032 | tf_op jit(solution)/shard_map/all_gather | solution.py:409
  87.0 4.0 fusion.2
  91.0 4.3 fusion.5
  95.3 3.6 add_convert_fusion.1
  99.0 25.2 %attend_forward.1 = bf16[4,2,256,256]{3,2,1,0:T(8,128)(2,1)} custom-call(bf16[4,2,256,768]{3,2,1,0:T(8,128)(2,1)S(1)} %bitcast.130, f32[1024,128]{1,0:T(8,128)S(1)} %copy.81.cosine_ref, f32[1024,128]{1,0:T(8,128)S(1)} %copy.82.sine_ref), custom_call_target="tpu_custom_call" | custom-call | flops 4294967296 | bytes 8388608 | tf_op jit(solution)/shard_map/attend_forward/pallas_call | solution.py:263
  125.9 3.6 all-to-all-start.1
  131.0 14.8 %all-to-all-done.1 = bf16[4,2,256,256]{3,2,1,0:T(8,128)(2,1)S(1)} async-done(((bf16[4,2,256,256]{3,2,1,0:T(8,128)(2,1)}), bf16[4,2,256,256]{3,2,1,0:T(8,128)(2,1)S(1)}, u32[]{:S(2)}, u32[]{:S(2)}) %all-to-all-start.1) | async-done | bytes 1048608 | tf_op jit(solution)/shard_map/all_to_all | solution.py:451
  154.3 4.3 collective-permute-start.8
  160.0 34.3 %collective-permute-done.8 = bf16[2,256,1024]{2,1,0:T(8,128)(2,1)} collective-permute-done((bf16[2,256,1024]{2,1,0:T(8,128)(2,1)}, bf16[2,256,1024]{2,1,0:T(8,128)(2,1)}, u32[]{:S(2)}, u32[]{:S(2)}) %collective-permute-start.8) | collective-permute-done | bytes 1048608 | tf_op jit(solution)/shard_map/ppermute | solution.py:130
  194.3 14.3 %collective-permute-start.9 = (bf16[2,256,1024]{2,1,0:T(8,128)(2,1)}, bf16[2,256,1024]{2,1,0:T(8,128)(2,1)}, u32[]{:S(2)}, u32[]{:S(2)}) collective-permute-start(bf16[2,256,1024]{2,1,0:T(8,128)(2,1)} %collective-permute-done.8), channel_id=1, source_target_pairs={{0,1},{1,2},{2,3},{4,5},{5,6},{6,7},{8,9},{9,10},{10,11},{12,13},{... | collective-permute-start | bytes 3145736 | tf_op jit(solution)/shard_map/ppermute | solution.py:130
  208.7 17.3 %collective-permute-done.11 = bf16[2,256,1024]{2,1,0:T(8,128)(2,1)} collective-permute-done((bf16[2,256,1024]{2,1,0:T(8,128)(2,1)}, bf16[2,256,1024]{2,1,0:T(8,128)(2,1)}, u32[]{:S(2)}, u32[]{:S(2)}) %collective-permute-start.11) | collective-permute-done | bytes 1048608 | tf_op jit(solution)/shard_map/ppermute | solution.py:131
  227.3 23.2 %collective-permute-done.9 = bf16[2,256,1024]{2,1,0:T(8,128)(2,1)} collective-permute-done((bf16[2,256,1024]{2,1,0:T(8,128)(2,1)}, bf16[2,256,1024]{2,1,0:T(8,128)(2,1)}, u32[]{:S(2)}, u32[]{:S(2)}) %collective-permute-start.9) | collective-permute-done | bytes 1048608 | tf_op jit(solution)/shard_map/ppermute | solution.py:130
  250.5 22.8 %collective-permute-start.10 = (bf16[2,256,1024]{2,1,0:T(8,128)(2,1)}, bf16[2,256,1024]{2,1,0:T(8,128)(2,1)}, u32[]{:S(2)}, u32[]{:S(2)}) collective-permute-start(bf16[2,256,1024]{2,1,0:T(8,128)(2,1)} %collective-permute-done.9), channel_id=1, source_target_pairs={{0,1},{1,2},{2,3},{4,5},{5,6},{6,7},{8,9},{9,10},{10,11},{12,13},{... | collective-permute-start | bytes 3145736 | tf_op jit(solution)/shard_map/ppermute | solution.py:130
  276.5 16.2 %collective-permute-done.10 = bf16[2,256,1024]{2,1,0:T(8,128)(2,1)} collective-permute-done((bf16[2,256,1024]{2,1,0:T(8,128)(2,1)}, bf16[2,256,1024]{2,1,0:T(8,128)(2,1)}, u32[]{:S(2)}, u32[]{:S(2)}) %collective-permute-start.10) | collective-permute-done | bytes 1048608 | tf_op jit(solution)/shard_map/ppermute | solution.py:130
  303.0 8.2 fusion.67
  311.2 10.6 %fusion.61 = (bf16[2048]{0:T(1024)(128)(2,1)S(1)}, bf16[2048]{0:T(1024)(128)(2,1)S(1)}, f32[2048,684]{0,1:T(8,128)}, f32[2048,684]{0,1:T(8,128)}) fusion(f32[684]{0:T(1024)S(1)} %fusion.59, f32[684]{0:T(1024)S(1)} %convert_element_type.402, f32[2048,684]{0,1:T(8,128)} %fusion.67, f32[684]{0:T(1024)S(1)} %convert_element_type.401, ...), kind=kOutput, calls=%fused_computation.162 | convolution fusion | flops 2884308992 | bytes 22421520 | tf_op jit(solution)/shard_map/dot_general | solution.py:300
  321.8 13.1 %psum.42 = bf16[2,2048]{1,0:T(2,128)(2,1)S(1)} all-reduce(bf16[2,2048]{1,0:T(2,128)(2,1)S(1)} %pad_maximum_fusion.3), channel_id=1, replica_groups=mesh['fsdp'=2,'heads'=4,'tensor'=4] {'tensor'}, use_global_device_ids=true, to_apply=%region_6.7 | all-reduce | flops 4096 | bytes 16384 | tf_op jit(solution)/shard_map/psum | solution.py:81
  335.0 10.7 %multiply_reduce_fusion = (f32[684]{0:T(1024)S(1)}, bf16[2048]{0:T(1024)(128)(2,1)S(1)}, bf16[2048]{0:T(1024)(128)(2,1)S(1)}, f32[684]{0:T(1024)S(1)}, f32[2048,684]{0,1:T(8,128)}) fusion(f32[2048,684]{0,1:T(8,128)} %get-tuple-element.64, f32[2048]{0:T(1024)S(1)} %add_rsqrt_fusion, f32[2048]{0:T(1024)S(1)} %bitcast.168, f32[684]{0:T(1024)S(1)} %fusion.59, ...), kind=kOutput, calls=%fused_computation.11 | convolution fusion | flops 2882906624 | bytes 16837312 | tf_op jit(solution)/shard_map/dot_general | solution.py:71
  345.8 8.5 psum.43
  354.4 12.5 %convert_reduce_fusion.2 = (f32[684]{0:T(1024)S(1)}, bf16[2048,684]{0,1:T(8,128)(2,1)S(1)}, f32[684]{0:T(1024)S(1)}, bf16[2048,684]{0,1:T(8,128)(2,1)S(1)}, bf16[2048,684]{0,1:T(8,128)(2,1)}) fusion(f32[2048,684]{0,1:T(8,128)} %fusion.67, f32[684]{0:T(1024)S(1)} %convert_element_type.401, f32[2048]{0:T(1024)S(1)} %bitcast.171, f32[2048]{0:T(1024)S(1)} %add_rsqrt_fusion, ...), kind=kLoop, calls=%fused_computation.12 | loop fusion | flops 46226088 | bytes 30870224 | tf_op jit(solution)/shard_map/reduce_sum | solution.py:335
  370.5 5.3 add_convert_fusion
  376.0 5.7 convolution_convert_fusion
  385.1 4.8 collective-permute-start.2
  391.2 41.4 %collective-permute-done.2 = bf16[2,256,1024]{2,1,0:T(8,128)(2,1)} collective-permute-done((bf16[2,256,1024]{2,1,0:T(8,128)(2,1)}, bf16[2,256,1024]{2,1,0:T(8,128)(2,1)}, u32[]{:S(2)}, u32[]{:S(2)}) %collective-permute-start.2) | collective-permute-done | bytes 1048608 | tf_op jit(solution)/shard_map/ppermute | solution.py:152
  435.5 23.2 %collective-permute-start.3 = (bf16[2,256,1024]{2,1,0:T(8,128)(2,1)}, bf16[2,256,1024]{2,1,0:T(8,128)(2,1)}, u32[]{:S(2)}, u32[]{:S(2)}) collective-permute-start(bf16[2,256,1024]{2,1,0:T(8,128)(2,1)} %fusion.28), channel_id=1, source_target_pairs={{0,1},{1,2},{2,3},{4,5},{5,6},{6,7},{8,9},{9,10},{10,11},{12,13},{... | collective-permute-start | bytes 3145736 | tf_op jit(solution)/shard_map/ppermute | solution.py:152
  461.8 31.3 %collective-permute-done.3 = bf16[2,256,1024]{2,1,0:T(8,128)(2,1)} collective-permute-done((bf16[2,256,1024]{2,1,0:T(8,128)(2,1)}, bf16[2,256,1024]{2,1,0:T(8,128)(2,1)}, u32[]{:S(2)}, u32[]{:S(2)}) %collective-permute-start.3) | collective-permute-done | bytes 1048608 | tf_op jit(solution)/shard_map/ppermute | solution.py:152
  493.1 4.5 fusion.29
  498.8 6.0 collective-permute-start.4
  504.8 17.8 %collective-permute-done.6 = bf16[2,256,1024]{2,1,0:T(8,128)(2,1)} collective-permute-done((bf16[2,256,1024]{2,1,0:T(8,128)(2,1)}, bf16[2,256,1024]{2,1,0:T(8,128)(2,1)}, u32[]{:S(2)}, u32[]{:S(2)}) %collective-permute-start.6) | collective-permute-done | bytes 1048608 | tf_op jit(solution)/shard_map/ppermute | solution.py:152
  529.3 21.1 %collective-permute-done.7 = bf16[2,256,1024]{2,1,0:T(8,128)(2,1)} collective-permute-done((bf16[2,256,1024]{2,1,0:T(8,128)(2,1)}, bf16[2,256,1024]{2,1,0:T(8,128)(2,1)}, u32[]{:S(2)}, u32[]{:S(2)}) %collective-permute-start.7) | collective-permute-done | bytes 1048608 | tf_op jit(solution)/shard_map/ppermute | solution.py:152
  550.5 3.7 convert_reduce_fusion.7
  557.8 6.3 convolution_convert_fusion.4
  567.0 6.5 convolution_convert_fusion.6
  584.5 6.2 convolution_convert_fusion.5
  592.7 6.2 all-to-all-done.2.grad_ref
  603.2 46.3 %attend_backward.1 = bf16[4,2,256,768]{3,2,1,0:T(8,128)(2,1)S(1)} custom-call(bf16[4,2,256,768]{3,2,1,0:T(8,128)(2,1)} %bitcast.131, bf16[4,2,256,256]{3,2,1,0:T(8,128)(2,1)S(1)} %copy-done.1, f32[1024,128]{1,0:T(8,128)S(1)} %copy-done.3, f32[1024,128]{1,0:T(8,128)S(1)} %copy-done.5), custom_call_target="tpu_custom_call" | custom-call | flops 10737418240 | bytes 8388608 | tf_op jit(solution)/shard_map/attend_backward/pallas_call | solution.py:263
  649.5 3.7 convolution_convert_fusion.1
  656.8 5.9 convolution_convert_fusion.3
  670.6 46.4 %all-reduce.10 = (f32[684]{0:T(1024)}, f32[684]{0:T(1024)}, f32[684]{0:T(1024)}, f32[684]{0:T(1024)}) all-reduce(f32[684]{0:T(1024)S(1)} %get-tuple-element.67, f32[684]{0:T(1024)S(1)} %get-tuple-element.55, f32[684]{0:T(1024)S(1)} %get-tuple-element.21, ...), channel_id=1, replica_groups=mesh['fsdp'=2,'heads'=4,'tensor'=4] {'fsdp','heads'}, use_global_device_ids=true, to_apply=%region_35.36 | all-reduce | flops 2736 | bytes 21888 | tf_op jit(solution)/shard_map/psum | solution.py:524
  720.7 14.3 %reduce-scatter.24.cloned.1.call-done = bf16[128,684]{1,0:T(8,128)(2,1)} async-done(((bf16[1024,684]{1,0:T(8,128)(2,1)}), bf16[128,684]{1,0:T(8,128)(2,1)}) %reduce-scatter.24.cloned.1.call-update) | async-done | bytes 175120
  737.9 19.3 %reduce-scatter.20.cloned.1.call-done = bf16[32,1024]{1,0:T(8,128)(2,1)} async-done(((bf16[128,1024]{1,0:T(8,128)(2,1)}), bf16[32,1024]{1,0:T(8,128)(2,1)}) %reduce-scatter.20.cloned.1.call-update) | async-done | bytes 65552 | tf_op jit(solution)/shard_map/reduce_scatter | solution.py:579
  758.7 65.8 %reduce-scatter.16.cloned.1.call-done = bf16[128,768]{1,0:T(8,128)(2,1)} async-done(((bf16[1024,768]{1,0:T(8,128)(2,1)}), bf16[128,768]{1,0:T(8,128)(2,1)}) %reduce-scatter.16.cloned.1.call-update) | async-done | bytes 196624 | tf_op jit(solution)/shard_map/reduce_scatter | solution.py:551
  824.5 3.6 all-to-all-start.3
  828.2 3.6 fusion.19
  834.3 40.5 %all-reduce.9 = (f32[1024]{0:T(1024)S(1)}, f32[1024]{0:T(1024)S(1)}, f32[1024]{0:T(1024)S(1)}, f32[1024]{0:T(1024)S(1)}, f32[1024]{0:T(1024)S(1)}, /*index=5*/f3...) all-reduce(f32[1024]{0:T(1024)S(1)} %get-tuple-element.29, ...), channel_id=3, replica_groups=mesh['fsdp'=2,'heads'=4,'tensor'=4] {'fsdp','heads','tensor'}, use_global_device_ids=true, to_apply=%region_18.19.clone | all-reduce | flops 8192 | bytes 65536
  (268 shorter events, 127.8 us)
Async XLA Ops:
  7.2 20.0 %copy-start.9 = (bf16[2,256,1024]{2,1,0:T(8,128)(2,1)S(1)}, bf16[2,256,1024]{2,1,0:T(8,128)(2,1)}, u32[]{:S(2)}) copy-start(bf16[2,256,1024]{2,1,0:T(8,128)(2,1)} %param.22) | copy-start | bytes 3145732
  7.2 65.5 %all-gather.18.cloned.1.call-start = ((), (), s32[]{:S(2)}) async-start(), calls=%async_computation.20 | async-start | bytes 1880064 | tf_op jit(solution)/shard_map/all_gather | solution.py:409
  27.1 119.8 %all-gather.8.cloned.1.call-start = ((), (), s32[]{:S(2)}) async-start(), calls=%async_computation.11 | async-start | bytes 2162688 | tf_op jit(solution)/shard_map/all_gather | solution.py:422
  27.1 24.7 %collective-permute-start = (bf16[1,1,2,256,1024]{4,3,2,1,0:T(8,128)(2,1)S(1)}, bf16[1,1,2,256,1024]{4,3,2,1,0:T(8,128)(2,1)}, u32[]{:S(2)}, u32[]{:S(2)}) collective-permute-start(bf16[1,1,2,256,1024]{4,3,2,1,0:T(8,128)(2,1)S(1)} %bitcast.132), channel_id=1, source_target_pairs={{0,8},{4,12},{8,0},{12,4},{1,9},{5,13},{9,1},{13,5},{2,10},{6,14},... | collective-permute-start | bytes 3145736 | tf_op jit(solution)/shard_map/ppermute | solution.py:96
  53.8 29.8 %collective-permute-start.1 = (bf16[2,1,2,256,1024]{4,3,2,1,0:T(8,128)(2,1)S(1)}, bf16[2,1,2,256,1024]{4,3,2,1,0:T(8,128)(2,1)}, u32[]{:S(2)}, u32[]{:S(2)}) collective-permute-start(bf16[2,1,2,256,1024]{4,3,2,1,0:T(8,128)(2,1)S(1)} %maximum_select_fusion.1), channel_id=1, source_target_pairs={{0,4},{4,0},{8,12},{12,8},{1,5},{5,1},{9,13},{13,9},{2,6},{6,2},{1... | collective-permute-start | bytes 6291464 | tf_op jit(solution)/shard_map/ppermute | solution.py:96
  55.0 44.0 %copy-start.2 = (f32[1024,128]{1,0:T(8,128)}, f32[1024,128]{1,0:T(8,128)S(1)}, u32[]{:S(2)}) copy-start(f32[1024,128]{1,0:T(8,128)S(1)} %copy.81.cosine_ref) | copy-start | bytes 1572868
  57.4 41.6 %copy-start.4 = (f32[1024,128]{1,0:T(8,128)}, f32[1024,128]{1,0:T(8,128)S(1)}, u32[]{:S(2)}) copy-start(f32[1024,128]{1,0:T(8,128)S(1)} %copy.82.sine_ref) | copy-start | bytes 1572868
  81.3 9.7 %copy-start.30 = (f32[1024]{0:T(1024)}, f32[1024]{0:T(1024)S(1)}, u32[]{:S(2)}) copy-start(f32[1024]{0:T(1024)S(1)} %reshape.607) | copy-start | bytes 12292
  83.5 11.8 %copy-start.24 = (bf16[2,4,4,32,768]{4,3,2,1,0:T(8,128)(2,1)}, bf16[2,4,4,32,768]{4,3,2,1,0:T(8,128)(2,1)S(1)}, u32[]{:S(2)}) copy-start(bf16[2,4,4,32,768]{4,3,2,1,0:T(8,128)(2,1)S(1)} %copy.80) | copy-start | bytes 4718596
  125.9 4.7 copy-start.10
  125.9 19.9 %all-to-all-start.1 = ((bf16[4,2,256,256]{3,2,1,0:T(8,128)(2,1)}), bf16[4,2,256,256]{3,2,1,0:T(8,128)(2,1)S(1)}, u32[]{:S(2)}, u32[]{:S(2)}) async-start(bf16[4,2,256,256]{3,2,1,0:T(8,128)(2,1)} %attend_forward.1), calls=%async_computation.1 | async-start | bytes 2097152 | tf_op jit(solution)/shard_map/all_to_all | solution.py:451
  129.6 173.4 %all-gather.12.cloned.1.call-start = ((), (), s32[]{:S(2)}) async-start(), calls=%async_computation.13 | async-start | bytes 1585152 | tf_op jit(solution)/shard_map/all_gather | solution.py:427
  130.3 172.7 %all-gather.10.cloned.1.call-start = ((), (), s32[]{:S(2)}) async-start(), calls=%async_computation.12 | async-start | bytes 5242880 | tf_op jit(solution)/shard_map/all_gather | solution.py:77
  150.8 399.7 %copy-start.7 = (f32[2,256,1024]{2,1,0:T(8,128)}, f32[2,256,1024]{2,1,0:T(8,128)S(1)}, u32[]{:S(2)}) copy-start(f32[2,256,1024]{2,1,0:T(8,128)S(1)} %get-tuple-element.66) | copy-start | bytes 6291460
  151.2 122.1 %copy-start.32 = (bf16[684]{0:T(1024)(128)(2,1)S(1)}, bf16[684]{0:T(1024)(128)(2,1)}, u32[]{:S(2)}) copy-start(bf16[684]{0:T(1024)(128)(2,1)} %param.37) | copy-start | bytes 4108
  151.2 122.1 %copy-start.33 = (bf16[684]{0:T(1024)(128)(2,1)S(1)}, bf16[684]{0:T(1024)(128)(2,1)}, u32[]{:S(2)}) copy-start(bf16[684]{0:T(1024)(128)(2,1)} %param.39) | copy-start | bytes 4108
  151.2 122.2 %copy-start.34 = (bf16[684]{0:T(1024)(128)(2,1)S(1)}, bf16[684]{0:T(1024)(128)(2,1)}, u32[]{:S(2)}) copy-start(bf16[684]{0:T(1024)(128)(2,1)} %param.40) | copy-start | bytes 4108
  151.3 122.2 %copy-start.35 = (bf16[684]{0:T(1024)(128)(2,1)S(1)}, bf16[684]{0:T(1024)(128)(2,1)}, u32[]{:S(2)}) copy-start(bf16[684]{0:T(1024)(128)(2,1)} %param.41) | copy-start | bytes 4108
  152.7 158.5 %all-gather.14.cloned.1.call-start = ((), (), s32[]{:S(2)}) async-start(), calls=%async_computation.14 | async-start | bytes 1585152 | tf_op jit(solution)/shard_map/all_gather | solution.py:428
  154.3 40.0 %collective-permute-start.8 = (bf16[2,256,1024]{2,1,0:T(8,128)(2,1)}, bf16[2,256,1024]{2,1,0:T(8,128)(2,1)}, u32[]{:S(2)}, u32[]{:S(2)}) collective-permute-start(bf16[2,256,1024]{2,1,0:T(8,128)(2,1)} %get-tuple-element.60), channel_id=1, source_target_pairs={{0,1},{1,2},{2,3},{4,5},{5,6},{6,7},{8,9},{9,10},{10,11},{12,13},{... | collective-permute-start | bytes 3145736 | tf_op jit(solution)/shard_map/ppermute | solution.py:130
  158.7 176.3 %all-gather.16.cloned.1.call-start = ((), (), s32[]{:S(2)}) async-start(), calls=%async_computation.15 | async-start | bytes 1585152 | tf_op jit(solution)/shard_map/all_gather | solution.py:429
  158.7 67.3 %collective-permute-start.11 = (bf16[2,256,1024]{2,1,0:T(8,128)(2,1)}, bf16[2,256,1024]{2,1,0:T(8,128)(2,1)}, u32[]{:S(2)}, u32[]{:S(2)}) collective-permute-start(bf16[2,256,1024]{2,1,0:T(8,128)(2,1)} %get-tuple-element.60), channel_id=1, source_target_pairs={{1,0},{2,1},{3,2},{5,4},{6,5},{7,6},{9,8},{10,9},{11,10},{13,12},{... | collective-permute-start | bytes 3145736 | tf_op jit(solution)/shard_map/ppermute | solution.py:131
  194.3 56.1 %collective-permute-start.9 = (bf16[2,256,1024]{2,1,0:T(8,128)(2,1)}, bf16[2,256,1024]{2,1,0:T(8,128)(2,1)}, u32[]{:S(2)}, u32[]{:S(2)}) collective-permute-start(bf16[2,256,1024]{2,1,0:T(8,128)(2,1)} %collective-permute-done.8), channel_id=1, source_target_pairs={{0,1},{1,2},{2,3},{4,5},{5,6},{6,7},{8,9},{9,10},{10,11},{12,13},{... | collective-permute-start | bytes 3145736 | tf_op jit(solution)/shard_map/ppermute | solution.py:130
  226.0 49.2 %collective-permute-start.12 = (bf16[2,256,1024]{2,1,0:T(8,128)(2,1)}, bf16[2,256,1024]{2,1,0:T(8,128)(2,1)}, u32[]{:S(2)}, u32[]{:S(2)}) collective-permute-start(bf16[2,256,1024]{2,1,0:T(8,128)(2,1)} %collective-permute-done.11), channel_id=1, source_target_pairs={{1,0},{2,1},{3,2},{5,4},{6,5},{7,6},{9,8},{10,9},{11,10},{13,12},{... | collective-permute-start | bytes 3145736 | tf_op jit(solution)/shard_map/ppermute | solution.py:131
  250.5 42.2 %collective-permute-start.10 = (bf16[2,256,1024]{2,1,0:T(8,128)(2,1)}, bf16[2,256,1024]{2,1,0:T(8,128)(2,1)}, u32[]{:S(2)}, u32[]{:S(2)}) collective-permute-start(bf16[2,256,1024]{2,1,0:T(8,128)(2,1)} %collective-permute-done.9), channel_id=1, source_target_pairs={{0,1},{1,2},{2,3},{4,5},{5,6},{6,7},{8,9},{9,10},{10,11},{12,13},{... | collective-permute-start | bytes 3145736 | tf_op jit(solution)/shard_map/ppermute | solution.py:130
  273.3 253.7 %reduce-scatter.14.cloned.1.call-start = ((), (), s32[]{:S(2)}) async-start(), calls=%async_computation.16 | async-start | bytes 5242880 | tf_op jit(solution)/shard_map/reduce_scatter | solution.py:158
  275.2 25.3 %collective-permute-start.13 = (bf16[2,256,1024]{2,1,0:T(8,128)(2,1)}, bf16[2,256,1024]{2,1,0:T(8,128)(2,1)S(1)}, u32[]{:S(2)}, u32[]{:S(2)}) collective-permute-start(bf16[2,256,1024]{2,1,0:T(8,128)(2,1)} %collective-permute-done.12), channel_id=1, source_target_pairs={{1,0},{2,1},{3,2},{5,4},{6,5},{7,6},{9,8},{10,9},{11,10},{13,12},{... | collective-permute-start | bytes 3145736 | tf_op jit(solution)/shard_map/ppermute | solution.py:131
  354.4 12.6 %copy-start.36 = (bf16[1024,684]{0,1:T(8,128)(2,1)S(1)}, bf16[1024,684]{0,1:T(8,128)(2,1)}, u32[]{:S(2)}) copy-start(bf16[1024,684]{0,1:T(8,128)(2,1)} %all-gather.12.cloned.1.call-done) | copy-start | bytes 4202500
  375.8 281.0 %reduce-scatter.18.cloned.1.call-start = ((), (), s32[]{:S(2)}) async-start(), calls=%async_computation.18 | async-start | bytes 2359296 | tf_op jit(solution)/shard_map/reduce_scatter | solution.py:580
  385.1 47.5 %collective-permute-start.2 = (bf16[2,256,1024]{2,1,0:T(8,128)(2,1)}, bf16[2,256,1024]{2,1,0:T(8,128)(2,1)}, u32[]{:S(2)}, u32[]{:S(2)}) collective-permute-start(bf16[2,256,1024]{2,1,0:T(8,128)(2,1)} %get-tuple-element.72), channel_id=1, source_target_pairs={{0,1},{1,2},{2,3},{4,5},{5,6},{6,7},{8,9},{9,10},{10,11},{12,13},{... | collective-permute-start | bytes 3145736 | tf_op jit(solution)/shard_map/ppermute | solution.py:152
  389.9 71.8 %collective-permute-start.5 = (bf16[2,256,1024]{2,1,0:T(8,128)(2,1)}, bf16[2,256,1024]{2,1,0:T(8,128)(2,1)}, u32[]{:S(2)}, u32[]{:S(2)}) collective-permute-start(bf16[2,256,1024]{2,1,0:T(8,128)(2,1)} %get-tuple-element.73), channel_id=1, source_target_pairs={{1,0},{2,1},{3,2},{5,4},{6,5},{7,6},{9,8},{10,9},{11,10},{13,12},{... | collective-permute-start | bytes 3145736 | tf_op jit(solution)/shard_map/ppermute | solution.py:152
  435.5 57.6 %collective-permute-start.3 = (bf16[2,256,1024]{2,1,0:T(8,128)(2,1)}, bf16[2,256,1024]{2,1,0:T(8,128)(2,1)}, u32[]{:S(2)}, u32[]{:S(2)}) collective-permute-start(bf16[2,256,1024]{2,1,0:T(8,128)(2,1)} %fusion.28), channel_id=1, source_target_pairs={{0,1},{1,2},{2,3},{4,5},{5,6},{6,7},{8,9},{9,10},{10,11},{12,13},{... | collective-permute-start | bytes 3145736 | tf_op jit(solution)/shard_map/ppermute | solution.py:152
  497.5 25.1 %collective-permute-start.6 = (bf16[2,256,1024]{2,1,0:T(8,128)(2,1)}, bf16[2,256,1024]{2,1,0:T(8,128)(2,1)}, u32[]{:S(2)}, u32[]{:S(2)}) collective-permute-start(bf16[2,256,1024]{2,1,0:T(8,128)(2,1)} %get-tuple-element.71), channel_id=1, source_target_pairs={{1,0},{2,1},{3,2},{5,4},{6,5},{7,6},{9,8},{10,9},{11,10},{13,12},{... | collective-permute-start | bytes 3145736 | tf_op jit(solution)/shard_map/ppermute | solution.py:152
  498.8 30.5 %collective-permute-start.4 = (bf16[2,256,1024]{2,1,0:T(8,128)(2,1)}, bf16[2,256,1024]{2,1,0:T(8,128)(2,1)}, u32[]{:S(2)}, u32[]{:S(2)}) collective-permute-start(bf16[2,256,1024]{2,1,0:T(8,128)(2,1)} %get-tuple-element.70), channel_id=1, source_target_pairs={{0,1},{1,2},{2,3},{4,5},{5,6},{6,7},{8,9},{9,10},{10,11},{12,13},{... | collective-permute-start | bytes 3145736 | tf_op jit(solution)/shard_map/ppermute | solution.py:152
  525.6 24.9 %collective-permute-start.7 = (bf16[2,256,1024]{2,1,0:T(8,128)(2,1)}, bf16[2,256,1024]{2,1,0:T(8,128)(2,1)}, u32[]{:S(2)}, u32[]{:S(2)}) collective-permute-start(bf16[2,256,1024]{2,1,0:T(8,128)(2,1)} %fusion.27), channel_id=1, source_target_pairs={{1,0},{2,1},{3,2},{5,4},{6,5},{7,6},{9,8},{10,9},{11,10},{13,12},{... | collective-permute-start | bytes 3145736 | tf_op jit(solution)/shard_map/ppermute | solution.py:152
  527.0 23.5 %copy-start.16 = (bf16[2,256,1024]{2,1,0:T(8,128)(2,1)S(1)}, bf16[2,256,1024]{2,1,0:T(8,128)(2,1)}, u32[]{:S(2)}) copy-start(bf16[2,256,1024]{2,1,0:T(8,128)(2,1)} %reduce-scatter.14.cloned.1.call-done) | copy-start | bytes 3145732
  529.3 25.8 %copy-start.29 = (bf16[64,8,4,256]{3,1,2,0:T(8,128)(2,1)S(1)}, bf16[64,8,4,256]{3,1,2,0:T(8,128)(2,1)}, u32[]{:S(2)}) copy-start(bf16[64,8,4,256]{3,1,2,0:T(8,128)(2,1)} %copy-done.28) | copy-start | bytes 3145732
  557.8 159.2 %reduce-scatter.26.cloned.1.call-start = ((), (), s32[]{:S(2)}) async-start(), calls=%async_computation.23 | async-start | bytes 1769472
  566.9 151.9 %reduce-scatter.22.cloned.1.call-start = ((), (), s32[]{:S(2)}) async-start(), calls=%async_computation.21 | async-start | bytes 1769472
  581.0 17.9 %all-to-all-start.2 = ((bf16[4,2,256,256]{3,2,1,0:T(8,128)(2,1)}), bf16[4,2,256,256]{3,2,1,0:T(8,128)(2,1)S(1)}, u32[]{:S(2)}, u32[]{:S(2)}) async-start(bf16[4,2,256,256]{3,2,1,0:T(8,128)(2,1)} %bitcast.127), calls=%async_computation.3 | async-start | bytes 2097152 | tf_op jit(solution)/shard_map/all_to_all | solution.py:535
  584.5 150.6 %reduce-scatter.24.cloned.1.call-start = ((), (), s32[]{:S(2)}) async-start(), calls=%async_computation.22 | async-start | bytes 1769472
  592.4 164.8 %reduce-scatter.20.cloned.1.call-start = ((), (), s32[]{:S(2)}) async-start(), calls=%async_computation.19 | async-start | bytes 327680 | tf_op jit(solution)/shard_map/reduce_scatter | solution.py:579
  603.2 46.3 %copy-start.25 = (bf16[2,4,4,32,768]{4,3,2,1,0:T(8,128)(2,1)S(1)}, bf16[2,4,4,32,768]{4,3,2,1,0:T(8,128)(2,1)}, u32[]{:S(2)}) copy-start(bf16[2,4,4,32,768]{4,3,2,1,0:T(8,128)(2,1)} %copy-done.24) | copy-start | bytes 4718596
  656.7 7.3 collective-permute-start.14
  656.8 167.7 %reduce-scatter.16.cloned.1.call-start = ((), (), s32[]{:S(2)}) async-start(), calls=%async_computation.17 | async-start | bytes 1769472 | tf_op jit(solution)/shard_map/reduce_scatter | solution.py:551
  670.2 157.9 %collective-permute-start.15 = (bf16[2,256,1024]{2,1,0:T(8,128)(2,1)}, bf16[2,256,1024]{2,1,0:T(8,128)(2,1)}, u32[]{:S(2)}, u32[]{:S(2)}) collective-permute-start(bf16[2,256,1024]{2,1,0:T(8,128)(2,1)} %fusion.36), channel_id=1, source_target_pairs={{0,8},{4,12},{8,0},{12,4},{1,9},{5,13},{9,1},{13,5},{2,10},{6,14},... | collective-permute-start | bytes 3145736 | tf_op jit(solution)/shard_map/ppermute | solution.py:115
  718.8 109.3 %copy-start.31 = (f32[1024]{0:T(1024)S(1)}, f32[1024]{0:T(1024)}, u32[]{:S(2)}) copy-start(f32[1024]{0:T(1024)} %copy-done.30) | copy-start | bytes 12292
  824.5 55.0 %all-to-all-start.3 = ((bf16[4,32,768]{2,1,0:T(8,128)(2,1)}), bf16[4,32,768]{2,1,0:T(8,128)(2,1)S(1)}, u32[]{:S(2)}, u32[]{:S(2)}) async-start(bf16[4,32,768]{2,1,0:T(8,128)(2,1)} %bitcast.165), calls=%async_computation.5 | async-start | bytes 393216 | tf_op jit(solution)/shard_map/all_to_all | solution.py:554
  (23 other events, 57.3 us)
Sparse Core Ops, SparseCore 0:
  27.2 45.4 all-gather.17
  75.7 54.7 all-gather.7
  132.4 23.9 all-gather.11
  158.4 112.9 all-gather.9
  273.1 26.0 all-gather.13
  300.9 25.0 all-gather.15
  375.9 113.5 reduce-scatter.13
  557.9 45.6 reduce-scatter.17
  606.9 38.3 reduce-scatter.25
  648.5 44.8 reduce-scatter.21
  696.7 38.3 reduce-scatter.23
  737.2 19.9 reduce-scatter.19
  760.6 63.8 reduce-scatter.15

commit v2 on v1

--- a/solution.py
+++ b/solution.py
@@ -122,36 +122,42 @@
     return (upward, [(target, source) for source, target in upward])
 
 
-def line_gather(block, axis_name):
+def line_step(below, above, axis_name):
+    upward, downward = line_pairs(lax.axis_size(axis_name))
+    below.append(lax.ppermute(below[-1], axis_name, upward))
+    above.append(lax.ppermute(above[-1], axis_name, downward))
+
+
+def line_pick(below, above, axis_name):
     ways = lax.axis_size(axis_name)
-    upward, downward = line_pairs(ways)
-    below, above = [block], [block]
-    for _ in range(ways - 1):
-        below.append(lax.ppermute(below[-1], axis_name, upward))
-        above.append(lax.ppermute(above[-1], axis_name, downward))
+    block = below[0]
     around = jnp.stack(below[:0:-1] + [block] + above[1:])
     picked = lax.dynamic_slice_in_dim(around, ways - 1 - lax.axis_index(axis_name), ways, 0)
     return picked.reshape((ways * block.shape[0],) + block.shape[1:])
 
 
-def line_scatter(terms, axis_name):
+def after(value, *others):
+    return lax.optimization_barrier((value,) + others)[0]
+
+
+def line_scatter(terms, axis_name, gates):
     ways = lax.axis_size(axis_name)
-    upward, downward = line_pairs(ways)
+    pairs = line_pairs(ways)
     index = lax.axis_index(axis_name)
 
     def term(offset):
         place = jnp.clip(index + offset, 0, ways - 1)
         return lax.dynamic_index_in_dim(terms, place, 0, keepdims=False).astype(jnp.float32)
 
-    total = term(0)
-    for sign, pairs in ((1, upward), (-1, downward)):
-        running = term(sign * (ways - 1))
-        for distance in range(ways - 1, 0, -1):
-            if distance < ways - 1:
-                running = term(sign * distance) + running.astype(jnp.float32)
-            running = lax.ppermute(running.astype(jnp.bfloat16), axis_name, pairs)
-        total = total + running.astype(jnp.float32)
-    return total
+    running = [None, None]
+    for step, distance in enumerate(range(ways - 1, 0, -1)):
+        for side, sign in ((0, 1), (1, -1)):
+            total = term(sign * distance)
+            if step > 0:
+                total = total + running[side].astype(jnp.float32)
+            gated = after(total.astype(jnp.bfloat16), gates[min(step, len(gates) - 1)])
+            running[side] = lax.ppermute(gated, axis_name, pairs[side])
+    return term(0) + running[0].astype(jnp.float32) + running[1].astype(jnp.float32)
 
 
 def scatter_rows(term_fn, row_total):
@@ -375,7 +381,8 @@
     grad_flags = slot_flag.astype(jnp.float32)[:, None, None]
     grad_total = grad_flags * cotangent.astype(jnp.float32)
     grad_branch = grad_total.astype(jnp.bfloat16)
-    grad_rows = line_gather(grad_branch, "tensor").reshape(-1, width)
+    below, above = [grad_branch], [grad_branch]
+    line_step(below, above, "tensor")
     stacked = jnp.stack(
         [
             member.reshape(row_part, head_ways, group_pairs, PAIR)
@@ -419,7 +426,12 @@
         .transpose(1, 0, 2)
         .reshape(8, width)
     )
-    out_full = lax.all_gather(out_weight, ("fsdp", "heads", "tensor"), axis=0, tiled=True)
+    out_full = lax.all_gather(
+        lax.all_gather(out_weight, "tensor", axis=0, tiled=True),
+        ("fsdp", "heads"),
+        axis=0,
+        tiled=True,
+    )
     gain_one, shift_one, query_shift, value_shift, out_shift, gain_two, shift_two, down_shift = [
         member.astype(jnp.float32) for member in gathered
     ]
@@ -441,14 +453,21 @@
 
     query_lanes, value_lanes = group_lanes(query_shift), group_lanes(value_shift)
     qkv_shift = jnp.stack([query_lanes, jnp.zeros_like(query_lanes), value_lanes], axis=1)
+    low_one = after(low_one, below[-1], above[-1])
+    line_step(below, above, "tensor")
     qkv_lin = (
         (jnp.dot(low_one, qkv_part, preferred_element_type=jnp.float32) + qkv_shift.reshape(-1))
         .astype(jnp.bfloat16)
         .reshape(head_ways, seq_local, piece_len, 3 * group_width)
     )
     tables = tuple(jnp.tile(table, (1, PAIR // HD)) for table in rope_tables())
-    mixed_heads = attend_forward(qkv_lin, tables)
+    attended = after(qkv_lin, below[-1], above[-1])
+    for _ in range(tensor_ways - 3):
+        line_step(below, above, "tensor")
+    mixed_heads = attend_forward(attended, tables)
     mixed_parts = lax.all_to_all(mixed_heads, "heads", split_axis=0, concat_axis=0, tiled=True)
+    mixed_parts = after(mixed_parts, below[-1], above[-1])
+    grad_rows = line_pick(below, above, "tensor").reshape(-1, width)
     mixed_flat = mixed_parts.transpose(1, 2, 0, 3).reshape(token_count, width)
     residual = inputs_f + (
         jnp.dot(mixed_flat, out_full, preferred_element_type=jnp.float32) + out_shift
@@ -458,7 +477,7 @@
     flag_rows = slot_flag.astype(jnp.float32)[:, None, None]
     down_shift_grad = jnp.sum(grad_branch.reshape(token_count, width), axis=0, dtype=jnp.float32)
     ffn_local = gate_part.shape[1]
-    token_rows3 = gather_rows(low_two)
+    token_rows3 = gather_rows(after(low_two, gate_part, up_part))
     token_rows = token_rows3.reshape(-1, width)
     col_index = lax.axis_index("tensor") * ffn_local + jnp.arange(ffn_local, dtype=jnp.int32)
     unit_mask = (col_index < FF_REAL).astype(jnp.float32)
@@ -483,11 +502,10 @@
             row_count, piece_len, width
         )
 
-    branch_terms = down_term(0, seq_local * tensor_ways).astype(jnp.bfloat16)
-    branch_out = line_scatter(
-        branch_terms.reshape((tensor_ways,) + inputs.shape), "tensor"
-    )
     down_grad = outer_product(normed_hidden, grad_rows)
+    down_weight_grad = lax.psum_scatter(
+        down_grad.astype(jnp.bfloat16), ("fsdp", "heads"), scatter_dimension=1, tiled=True
+    )
     grad_normed = times_transpose(grad_rows, down_part)
     scaled, scaled_sum, cross_sum = hidden_backward_terms(
         grad_normed, unit_hidden, inner_scale, unit_mask
@@ -499,7 +517,7 @@
     gate_grad = outer_product(token_rows, grad_gate)
     up_grad = outer_product(token_rows, grad_up)
     vector_grads = vector_sums(grad_gate, grad_up, grad_normed, unit_hidden, unit_mask)
-    gate_seqs = grad_gate.reshape(-1, piece_len, ffn_local)
+    gate_seqs = after(grad_gate, down_weight_grad).reshape(-1, piece_len, ffn_local)
     up_seqs = grad_up.reshape(-1, piece_len, ffn_local)
 
     def input_term(row_start, row_count):
@@ -509,18 +527,15 @@
         return summed.reshape(row_count, piece_len, width)
 
     grad_normed_two = scatter_rows(input_term, seq_local)
-    output = (flag_rows * (residual + branch_out + down_shift)).astype(jnp.bfloat16)
-    gate_weight_grad, up_weight_grad, down_weight_grad = (
+    gate_weight_grad, up_weight_grad = (
         lax.psum_scatter(
             gate_grad.astype(jnp.bfloat16), ("fsdp", "heads"), scatter_dimension=0, tiled=True
         ).astype(jnp.float32),
         lax.psum_scatter(
             up_grad.astype(jnp.bfloat16), ("fsdp", "heads"), scatter_dimension=0, tiled=True
         ).astype(jnp.float32),
-        lax.psum_scatter(
-            down_grad.astype(jnp.bfloat16), ("fsdp", "heads"), scatter_dimension=1, tiled=True
-        ).astype(jnp.float32),
-    )
+    )
+    down_weight_grad = down_weight_grad.astype(jnp.float32)
     gate_bias_grad, up_bias_grad, inner_gain_grad, inner_shift_grad = lax.psum(
         (vector_grads[0], vector_grads[1], vector_grads[2], vector_grads[3]), ("fsdp", "heads")
     )
@@ -536,6 +551,13 @@
         grad_parts.transpose(2, 0, 1, 3), "heads", split_axis=0, concat_axis=0, tiled=True
     )
     qkv_grad = attend_backward(qkv_lin, grad_heads, tables)
+    branch_terms = down_term(0, seq_local * tensor_ways).astype(jnp.bfloat16)
+    branch_out = line_scatter(
+        branch_terms.reshape((tensor_ways,) + inputs.shape),
+        "tensor",
+        (grad_mixed, grad_heads, qkv_grad),
+    )
+    output = (flag_rows * (residual + branch_out + down_shift)).astype(jnp.bfloat16)
     qkv_grad = qkv_grad.reshape(head_ways * token_count, 3 * group_width)
     group_terms = times_transpose(qkv_grad, qkv_part).astype(jnp.bfloat16)
     grad_normed_one = cube_scatter(
@@ -548,16 +570,10 @@
         .transpose(0, 2, 1, 3, 4)
         .reshape(width, 3 * group_width)
     )
-    qkv_rows = lax.psum_scatter(
-        qkv_weight_part, ("fsdp", "tensor"), scatter_dimension=0, tiled=True
-    )
-    qkv_columns = lax.all_to_all(qkv_rows, "heads", split_axis=0, concat_axis=0, tiled=True)
-    qkv_weight_grads = (
-        qkv_columns.reshape(head_ways, row_part, group_pairs, 3, PAIR)
-        .transpose(3, 1, 0, 2, 4)
-        .reshape(3, row_part, width)
-        .astype(jnp.float32)
-    )
+    qkv_half = cube_scatter(
+        qkv_weight_part.reshape(fsdp_ways, -1, 3 * group_width), "fsdp"
+    ).astype(jnp.bfloat16)
+    qkv_rows = lax.psum_scatter(qkv_half, "tensor", scatter_dimension=0, tiled=True)
     qkv_shift_grad = jnp.sum(qkv_grad, axis=0, dtype=jnp.float32).reshape(group_pairs, 3, PAIR)
 
     def place_lanes(own_lanes):
@@ -572,46 +588,45 @@
     ).astype(jnp.bfloat16)
     gain_one_grad = jnp.sum((grad_normed_one * unit_one).reshape(token_count, width), axis=0)
     shift_one_grad = jnp.sum(grad_normed_one.reshape(token_count, width), axis=0)
-    attn_sums = (
-        qkv_weight_grads[0],
-        qkv_weight_grads[1],
-        qkv_weight_grads[2],
+    vector_sums_all = lax.psum(
+        jnp.stack(
+            [
+                gain_one_grad,
+                shift_one_grad,
+                query_shift_grad,
+                value_shift_grad,
+                out_shift_grad,
+                gain_two_grad,
+                shift_two_grad,
+                down_shift_grad,
+            ]
+        ),
+        ("fsdp", "heads", "tensor"),
+    )
+    device_place = (
+        lax.axis_index("fsdp") * head_ways + group_index
+    ) * tensor_ways + lax.axis_index("tensor")
+    own_sums = lax.dynamic_slice_in_dim(vector_sums_all, device_place * row_part, row_part, 1)
+    qkv_rows = after(qkv_rows, own_sums)
+    qkv_columns = lax.all_to_all(qkv_rows, "heads", split_axis=0, concat_axis=0, tiled=True)
+    qkv_weight_grads = (
+        qkv_columns.reshape(head_ways, row_part, group_pairs, 3, PAIR)
+        .transpose(3, 1, 0, 2, 4)
+        .reshape(3, row_part, width)
+        .astype(jnp.float32)
+    )
+    out_weight_grad = lax.psum_scatter(
         lax.psum_scatter(
-            lax.psum_scatter(
-                out_weight_part.astype(jnp.bfloat16),
-                ("fsdp", "heads"),
-                scatter_dimension=0,
-                tiled=True,
-            ),
-            "tensor",
+            out_weight_part.astype(jnp.bfloat16),
+            ("fsdp", "heads"),
             scatter_dimension=0,
             tiled=True,
-        ).astype(jnp.float32),
-        lax.psum_scatter(
-            gain_one_grad, ("fsdp", "heads", "tensor"), scatter_dimension=0, tiled=True
         ),
-        lax.psum_scatter(
-            shift_one_grad, ("fsdp", "heads", "tensor"), scatter_dimension=0, tiled=True
-        ),
-        lax.psum_scatter(
-            query_shift_grad, ("fsdp", "heads", "tensor"), scatter_dimension=0, tiled=True
-        ),
-        lax.psum_scatter(
-            value_shift_grad, ("fsdp", "heads", "tensor"), scatter_dimension=0, tiled=True
-        ),
-        lax.psum_scatter(
-            out_shift_grad, ("fsdp", "heads", "tensor"), scatter_dimension=0, tiled=True
-        ),
-        lax.psum_scatter(
-            gain_two_grad, ("fsdp", "heads", "tensor"), scatter_dimension=0, tiled=True
-        ),
-        lax.psum_scatter(
-            shift_two_grad, ("fsdp", "heads", "tensor"), scatter_dimension=0, tiled=True
-        ),
-        lax.psum_scatter(
-            down_shift_grad, ("fsdp", "heads", "tensor"), scatter_dimension=0, tiled=True
-        ),
-    )
+        "tensor",
+        scatter_dimension=0,
+        tiled=True,
+    ).astype(jnp.float32)
+    attn_sums = tuple(qkv_weight_grads) + (out_weight_grad,) + tuple(own_sums)
     return (
         output,
         input_grad,

time: 900 us -> 733 us (0.81)
  waiting for transfers between devices: 368 us -> 246 us
  starting transfers between devices: 96.1 us -> 52.6 us
    ppermute x12, waiting for transfers between devices: 207 us -> 41 us  [the longest x3 31.1 us: line_step(): above.append(lax.ppermute(above[-1], axis_name, downward))]
    all_gather x1, waiting for transfers between devices: 0.01 us -> 70.4 us  [gather_rows(): return lax.all_gather(block_values, 'tensor', axis=0, tiled=True)]
    reduce_scatter x1, waiting for transfers between devices: 65.8 us -> 0.01 us  [on_device(): lax.psum_scatter(qkv_half, 'tensor', scatter_dimension=0, tiled=True)]
    reduce_scatter x1, waiting for transfers between devices: 0.01 us -> 61.1 us  [scatter_rows(): lax.psum_scatter(term_fn(jnp.int32(0), row_total * lax.axis_size('tensor'...]
    psum x0 -> x1, blocking collectives: none -> 52.1 us  [on_device(): lax.psum(jnp.stack([gain_one_grad, shift_one_grad, query_shift_grad, valu...]
    ppermute x12, starting transfers between devices: 83.2 us -> 39 us  [the longest x6 18 us: line_scatter(): running[side] = lax.ppermute(gated, axis_name, pairs[side])]
    unnamed x1 -> x0, blocking collectives: 40.5 us -> none
    unnamed x16, waiting for transfers between devices: 15.2 us -> 36.5 us
  transfers between devices with their start and end apart: 32 -> 33, of which waited for: 17 -> 13; matrix products, arithmetic and copies ran while one was open for 17% -> 21% of each run, Pallas kernels for 8% -> 10%
where the time goes in v2:
time: 733 us; the launch traced here: 727 us
  waiting for transfers between devices  246 us (34%)
  blocking collectives  124 us (17%)
  matrix products  77.6 us (11%)
  Pallas kernels  71.5 us (10%)
  other arithmetic  70.3 us (10%)
  local copies, waits for them, and re-layouts  68.9 us (9%)
  starting transfers between devices  52.6 us (7%)
  between operations  15.4 us (2%)
    pallas_call x2, Pallas kernels, attention_call(): pl.pallas_call(kernel, name=name, grid=(seq_count, pair_count), in_specs=...  71.5 us
    all_gather x1, waiting for transfers between devices, gather_rows(): return lax.all_gather(block_values, 'tensor', axis=0, tiled=True)  70.4 us
    reduce_scatter x1, waiting for transfers between devices, scatter_rows(): lax.psum_scatter(term_fn(jnp.int32(0), row_total * lax.axis_size('tensor'...  61.1 us
    psum x1, blocking collectives, on_device(): lax.psum(jnp.stack([gain_one_grad, shift_one_grad, query_shift_grad, valu...  52.1 us
    unnamed x16, waiting for transfers between devices  36.5 us
    ppermute x3, waiting for transfers between devices, line_step(): above.append(lax.ppermute(above[-1], axis_name, downward))  31.1 us
    unnamed x106, local copies, waits for them, and re-layouts  29.4 us
    dot_general x5, matrix products, times_transpose(): lax.dot_general(left_rows, right_rows, (((1,), (1,)), ((), ())), preferre...  26.9 us
  transfers between devices with their start and end apart: 33, of which 13 were waited for; matrix products, arithmetic and copies ran while one was open for 21% of the time, Pallas kernels for 10%

profile of v2, /device:TPU:0, one launch (start us, length us, event | category | flops | bytes accessed | tf_op | source)
XLA Modules:
  0.0 726.8 jit_solution(16027452343089296979)
XLA Ops:
  11.0 5.4 concatenate.44
  16.5 9.9 %all_to_all.24 = bf16[4,33,768]{2,1,0:T(8,128)(2,1)S(1)} all-to-all(bf16[4,33,768]{2,1,0:T(8,128)(2,1)S(1)} %pad_maximum_fusion.1), channel_id=1, replica_groups=mesh['fsdp'=2,'heads'=4,'tensor'=4] {'heads'}, dimensions={0} | all-to-all | bytes 405504 | tf_op jit(solution)/shard_map/all_to_all | solution.py:413
  27.2 15.7 %all_gather.22 = bf16[128,1024]{1,0:T(8,128)(2,1)} all-gather(bf16[32,1024]{1,0:T(8,128)(2,1)S(1)} %copy-done.32), channel_id=1, replica_groups=mesh['fsdp'=2,'heads'=4,'tensor'=4] {'tensor'}, dimensions={0}, use_global_device_ids=true | all-gather | bytes 327680 | tf_op jit(solution)/shard_map/all_gather | solution.py:430
  46.9 5.6 collective-permute-start.2
  52.4 12.6 %collective-permute-done = bf16[1,1,2,256,1024]{4,3,2,1,0:T(8,128)(2,1)} collective-permute-done((bf16[1,1,2,256,1024]{4,3,2,1,0:T(8,128)(2,1)S(1)}, bf16[1,1,2,256,1024]{4,3,2,1,0:T(8,128)(2,1)}, u32[]{:S(2)}, u32[]{:S(2)}) %collective-permute-start) | collective-permute-done | bytes 1048608 | tf_op jit(solution)/shard_map/ppermute | solution.py:96
  67.0 17.2 %collective-permute-done.3 = bf16[2,256,1024]{2,1,0:T(8,128)(2,1)} collective-permute-done((bf16[2,256,1024]{2,1,0:T(8,128)(2,1)}, bf16[2,256,1024]{2,1,0:T(8,128)(2,1)}, u32[]{:S(2)}, u32[]{:S(2)}) %collective-permute-start.3) | collective-permute-done | bytes 1048608 | tf_op jit(solution)/shard_map/ppermute | solution.py:128
  85.5 5.5 collective-permute-start.4
  94.7 13.9 %collective-permute-done.5 = bf16[2,256,1024]{2,1,0:T(8,128)(2,1)} collective-permute-done((bf16[2,256,1024]{2,1,0:T(8,128)(2,1)}, bf16[2,256,1024]{2,1,0:T(8,128)(2,1)}, u32[]{:S(2)}, u32[]{:S(2)}) %collective-permute-start.5) | collective-permute-done | bytes 1048608 | tf_op jit(solution)/shard_map/ppermute | solution.py:128
  109.9 6.0 collective-permute-start.6
  116.0 3.5 reshape.478
  125.8 3.4 fusion.61
  129.2 4.0 multiply_reduce_fusion
  138.3 3.6 add_convert_fusion.1
  142.0 25.2 %attend_forward.1 = bf16[4,2,256,256]{3,2,1,0:T(8,128)(2,1)} custom-call(bf16[4,2,256,768]{3,2,1,0:T(8,128)(2,1)S(1)} %bitcast.176, f32[1024,128]{1,0:T(8,128)S(1)} %copy.81.cosine_ref, f32[1024,128]{1,0:T(8,128)S(1)} %copy.82.sine_ref), custom_call_target="tpu_custom_call" | custom-call | flops 4294967296 | bytes 8388608 | tf_op jit(solution)/shard_map/attend_forward/pallas_call | solution.py:269
  168.9 3.6 all-to-all-start.1
  173.8 15.0 %all-to-all-done.1 = bf16[4,2,256,256]{3,2,1,0:T(8,128)(2,1)S(1)} async-done(((bf16[4,2,256,256]{3,2,1,0:T(8,128)(2,1)}), bf16[4,2,256,256]{3,2,1,0:T(8,128)(2,1)S(1)}, u32[]{:S(2)}, u32[]{:S(2)}) %all-to-all-start.1) | async-done | bytes 1048608 | tf_op jit(solution)/shard_map/all_to_all | solution.py:468
  189.9 3.2 convolution_add_fusion
  195.6 3.8 all-gather.12.cloned.1.call-done
  211.8 70.4 %all-gather.14.cloned.1.call-done = bf16[8,256,1024]{2,1,0:T(8,128)(2,1)} async-done(((bf16[2,256,1024]{2,1,0:T(8,128)(2,1)}), bf16[8,256,1024]{2,1,0:T(8,128)(2,1)}) %all-gather.14.cloned.1.call-update) | async-done | bytes 4194320 | tf_op jit(solution)/shard_map/all_gather | solution.py:77
  282.2 5.5 fusion.67
  287.7 7.5 %fusion.62 = (bf16[2048]{0:T(1024)(128)(2,1)S(1)}, bf16[2048]{0:T(1024)(128)(2,1)S(1)}, f32[2048,684]{0,1:T(8,128)}, f32[2048,684]{0,1:T(8,128)}) fusion(f32[684]{0:T(1024)S(1)} %fusion.59, f32[684]{0:T(1024)S(1)} %convert_element_type.398, f32[2048,684]{0,1:T(8,128)S(1)} %fusion.67, f32[684]{0:T(1024)S(1)} %convert_element_type.397, ...), kind=kOutput, calls=%fused_computation.178 | convolution fusion | flops 2884308992 | bytes 22421520 | tf_op jit(solution)/shard_map/dot_general | solution.py:306
  295.3 9.3 %psum.49 = bf16[2,2048]{1,0:T(2,128)(2,1)S(1)} all-reduce(bf16[2,2048]{1,0:T(2,128)(2,1)S(1)} %pad_maximum_fusion.3), channel_id=1, replica_groups=mesh['fsdp'=2,'heads'=4,'tensor'=4] {'tensor'}, use_global_device_ids=true, to_apply=%region_6.7 | all-reduce | flops 4096 | bytes 16384 | tf_op jit(solution)/shard_map/psum | solution.py:81
  307.5 10.7 %multiply_reduce_fusion.1 = (f32[684]{0:T(1024)S(1)}, bf16[2048]{0:T(1024)(128)(2,1)S(1)}, bf16[2048]{0:T(1024)(128)(2,1)S(1)}, f32[684]{0:T(1024)S(1)}, f32[2048,684]{0,1:T(8,128)}) fusion(f32[2048,684]{0,1:T(8,128)} %get-tuple-element.80, f32[2048]{0:T(1024)S(1)} %add_rsqrt_fusion, f32[2048]{0:T(1024)S(1)} %bitcast.208, f32[684]{0:T(1024)S(1)} %fusion.59, ...), kind=kOutput, calls=%fused_computation.9 | convolution fusion | flops 2882906624 | bytes 16837312 | tf_op jit(solution)/shard_map/dot_general | solution.py:71
  318.3 11.9 %psum.50 = bf16[2,2048]{1,0:T(2,128)(2,1)S(1)} all-reduce(bf16[2,2048]{1,0:T(2,128)(2,1)S(1)} %pad_maximum_fusion.4), channel_id=1, replica_groups=mesh['fsdp'=2,'heads'=4,'tensor'=4] {'tensor'}, use_global_device_ids=true, to_apply=%region_9.10 | all-reduce | flops 4096 | bytes 16384 | tf_op jit(solution)/shard_map/psum | solution.py:81
  330.2 12.0 %convert_reduce_fusion.1 = (f32[684]{0:T(1024)S(1)}, bf16[2048,684]{0,1:T(8,128)(2,1)}, f32[684]{0:T(1024)S(1)}, bf16[2048,684]{0,1:T(8,128)(2,1)}, bf16[2048,684]{0,1:T(8,128)(2,1)S(1)}) fusion(f32[2048,684]{0,1:T(8,128)} %copy-done.16, f32[684]{0:T(1024)S(1)} %convert_element_type.397, f32[2048]{0:T(1024)S(1)} %bitcast.211, f32[2048]{0:T(1024)S(1)} %add_rsqrt_fusion, ...), kind=kLoop, calls=%fused_computation.10 | loop fusion | flops 46226088 | bytes 30870224 | tf_op jit(solution)/shard_map/reduce_sum | solution.py:341
  348.9 35.3 %reduce-scatter.22.cloned.1.call-done = bf16[128,684]{1,0:T(8,128)(2,1)} async-done(((bf16[1024,684]{1,0:T(8,128)(2,1)}), bf16[128,684]{1,0:T(8,128)(2,1)}) %reduce-scatter.22.cloned.1.call-update) | async-done | bytes 175120
  386.0 5.9 fusion.68
  391.9 5.3 add_convert_fusion
  397.3 6.2 convolution_convert_fusion.4
  405.3 6.2 convolution_convert_fusion.5
  413.1 61.1 %reduce-scatter.14.cloned.1.call-done = bf16[2,256,1024]{2,1,0:T(8,128)(2,1)} async-done(((bf16[8,256,1024]{2,1,0:T(8,128)(2,1)}), bf16[2,256,1024]{2,1,0:T(8,128)(2,1)}) %reduce-scatter.14.cloned.1.call-update) | async-done | bytes 1048592 | tf_op jit(solution)/shard_map/reduce_scatter | solution.py:164
  481.9 3.5 all-to-all-start.2
  485.5 7.1 convolution_convert_fusion
  495.7 4.3 collective-permute-start.8
  507.3 46.3 %attend_backward.1 = bf16[4,2,256,768]{3,2,1,0:T(8,128)(2,1)S(1)} custom-call(bf16[4,2,256,768]{3,2,1,0:T(8,128)(2,1)} %bitcast.177, bf16[4,2,256,256]{3,2,1,0:T(8,128)(2,1)S(1)} %copy-done.1, f32[1024,128]{1,0:T(8,128)S(1)} %copy-done.5, f32[1024,128]{1,0:T(8,128)S(1)} %copy-done.3), custom_call_target="tpu_custom_call" | custom-call | flops 10737418240 | bytes 8388608 | tf_op jit(solution)/shard_map/attend_backward/pallas_call | solution.py:269
  553.6 3.7 convolution_convert_fusion.1
  565.2 5.5 collective-permute-start.9
  570.8 25.6 %all-reduce.1 = (f32[684]{0:T(1024)}, f32[684]{0:T(1024)}, f32[684]{0:T(1024)}, f32[684]{0:T(1024)}) all-reduce(f32[684]{0:T(1024)S(1)} %get-tuple-element.83, f32[684]{0:T(1024)S(1)} %get-tuple-element.71, f32[684]{0:T(1024)S(1)} %get-tuple-element.45, ...), channel_id=1, replica_groups=mesh['fsdp'=2,'heads'=4,'tensor'=4] {'fsdp','heads'}, use_global_device_ids=true, to_apply=%region_31.32 | all-reduce | flops 2736 | bytes 21888 | tf_op jit(solution)/shard_map/psum | solution.py:539
  600.8 5.8 convolution_convert_fusion.3
  609.5 4.8 fusion.28
  615.8 4.5 convert_add_fusion
  627.8 4.1 collective-permute-start.10
  631.8 9.9 %collective-permute-done.12 = bf16[2,256,1024]{2,1,0:T(8,128)(2,1)} collective-permute-done((bf16[2,256,1024]{2,1,0:T(8,128)(2,1)}, bf16[2,256,1024]{2,1,0:T(8,128)(2,1)}, u32[]{:S(2)}, u32[]{:S(2)}) %collective-permute-start.12) | collective-permute-done | bytes 1048608 | tf_op jit(solution)/shard_map/ppermute | solution.py:159
  647.8 4.5 fusion.18
  652.4 52.1 %psum.51 = f32[8,1024]{1,0:T(8,128)S(1)} all-reduce(f32[8,1024]{1,0:T(8,128)S(1)} %stack.108), channel_id=1, replica_groups=mesh['fsdp'=2,'heads'=4,'tensor'=4] {'fsdp','heads','tensor'}, use_global_device_ids=true, to_apply=%region_25.26 | all-reduce | flops 8192 | bytes 65536 | tf_op jit(solution)/shard_map/psum | solution.py:591
  704.6 3.6 all-to-all-start.3
  708.1 3.9 fusion.17
  716.4 3.6 fusion.33
  (283 shorter events, 114.3 us)
Async XLA Ops:
  7.2 20.0 %copy-start.32 = (bf16[32,1024]{1,0:T(8,128)(2,1)S(1)}, bf16[32,1024]{1,0:T(8,128)(2,1)}, u32[]{:S(2)}) copy-start(bf16[32,1024]{1,0:T(8,128)(2,1)} %param.32) | copy-start | bytes 196612
  7.2 35.9 %copy-start.9 = (bf16[2,256,1024]{2,1,0:T(8,128)(2,1)S(1)}, bf16[2,256,1024]{2,1,0:T(8,128)(2,1)}, u32[]{:S(2)}) copy-start(bf16[2,256,1024]{2,1,0:T(8,128)(2,1)} %param.22) | copy-start | bytes 3145732
  7.2 36.4 %copy-start.44 = (s32[2]{0:T(128)S(1)}, s32[2]{0:T(128)}, u32[]{:S(2)}) copy-start(s32[2]{0:T(128)} %param.23) | copy-start | bytes 28
  7.2 36.4 %copy-start.12 = (bf16[2,256,1024]{2,1,0:T(8,128)(2,1)S(1)}, bf16[2,256,1024]{2,1,0:T(8,128)(2,1)}, u32[]{:S(2)}) copy-start(bf16[2,256,1024]{2,1,0:T(8,128)(2,1)} %param.24) | copy-start | bytes 3145732
  7.2 108.7 %all-gather.18.cloned.1.call-start = ((), (), s32[]{:S(2)}) async-start(), calls=%async_computation.20 | async-start | bytes 1880064 | tf_op jit(solution)/shard_map/all_gather | solution.py:416
  27.2 162.7 %all-gather.8.cloned.1.call-start = ((), (), s32[]{:S(2)}) async-start(), calls=%async_computation.11 | async-start | bytes 2359296 | tf_op jit(solution)/shard_map/all_gather | solution.py:429
  43.0 152.6 %all-gather.10.cloned.1.call-start = ((), (), s32[]{:S(2)}) async-start(), calls=%async_computation.12 | async-start | bytes 1585152 | tf_op jit(solution)/shard_map/all_gather | solution.py:439
  43.1 22.0 %collective-permute-start = (bf16[1,1,2,256,1024]{4,3,2,1,0:T(8,128)(2,1)S(1)}, bf16[1,1,2,256,1024]{4,3,2,1,0:T(8,128)(2,1)}, u32[]{:S(2)}, u32[]{:S(2)}) collective-permute-start(bf16[1,1,2,256,1024]{4,3,2,1,0:T(8,128)(2,1)S(1)} %bitcast.178), channel_id=1, source_target_pairs={{0,8},{4,12},{8,0},{12,4},{1,9},{5,13},{9,1},{13,5},{2,10},{6,14},... | collective-permute-start | bytes 3145736 | tf_op jit(solution)/shard_map/ppermute | solution.py:96
  45.6 38.6 %collective-permute-start.3 = (bf16[2,256,1024]{2,1,0:T(8,128)(2,1)}, bf16[2,256,1024]{2,1,0:T(8,128)(2,1)}, u32[]{:S(2)}, u32[]{:S(2)}) collective-permute-start(bf16[2,256,1024]{2,1,0:T(8,128)(2,1)} %get-tuple-element.76), channel_id=1, source_target_pairs={{1,0},{2,1},{3,2},{5,4},{6,5},{7,6},{9,8},{10,9},{11,10},{13,12},{... | collective-permute-start | bytes 3145736 | tf_op jit(solution)/shard_map/ppermute | solution.py:128
  46.9 38.6 %collective-permute-start.2 = (bf16[2,256,1024]{2,1,0:T(8,128)(2,1)}, bf16[2,256,1024]{2,1,0:T(8,128)(2,1)}, u32[]{:S(2)}, u32[]{:S(2)}) collective-permute-start(bf16[2,256,1024]{2,1,0:T(8,128)(2,1)} %get-tuple-element.76), channel_id=1, source_target_pairs={{0,1},{1,2},{2,3},{4,5},{5,6},{6,7},{8,9},{9,10},{10,11},{12,13},{... | collective-permute-start | bytes 3145736 | tf_op jit(solution)/shard_map/ppermute | solution.py:127
  66.9 58.9 %collective-permute-start.1 = (bf16[2,1,2,256,1024]{4,3,2,1,0:T(8,128)(2,1)S(1)}, bf16[2,1,2,256,1024]{4,3,2,1,0:T(8,128)(2,1)}, u32[]{:S(2)}, u32[]{:S(2)}) collective-permute-start(bf16[2,1,2,256,1024]{4,3,2,1,0:T(8,128)(2,1)S(1)} %maximum_select_fusion.1), channel_id=1, source_target_pairs={{0,4},{4,0},{8,12},{12,8},{1,5},{5,1},{9,13},{13,9},{2,6},{6,2},{1... | collective-permute-start | bytes 6291464 | tf_op jit(solution)/shard_map/ppermute | solution.py:96
  84.2 24.4 %collective-permute-start.5 = (bf16[2,256,1024]{2,1,0:T(8,128)(2,1)}, bf16[2,256,1024]{2,1,0:T(8,128)(2,1)}, u32[]{:S(2)}, u32[]{:S(2)}) collective-permute-start(bf16[2,256,1024]{2,1,0:T(8,128)(2,1)} %collective-permute-done.3), channel_id=1, source_target_pairs={{1,0},{2,1},{3,2},{5,4},{6,5},{7,6},{9,8},{10,9},{11,10},{13,12},{... | collective-permute-start | bytes 3145736 | tf_op jit(solution)/shard_map/ppermute | solution.py:128
  85.5 24.3 %collective-permute-start.4 = (bf16[2,256,1024]{2,1,0:T(8,128)(2,1)}, bf16[2,256,1024]{2,1,0:T(8,128)(2,1)}, u32[]{:S(2)}, u32[]{:S(2)}) collective-permute-start(bf16[2,256,1024]{2,1,0:T(8,128)(2,1)} %collective-permute-done.2), channel_id=1, source_target_pairs={{0,1},{1,2},{2,3},{4,5},{5,6},{6,7},{8,9},{9,10},{10,11},{12,13},{... | collective-permute-start | bytes 3145736 | tf_op jit(solution)/shard_map/ppermute | solution.py:127
  92.2 49.7 %copy-start.2 = (f32[1024,128]{1,0:T(8,128)}, f32[1024,128]{1,0:T(8,128)S(1)}, u32[]{:S(2)}) copy-start(f32[1024,128]{1,0:T(8,128)S(1)} %copy.82.sine_ref) | copy-start | bytes 1572868
  94.6 47.4 %copy-start.4 = (f32[1024,128]{1,0:T(8,128)}, f32[1024,128]{1,0:T(8,128)S(1)}, u32[]{:S(2)}) copy-start(f32[1024,128]{1,0:T(8,128)S(1)} %copy.81.cosine_ref) | copy-start | bytes 1572868
  108.6 65.2 %collective-permute-start.7 = (bf16[2,256,1024]{2,1,0:T(8,128)(2,1)}, bf16[2,256,1024]{2,1,0:T(8,128)(2,1)}, u32[]{:S(2)}, u32[]{:S(2)}) collective-permute-start(bf16[2,256,1024]{2,1,0:T(8,128)(2,1)} %collective-permute-done.5), channel_id=1, source_target_pairs={{1,0},{2,1},{3,2},{5,4},{6,5},{7,6},{9,8},{10,9},{11,10},{13,12},{... | collective-permute-start | bytes 3145736 | tf_op jit(solution)/shard_map/ppermute | solution.py:128
  109.9 63.9 %collective-permute-start.6 = (bf16[2,256,1024]{2,1,0:T(8,128)(2,1)}, bf16[2,256,1024]{2,1,0:T(8,128)(2,1)}, u32[]{:S(2)}, u32[]{:S(2)}) collective-permute-start(bf16[2,256,1024]{2,1,0:T(8,128)(2,1)} %collective-permute-done.4), channel_id=1, source_target_pairs={{0,1},{1,2},{2,3},{4,5},{5,6},{6,7},{8,9},{9,10},{10,11},{12,13},{... | collective-permute-start | bytes 3145736 | tf_op jit(solution)/shard_map/ppermute | solution.py:127
  125.3 10.9 %copy-start.30 = (f32[1024]{0:T(1024)}, f32[1024]{0:T(1024)S(1)}, u32[]{:S(2)}) copy-start(f32[1024]{0:T(1024)S(1)} %reshape.457) | copy-start | bytes 12292
  168.9 19.9 %all-to-all-start.1 = ((bf16[4,2,256,256]{3,2,1,0:T(8,128)(2,1)}), bf16[4,2,256,256]{3,2,1,0:T(8,128)(2,1)S(1)}, u32[]{:S(2)}, u32[]{:S(2)}) async-start(bf16[4,2,256,256]{3,2,1,0:T(8,128)(2,1)} %attend_forward.1), calls=%async_computation.1 | async-start | bytes 2097152 | tf_op jit(solution)/shard_map/all_to_all | solution.py:468
  172.6 26.9 %all-gather.12.cloned.1.call-start = ((), (), s32[]{:S(2)}) async-start(), calls=%async_computation.13 | async-start | bytes 1585152 | tf_op jit(solution)/shard_map/all_gather | solution.py:440
  173.1 109.1 %all-gather.14.cloned.1.call-start = ((), (), s32[]{:S(2)}) async-start(), calls=%async_computation.14 | async-start | bytes 5242880 | tf_op jit(solution)/shard_map/all_gather | solution.py:77
  193.8 282.7 %copy-start.7 = (f32[2,256,1024]{2,1,0:T(8,128)}, f32[2,256,1024]{2,1,0:T(8,128)S(1)}, u32[]{:S(2)}) copy-start(f32[2,256,1024]{2,1,0:T(8,128)S(1)} %get-tuple-element.82) | copy-start | bytes 6291460
  199.5 108.0 %all-gather.16.cloned.1.call-start = ((), (), s32[]{:S(2)}) async-start(), calls=%async_computation.15 | async-start | bytes 1585152 | tf_op jit(solution)/shard_map/all_gather | solution.py:441
  200.1 184.2 %reduce-scatter.22.cloned.1.call-start = ((), (), s32[]{:S(2)}) async-start(), calls=%async_computation.21 | async-start | bytes 1769472
  330.2 13.6 %copy-start.18 = (bf16[4,2,256,1024]{3,2,1,0:T(8,128)(2,1)S(1)}, bf16[4,2,256,1024]{3,2,1,0:T(8,128)(2,1)}, u32[]{:S(2)}) copy-start(bf16[4,2,256,1024]{3,2,1,0:T(8,128)(2,1)} %constant_dynamic-slice_fusion.1) | copy-start | bytes 12582916
  348.5 125.7 %reduce-scatter.14.cloned.1.call-start = ((), (), s32[]{:S(2)}) async-start(), calls=%async_computation.16 | async-start | bytes 5242880 | tf_op jit(solution)/shard_map/reduce_scatter | solution.py:164
  397.2 199.8 %reduce-scatter.26.cloned.1.call-start = ((), (), s32[]{:S(2)}) async-start(), calls=%async_computation.23 | async-start | bytes 1769472
  405.1 193.9 %reduce-scatter.24.cloned.1.call-start = ((), (), s32[]{:S(2)}) async-start(), calls=%async_computation.22 | async-start | bytes 1769472
  413.1 63.5 %copy-start.13 = (bf16[2,256,1024]{2,1,0:T(8,128)(2,1)S(1)}, bf16[2,256,1024]{2,1,0:T(8,128)(2,1)}, u32[]{:S(2)}) copy-start(bf16[2,256,1024]{2,1,0:T(8,128)(2,1)} %param.24) | copy-start | bytes 3145732
  481.9 21.1 %all-to-all-start.2 = ((bf16[4,2,256,256]{3,2,1,0:T(8,128)(2,1)}), bf16[4,2,256,256]{3,2,1,0:T(8,128)(2,1)S(1)}, u32[]{:S(2)}, u32[]{:S(2)}) async-start(bf16[4,2,256,256]{3,2,1,0:T(8,128)(2,1)} %bitcast.173), calls=%async_computation.3 | async-start | bytes 2097152 | tf_op jit(solution)/shard_map/all_to_all | solution.py:550
  485.4 137.6 %reduce-scatter.18.cloned.1.call-start = ((), (), s32[]{:S(2)}) async-start(), calls=%async_computation.18 | async-start | bytes 2359296 | tf_op jit(solution)/shard_map/reduce_scatter | solution.py:619
  495.7 66.6 %collective-permute-start.8 = (bf16[2,256,1024]{2,1,0:T(8,128)(2,1)}, bf16[2,256,1024]{2,1,0:T(8,128)(2,1)}, u32[]{:S(2)}, u32[]{:S(2)}) collective-permute-start(bf16[2,256,1024]{2,1,0:T(8,128)(2,1)} %get-tuple-element.38), channel_id=1, source_target_pairs={{0,1},{1,2},{2,3},{4,5},{5,6},{6,7},{8,9},{9,10},{10,11},{12,13},{... | collective-permute-start | bytes 3145736 | tf_op jit(solution)/shard_map/ppermute | solution.py:159
  502.7 143.6 %reduce-scatter.20.cloned.1.call-start = ((), (), s32[]{:S(2)}) async-start(), calls=%async_computation.19 | async-start | bytes 327680 | tf_op jit(solution)/shard_map/reduce_scatter | solution.py:618
  507.3 46.3 %copy-start.24 = (bf16[2,4,4,32,768]{4,3,2,1,0:T(8,128)(2,1)S(1)}, bf16[2,4,4,32,768]{4,3,2,1,0:T(8,128)(2,1)}, u32[]{:S(2)}) copy-start(bf16[2,4,4,32,768]{4,3,2,1,0:T(8,128)(2,1)} %copy.80) | copy-start | bytes 4718596
  559.3 37.0 %copy-start.29 = (bf16[684,128]{1,0:T(8,128)(2,1)S(1)}, bf16[684,128]{1,0:T(8,128)(2,1)}, u32[]{:S(2)}) copy-start(bf16[684,128]{1,0:T(8,128)(2,1)} %copy.94) | copy-start | bytes 525316
  560.8 55.0 %collective-permute-start.14 = (bf16[2,2,256,1024]{3,2,1,0:T(8,128)(2,1)}, bf16[2,2,256,1024]{3,2,1,0:T(8,128)(2,1)}, u32[]{:S(2)}, u32[]{:S(2)}) collective-permute-start(bf16[2,2,256,1024]{3,2,1,0:T(8,128)(2,1)} %dynamic-slice_bitcast_fusion), channel_id=1, source_target_pairs={{0,4},{4,0},{8,12},{12,8},{1,5},{5,1},{9,13},{13,9},{2,6},{6,2},{1... | collective-permute-start | bytes 6291464 | tf_op jit(solution)/shard_map/ppermute | solution.py:115
  561.0 48.5 %collective-permute-start.11 = (bf16[2,256,1024]{2,1,0:T(8,128)(2,1)}, bf16[2,256,1024]{2,1,0:T(8,128)(2,1)}, u32[]{:S(2)}, u32[]{:S(2)}) collective-permute-start(bf16[2,256,1024]{2,1,0:T(8,128)(2,1)} %get-tuple-element.41), channel_id=1, source_target_pairs={{1,0},{2,1},{3,2},{5,4},{6,5},{7,6},{9,8},{10,9},{11,10},{13,12},{... | collective-permute-start | bytes 3145736 | tf_op jit(solution)/shard_map/ppermute | solution.py:159
  565.2 44.2 %collective-permute-start.9 = (bf16[2,256,1024]{2,1,0:T(8,128)(2,1)}, bf16[2,256,1024]{2,1,0:T(8,128)(2,1)}, u32[]{:S(2)}, u32[]{:S(2)}) collective-permute-start(bf16[2,256,1024]{2,1,0:T(8,128)(2,1)} %fusion.27), channel_id=1, source_target_pairs={{0,1},{1,2},{2,3},{4,5},{5,6},{6,7},{8,9},{9,10},{10,11},{12,13},{... | collective-permute-start | bytes 3145736 | tf_op jit(solution)/shard_map/ppermute | solution.py:159
  608.9 16.4 %collective-permute-start.16 = (bf16[512,768]{1,0:T(8,128)(2,1)}, bf16[512,768]{1,0:T(8,128)(2,1)}, u32[]{:S(2)}, u32[]{:S(2)}) collective-permute-start(bf16[512,768]{1,0:T(8,128)(2,1)} %dynamic-slice_bitcast_fusion.3), channel_id=1, source_target_pairs={{0,16},{16,0},{1,17},{17,1},{2,18},{18,2},{3,19},{19,3},{4,20},{20... | collective-permute-start | bytes 2359304 | tf_op jit(solution)/shard_map/ppermute | solution.py:115
  614.3 27.4 %collective-permute-start.12 = (bf16[2,256,1024]{2,1,0:T(8,128)(2,1)}, bf16[2,256,1024]{2,1,0:T(8,128)(2,1)}, u32[]{:S(2)}, u32[]{:S(2)}) collective-permute-start(bf16[2,256,1024]{2,1,0:T(8,128)(2,1)} %get-tuple-element.42), channel_id=1, source_target_pairs={{1,0},{2,1},{3,2},{5,4},{6,5},{7,6},{9,8},{10,9},{11,10},{13,12},{... | collective-permute-start | bytes 3145736 | tf_op jit(solution)/shard_map/ppermute | solution.py:159
  623.0 24.8 %collective-permute-start.15 = (bf16[2,256,1024]{2,1,0:T(8,128)(2,1)}, bf16[2,256,1024]{2,1,0:T(8,128)(2,1)}, u32[]{:S(2)}, u32[]{:S(2)}) collective-permute-start(bf16[2,256,1024]{2,1,0:T(8,128)(2,1)} %fusion.36), channel_id=1, source_target_pairs={{0,8},{4,12},{8,0},{12,4},{1,9},{5,13},{9,1},{13,5},{2,10},{6,14},... | collective-permute-start | bytes 3145736 | tf_op jit(solution)/shard_map/ppermute | solution.py:115
  623.1 81.5 %reduce-scatter.16.cloned.1.call-start = ((), (), s32[]{:S(2)}) async-start(), calls=%async_computation.17 | async-start | bytes 983040 | tf_op jit(solution)/shard_map/reduce_scatter | solution.py:576
  623.6 24.2 %copy-start.11 = (bf16[2,256,1024]{2,1,0:T(8,128)(2,1)S(1)}, bf16[2,256,1024]{2,1,0:T(8,128)(2,1)}, u32[]{:S(2)}) copy-start(bf16[2,256,1024]{2,1,0:T(8,128)(2,1)} %param.22) | copy-start | bytes 3145732
  623.6 24.2 %copy-start.31 = (f32[1024]{0:T(1024)S(1)}, f32[1024]{0:T(1024)}, u32[]{:S(2)}) copy-start(f32[1024]{0:T(1024)} %copy-done.30) | copy-start | bytes 12292
  627.8 88.6 %collective-permute-start.10 = (bf16[2,256,1024]{2,1,0:T(8,128)(2,1)}, bf16[2,256,1024]{2,1,0:T(8,128)(2,1)}, u32[]{:S(2)}, u32[]{:S(2)}) collective-permute-start(bf16[2,256,1024]{2,1,0:T(8,128)(2,1)} %get-tuple-element.40), channel_id=1, source_target_pairs={{0,1},{1,2},{2,3},{4,5},{5,6},{6,7},{8,9},{9,10},{10,11},{12,13},{... | collective-permute-start | bytes 3145736 | tf_op jit(solution)/shard_map/ppermute | solution.py:159
  644.7 71.7 %collective-permute-start.13 = (bf16[2,256,1024]{2,1,0:T(8,128)(2,1)}, bf16[2,256,1024]{2,1,0:T(8,128)(2,1)}, u32[]{:S(2)}, u32[]{:S(2)}) collective-permute-start(bf16[2,256,1024]{2,1,0:T(8,128)(2,1)} %fusion.26), channel_id=1, source_target_pairs={{1,0},{2,1},{3,2},{5,4},{6,5},{7,6},{9,8},{10,9},{11,10},{13,12},{... | collective-permute-start | bytes 3145736 | tf_op jit(solution)/shard_map/ppermute | solution.py:159
  647.8 60.4 %copy-start.8 = (f32[2,256,1024]{2,1,0:T(8,128)S(1)}, f32[2,256,1024]{2,1,0:T(8,128)}, u32[]{:S(2)}) copy-start(f32[2,256,1024]{2,1,0:T(8,128)} %copy-done.7) | copy-start | bytes 6291460
  704.6 8.9 %all-to-all-start.3 = ((bf16[4,32,768]{2,1,0:T(8,128)(2,1)}), bf16[4,32,768]{2,1,0:T(8,128)(2,1)S(1)}, u32[]{:S(2)}, u32[]{:S(2)}) async-start(bf16[4,32,768]{2,1,0:T(8,128)(2,1)} %bitcast.205), calls=%async_computation.5 | async-start | bytes 393216 | tf_op jit(solution)/shard_map/all_to_all | solution.py:611
  (30 other events, 120.3 us)
Sparse Core Ops, SparseCore 0:
  27.3 53.2 all-gather.17
  82.5 29.0 all-gather.7
  113.5 25.0 all-gather.9
  174.9 24.4 all-gather.11
  201.4 80.7 all-gather.13
  283.9 23.5 all-gather.15
  348.6 35.5 reduce-scatter.21
  397.4 76.7 reduce-scatter.13
  477.5 38.8 reduce-scatter.25
  519.5 38.3 reduce-scatter.23
  561.2 41.2 reduce-scatter.17
  623.2 23.0 reduce-scatter.19
  648.6 29.7 reduce-scatter.15

commit v3 on v2

--- a/solution.py
+++ b/solution.py
@@ -381,8 +381,6 @@
     grad_flags = slot_flag.astype(jnp.float32)[:, None, None]
     grad_total = grad_flags * cotangent.astype(jnp.float32)
     grad_branch = grad_total.astype(jnp.bfloat16)
-    below, above = [grad_branch], [grad_branch]
-    line_step(below, above, "tensor")
     stacked = jnp.stack(
         [
             member.reshape(row_part, head_ways, group_pairs, PAIR)
@@ -420,6 +418,9 @@
         fsdp_ways, tensor_ways, head_ways, row_part + 1, 3 * group_width
     ).transpose(0, 2, 1, 3, 4)
     qkv_part = columns[:, :, :, :row_part].reshape(width, 3 * group_width)
+    gated_branch = after(grad_branch, columns)
+    below, above = [gated_branch], [gated_branch]
+    line_step(below, above, "tensor")
     gathered = (
         columns[:, :, :, row_part, : vectors.shape[0]]
         .reshape(-1, 8, row_part)
@@ -453,8 +454,6 @@
 
     query_lanes, value_lanes = group_lanes(query_shift), group_lanes(value_shift)
     qkv_shift = jnp.stack([query_lanes, jnp.zeros_like(query_lanes), value_lanes], axis=1)
-    low_one = after(low_one, below[-1], above[-1])
-    line_step(below, above, "tensor")
     qkv_lin = (
         (jnp.dot(low_one, qkv_part, preferred_element_type=jnp.float32) + qkv_shift.reshape(-1))
         .astype(jnp.bfloat16)
@@ -465,8 +464,9 @@
     for _ in range(tensor_ways - 3):
         line_step(below, above, "tensor")
     mixed_heads = attend_forward(attended, tables)
+    below[-1], above[-1] = after(below[-1], mixed_heads), after(above[-1], mixed_heads)
+    line_step(below, above, "tensor")
     mixed_parts = lax.all_to_all(mixed_heads, "heads", split_axis=0, concat_axis=0, tiled=True)
-    mixed_parts = after(mixed_parts, below[-1], above[-1])
     grad_rows = line_pick(below, above, "tensor").reshape(-1, width)
     mixed_flat = mixed_parts.transpose(1, 2, 0, 3).reshape(token_count, width)
     residual = inputs_f + (
@@ -477,7 +477,7 @@
     flag_rows = slot_flag.astype(jnp.float32)[:, None, None]
     down_shift_grad = jnp.sum(grad_branch.reshape(token_count, width), axis=0, dtype=jnp.float32)
     ffn_local = gate_part.shape[1]
-    token_rows3 = gather_rows(after(low_two, gate_part, up_part))
+    token_rows3 = gather_rows(after(low_two, gate_part, up_part, below[-1], above[-1]))
     token_rows = token_rows3.reshape(-1, width)
     col_index = lax.axis_index("tensor") * ffn_local + jnp.arange(ffn_local, dtype=jnp.int32)
     unit_mask = (col_index < FF_REAL).astype(jnp.float32)
@@ -506,7 +506,7 @@
     down_weight_grad = lax.psum_scatter(
         down_grad.astype(jnp.bfloat16), ("fsdp", "heads"), scatter_dimension=1, tiled=True
     )
-    grad_normed = times_transpose(grad_rows, down_part)
+    grad_normed = times_transpose(after(grad_rows, down_grad), down_part)
     scaled, scaled_sum, cross_sum = hidden_backward_terms(
         grad_normed, unit_hidden, inner_scale, unit_mask
     )
@@ -539,6 +539,7 @@
     gate_bias_grad, up_bias_grad, inner_gain_grad, inner_shift_grad = lax.psum(
         (vector_grads[0], vector_grads[1], vector_grads[2], vector_grads[3]), ("fsdp", "heads")
     )
+    grad_normed_two = after(grad_normed_two, gate_bias_grad)
     grad_residual = grad_total + norm_backward(grad_normed_two, unit_two, inv_two, gain_two)
     gain_two_grad = jnp.sum((grad_normed_two * unit_two).reshape(token_count, width), axis=0)
     shift_two_grad = jnp.sum(grad_normed_two.reshape(token_count, width), axis=0)
@@ -563,17 +564,6 @@
     grad_normed_one = cube_scatter(
         group_terms.reshape((head_ways,) + inputs.shape), "heads"
     )
-    qkv_weight_part = (
-        outer_product(low_one, qkv_grad)
-        .astype(jnp.bfloat16)
-        .reshape(fsdp_ways, head_ways, tensor_ways, row_part, 3 * group_width)
-        .transpose(0, 2, 1, 3, 4)
-        .reshape(width, 3 * group_width)
-    )
-    qkv_half = cube_scatter(
-        qkv_weight_part.reshape(fsdp_ways, -1, 3 * group_width), "fsdp"
-    ).astype(jnp.bfloat16)
-    qkv_rows = lax.psum_scatter(qkv_half, "tensor", scatter_dimension=0, tiled=True)
     qkv_shift_grad = jnp.sum(qkv_grad, axis=0, dtype=jnp.float32).reshape(group_pairs, 3, PAIR)
 
     def place_lanes(own_lanes):
@@ -588,43 +578,58 @@
     ).astype(jnp.bfloat16)
     gain_one_grad = jnp.sum((grad_normed_one * unit_one).reshape(token_count, width), axis=0)
     shift_one_grad = jnp.sum(grad_normed_one.reshape(token_count, width), axis=0)
-    vector_sums_all = lax.psum(
-        jnp.stack(
-            [
-                gain_one_grad,
-                shift_one_grad,
-                query_shift_grad,
-                value_shift_grad,
-                out_shift_grad,
-                gain_two_grad,
-                shift_two_grad,
-                down_shift_grad,
-            ]
-        ),
-        ("fsdp", "heads", "tensor"),
-    )
-    device_place = (
-        lax.axis_index("fsdp") * head_ways + group_index
-    ) * tensor_ways + lax.axis_index("tensor")
-    own_sums = lax.dynamic_slice_in_dim(vector_sums_all, device_place * row_part, row_part, 1)
-    qkv_rows = after(qkv_rows, own_sums)
-    qkv_columns = lax.all_to_all(qkv_rows, "heads", split_axis=0, concat_axis=0, tiled=True)
+    vector_terms = jnp.stack(
+        [
+            gain_one_grad,
+            shift_one_grad,
+            query_shift_grad,
+            value_shift_grad,
+            out_shift_grad,
+            gain_two_grad,
+            shift_two_grad,
+            down_shift_grad,
+        ]
+    )
+    vector_lanes = vector_terms.shape[0] * row_part
+    vector_rows = (
+        vector_terms.reshape(-1, fsdp_ways, head_ways, tensor_ways, row_part)
+        .transpose(1, 3, 2, 0, 4)
+        .reshape(fsdp_ways, tensor_ways, head_ways, 1, vector_lanes)
+    )
+    extra_rows = 1
+    while head_ways * (row_part + extra_rows) % 16 != 0:
+        extra_rows += 1
+    vector_rows = jnp.pad(
+        vector_rows,
+        ((0, 0),) * 3 + ((0, extra_rows - 1), (0, 3 * group_width - vector_lanes)),
+    )
+    qkv_terms = outer_product(low_one, qkv_grad).astype(jnp.bfloat16)
+    qkv_terms = qkv_terms.reshape(
+        fsdp_ways, head_ways, tensor_ways, row_part, 3 * group_width
+    ).transpose(0, 2, 1, 3, 4)
+    qkv_terms = jnp.concatenate([qkv_terms, vector_rows.astype(jnp.bfloat16)], axis=3)
+    qkv_half = cube_scatter(
+        qkv_terms.reshape(fsdp_ways, -1, 3 * group_width), "fsdp"
+    ).astype(jnp.bfloat16)
+    qkv_rows = lax.psum_scatter(qkv_half, "tensor", scatter_dimension=0, tiled=True)
+    qkv_columns = lax.all_to_all(
+        qkv_rows, "heads", split_axis=0, concat_axis=0, tiled=True
+    ).reshape(head_ways, row_part + extra_rows, 3 * group_width)
     qkv_weight_grads = (
-        qkv_columns.reshape(head_ways, row_part, group_pairs, 3, PAIR)
+        qkv_columns[:, :row_part]
+        .reshape(head_ways, row_part, group_pairs, 3, PAIR)
         .transpose(3, 1, 0, 2, 4)
         .reshape(3, row_part, width)
         .astype(jnp.float32)
     )
+    own_sums = jnp.sum(
+        qkv_columns[:, row_part, :vector_lanes].astype(jnp.float32), axis=0
+    ).reshape(-1, row_part)
+    out_terms = out_weight_part.astype(jnp.bfloat16).reshape(fsdp_ways, -1, width)
+    out_half = cube_scatter(out_terms, "fsdp").astype(jnp.bfloat16)
+    out_eighth = cube_scatter(out_half.reshape(head_ways, -1, width), "heads")
     out_weight_grad = lax.psum_scatter(
-        lax.psum_scatter(
-            out_weight_part.astype(jnp.bfloat16),
-            ("fsdp", "heads"),
-            scatter_dimension=0,
-            tiled=True,
-        ),
-        "tensor",
-        scatter_dimension=0,
-        tiled=True,
+        out_eighth.astype(jnp.bfloat16), "tensor", scatter_dimension=0, tiled=True
     ).astype(jnp.float32)
     attn_sums = tuple(qkv_weight_grads) + (out_weight_grad,) + tuple(own_sums)
     return (

time: 733 us -> 714 us (0.974)
  blocking collectives: 124 us -> 70.2 us
  other arithmetic: 70.3 us -> 82 us
  waiting for transfers between devices: 246 us -> 256 us
    psum x1 -> x0, blocking collectives: 52.1 us -> none  [on_device(): lax.psum(jnp.stack([gain_one_grad, shift_one_grad, query_shift_grad, valu...]
    reduce_scatter x1, waiting for transfers between devices: 0.01 us -> 21.4 us  [on_device(): lax.psum_scatter(qkv_half, 'tensor', scatter_dimension=0, tiled=True)]
    ppermute x3 -> x6, waiting for transfers between devices: 1.59 us -> 22.3 us  [cube_scatter(): lax.ppermute(sent.astype(jnp.bfloat16), axis_name, cube_pairs(ways, bit))]
    ppermute x3, waiting for transfers between devices: 0.01 us -> 19.5 us  [line_step(): below.append(lax.ppermute(below[-1], axis_name, upward))]
    reduce_scatter x1, waiting for transfers between devices: 61.1 us -> 42.8 us  [scatter_rows(): lax.psum_scatter(term_fn(jnp.int32(0), row_total * lax.axis_size('tensor'...]
    ppermute x3, waiting for transfers between devices: 31.1 us -> 16.1 us  [line_step(): above.append(lax.ppermute(above[-1], axis_name, downward))]
    unnamed x16 -> x15, waiting for transfers between devices: 36.5 us -> 24.3 us
    all_to_all x1, waiting for transfers between devices: 15 us -> 6 us  [on_device(): lax.all_to_all(mixed_heads, 'heads', split_axis=0, concat_axis=0, tiled=T...]
  transfers between devices with their start and end apart: 33 -> 35, of which waited for: 13 -> 20; matrix products, arithmetic and copies ran while one was open for 21% -> 26% of each run, Pallas kernels for 10% -> 10%
where the time goes in v3:
time: 714 us; the launch traced here: 707 us
  waiting for transfers between devices  256 us (36%)
  other arithmetic  82 us (11%)
  matrix products  77.4 us (11%)
  local copies, waits for them, and re-layouts  75.4 us (11%)
  Pallas kernels  71.5 us (10%)
  blocking collectives  70.2 us (10%)
  starting transfers between devices  58.9 us (8%)
  between operations  16 us (2%)
    pallas_call x2, Pallas kernels, attention_call(): pl.pallas_call(kernel, name=name, grid=(seq_count, pair_count), in_specs=...  71.5 us
    all_gather x1, waiting for transfers between devices, gather_rows(): return lax.all_gather(block_values, 'tensor', axis=0, tiled=True)  68.1 us
    reduce_scatter x1, waiting for transfers between devices, scatter_rows(): lax.psum_scatter(term_fn(jnp.int32(0), row_total * lax.axis_size('tensor'...  42.8 us
    unnamed x134, local copies, waits for them, and re-layouts  32.7 us
    dot_general x5, matrix products, times_transpose(): lax.dot_general(left_rows, right_rows, (((1,), (1,)), ((), ())), preferre...  27.6 us
    psum x1, blocking collectives, on_device(): lax.psum((vector_grads[0], vector_grads[1], vector_grads[2], vector_grads...  25.6 us
    unnamed x15, waiting for transfers between devices  24.3 us
    dot_general x5, matrix products, outer_product(): lax.dot_general(left_rows, right_rows, (((0,), (0,)), ((), ())), preferre...  22.3 us
  transfers between devices with their start and end apart: 35, of which 20 were waited for; matrix products, arithmetic and copies ran while one was open for 26% of the time, Pallas kernels for 10%

profile of v3, /device:TPU:0, one launch (start us, length us, event | category | flops | bytes accessed | tf_op | source)
XLA Modules:
  0.0 707.4 jit_solution(15312286596223155766)
XLA Ops:
  10.9 5.4 concatenate.49
  16.4 9.9 %all_to_all.24 = bf16[4,33,768]{2,1,0:T(8,128)(2,1)S(1)} all-to-all(bf16[4,33,768]{2,1,0:T(8,128)(2,1)S(1)} %pad_maximum_fusion.1), channel_id=1, replica_groups=mesh['fsdp'=2,'heads'=4,'tensor'=4] {'heads'}, dimensions={0} | all-to-all | bytes 405504 | tf_op jit(solution)/shard_map/all_to_all | solution.py:411
  27.2 15.7 %all_gather.22 = bf16[128,1024]{1,0:T(8,128)(2,1)} all-gather(bf16[32,1024]{1,0:T(8,128)(2,1)S(1)} %copy-done.36), channel_id=1, replica_groups=mesh['fsdp'=2,'heads'=4,'tensor'=4] {'tensor'}, dimensions={0}, use_global_device_ids=true | all-gather | bytes 327680 | tf_op jit(solution)/shard_map/all_gather | solution.py:431
  43.5 21.4 %collective-permute-done = bf16[1,1,2,256,1024]{4,3,2,1,0:T(8,128)(2,1)} collective-permute-done((bf16[1,1,2,256,1024]{4,3,2,1,0:T(8,128)(2,1)S(1)}, bf16[1,1,2,256,1024]{4,3,2,1,0:T(8,128)(2,1)}, u32[]{:S(2)}, u32[]{:S(2)}) %collective-permute-start) | collective-permute-done | bytes 1048608 | tf_op jit(solution)/shard_map/ppermute | solution.py:96
  81.5 6.0 collective-permute-start.2
  95.8 4.0 fusion.2
  99.8 4.2 fusion.5
  104.0 3.6 add_convert_fusion.1
  109.5 25.2 %attend_forward.1 = bf16[4,2,256,256]{3,2,1,0:T(8,128)(2,1)} custom-call(bf16[4,2,256,768]{3,2,1,0:T(8,128)(2,1)S(1)} %bitcast.166, f32[1024,128]{1,0:T(8,128)S(1)} %copy.85.cosine_ref, f32[1024,128]{1,0:T(8,128)S(1)} %copy.86.sine_ref), custom_call_target="tpu_custom_call" | custom-call | flops 4294967296 | bytes 8388608 | tf_op jit(solution)/shard_map/attend_forward/pallas_call | solution.py:269
  136.4 3.6 all-to-all-start.1
  141.9 6.0 collective-permute-start.4
  148.4 6.0 all-to-all-done.1
  158.7 10.4 %collective-permute-done.6 = bf16[2,256,1024]{2,1,0:T(8,128)(2,1)} collective-permute-done((bf16[2,256,1024]{2,1,0:T(8,128)(2,1)}, bf16[2,256,1024]{2,1,0:T(8,128)(2,1)}, u32[]{:S(2)}, u32[]{:S(2)}) %collective-permute-start.6) | collective-permute-done | bytes 1048608 | tf_op jit(solution)/shard_map/ppermute | solution.py:128
  170.3 5.4 collective-permute-start.5
  180.0 17.2 %collective-permute-done.5 = bf16[2,256,1024]{2,1,0:T(8,128)(2,1)} collective-permute-done((bf16[2,256,1024]{2,1,0:T(8,128)(2,1)}, bf16[2,256,1024]{2,1,0:T(8,128)(2,1)}, u32[]{:S(2)}, u32[]{:S(2)}) %collective-permute-start.5) | collective-permute-done | bytes 1048608 | tf_op jit(solution)/shard_map/ppermute | solution.py:127
  197.2 5.1 collective-permute-done.7
  215.0 68.1 %all-gather.14.cloned.1.call-done = bf16[8,256,1024]{2,1,0:T(8,128)(2,1)} async-done(((bf16[2,256,1024]{2,1,0:T(8,128)(2,1)}), bf16[8,256,1024]{2,1,0:T(8,128)(2,1)}) %all-gather.14.cloned.1.call-update) | async-done | bytes 4194320 | tf_op jit(solution)/shard_map/all_gather | solution.py:77
  283.1 5.5 fusion.67
  288.6 7.6 %fusion.59 = (bf16[2048]{0:T(1024)(128)(2,1)S(1)}, bf16[2048]{0:T(1024)(128)(2,1)S(1)}, f32[2048,684]{0,1:T(8,128)}, f32[2048,684]{0,1:T(8,128)}) fusion(f32[684]{0:T(1024)S(1)} %fusion.57, f32[684]{0:T(1024)S(1)} %convert_element_type.456, f32[2048,684]{0,1:T(8,128)S(1)} %fusion.67, f32[684]{0:T(1024)S(1)} %convert_element_type.455, ...), kind=kOutput, calls=%fused_computation.186 | convolution fusion | flops 2884308992 | bytes 22421520 | tf_op jit(solution)/shard_map/dot_general | solution.py:306
  296.3 9.1 %psum.42 = bf16[2,2048]{1,0:T(2,128)(2,1)S(1)} all-reduce(bf16[2,2048]{1,0:T(2,128)(2,1)S(1)} %pad_maximum_fusion.3), channel_id=1, replica_groups=mesh['fsdp'=2,'heads'=4,'tensor'=4] {'tensor'}, use_global_device_ids=true, to_apply=%region_6.7 | all-reduce | flops 4096 | bytes 16384 | tf_op jit(solution)/shard_map/psum | solution.py:81
  305.5 3.7 multiply_convert_fusion.2
  315.3 11.4 %multiply_reduce_fusion = (f32[684]{0:T(1024)}, bf16[2048]{0:T(1024)(128)(2,1)S(1)}, bf16[2048]{0:T(1024)(128)(2,1)S(1)}, f32[684]{0:T(1024)}, f32[2048,684]{0,1:T(8,128)}) fusion(f32[2048,684]{0,1:T(8,128)} %get-tuple-element.84, f32[2048]{0:T(1024)S(1)} %add_rsqrt_fusion, f32[2048]{0:T(1024)S(1)} %bitcast.209, f32[684]{0:T(1024)S(1)} %fusion.57, ...), kind=kOutput, calls=%fused_computation.12 | convolution fusion | flops 2882906624 | bytes 16837312 | tf_op jit(solution)/shard_map/dot_general | solution.py:71
  326.8 9.9 %psum.43 = bf16[2,2048]{1,0:T(2,128)(2,1)S(1)} all-reduce(bf16[2,2048]{1,0:T(2,128)(2,1)S(1)} %pad_maximum_fusion.4), channel_id=1, replica_groups=mesh['fsdp'=2,'heads'=4,'tensor'=4] {'tensor'}, use_global_device_ids=true, to_apply=%region_9.10 | all-reduce | flops 4096 | bytes 16384 | tf_op jit(solution)/shard_map/psum | solution.py:81
  337.0 13.5 %convert_reduce_fusion.2 = (f32[684]{0:T(1024)}, bf16[2048,684]{0,1:T(8,128)(2,1)}, f32[684]{0:T(1024)}, bf16[2048,684]{0,1:T(8,128)(2,1)}) fusion(f32[2048,684]{0,1:T(8,128)} %copy-done.19, f32[684]{0:T(1024)S(1)} %convert_element_type.455, f32[2048]{0:T(1024)S(1)} %bitcast.212, f32[2048]{0:T(1024)S(1)} %add_rsqrt_fusion, ...), kind=kLoop, calls=%fused_computation.13 | loop fusion | flops 40622760 | bytes 28065824 | tf_op jit(solution)/shard_map/reduce_sum | solution.py:341
  350.5 23.1 %reduce-scatter.19.cloned.1.call-done = bf16[128,684]{1,0:T(8,128)(2,1)} async-done(((bf16[1024,684]{1,0:T(8,128)(2,1)}), bf16[128,684]{1,0:T(8,128)(2,1)}) %reduce-scatter.19.cloned.1.call-update) | async-done | bytes 175120
  375.3 5.9 fusion.69
  381.3 5.3 add_convert_fusion
  387.4 6.2 convolution_convert_fusion.4
  395.2 25.6 %all-reduce.2 = (f32[684]{0:T(1024)}, f32[684]{0:T(1024)}, f32[684]{0:T(1024)}, f32[684]{0:T(1024)}) all-reduce(f32[684]{0:T(1024)S(1)} %copy-done.39, f32[684]{0:T(1024)S(1)} %copy-done.38, f32[684]{0:T(1024)S(1)} %copy-done.44, f32[684]{0:T(1024)S(1)} %copy-done.45), channel_id=1, replica_groups=mesh['fsdp'=2,'heads'=4,'tensor'=4] {'fsdp','heads'}, use_global_device_ids=true, to_apply=%region_13.14 | all-reduce | flops 2736 | bytes 21888 | tf_op jit(solution)/shard_map/psum | solution.py:539
  420.8 42.8 %reduce-scatter.13.cloned.1.call-done = bf16[2,256,1024]{2,1,0:T(8,128)(2,1)} async-done(((bf16[8,256,1024]{2,1,0:T(8,128)(2,1)}), bf16[2,256,1024]{2,1,0:T(8,128)(2,1)}) %reduce-scatter.13.cloned.1.call-update) | async-done | bytes 1048592 | tf_op jit(solution)/shard_map/reduce_scatter | solution.py:164
  472.3 3.5 all-to-all-start.2
  475.9 6.4 convolution_convert_fusion.5
  484.2 7.6 %convolution_convert_fusion = bf16[2048,1024]{1,0:T(8,128)(2,1)} fusion(bf16[2048,684]{0,1:T(8,128)(2,1)} %copy-done.25, bf16[684,1024]{1,0:T(8,128)(2,1)} %all-gather.16.cloned.1.call-done), kind=kOutput, calls=%fused_computation.28 | convolution fusion | flops 2871001088 | bytes 8396800 | tf_op jit(solution)/shard_map/dot_general | solution.py:501
  496.1 46.3 %attend_backward.1 = bf16[4,2,256,768]{3,2,1,0:T(8,128)(2,1)S(1)} custom-call(bf16[4,2,256,768]{3,2,1,0:T(8,128)(2,1)} %bitcast.167, bf16[4,2,256,256]{3,2,1,0:T(8,128)(2,1)S(1)} %copy-done.1, f32[1024,128]{1,0:T(8,128)S(1)} %copy-done.5, f32[1024,128]{1,0:T(8,128)S(1)} %copy-done.3), custom_call_target="tpu_custom_call" | custom-call | flops 10737418240 | bytes 8388608 | tf_op jit(solution)/shard_map/attend_backward/pallas_call | solution.py:269
  542.5 3.7 convolution_convert_fusion.1
  559.2 4.3 collective-permute-start.8
  565.1 3.6 convolution_convert_fusion.3
  578.3 5.1 collective-permute-done.17
  588.6 5.7 collective-permute-start.9
  595.5 6.2 collective-permute-done.15
  601.6 3.5 fusion.16
  615.2 3.9 fusion.22
  621.2 11.0 %collective-permute-done.16 = bf16[576,768]{1,0:T(8,128)(2,1)} collective-permute-done((bf16[576,768]{1,0:T(8,128)(2,1)}, bf16[576,768]{1,0:T(8,128)(2,1)}, u32[]{:S(2)}, u32[]{:S(2)}) %collective-permute-start.16) | collective-permute-done | bytes 884768 | tf_op jit(solution)/shard_map/ppermute | solution.py:115
  634.5 5.1 collective-permute-start.10
  639.6 10.1 %collective-permute-done.12 = bf16[2,256,1024]{2,1,0:T(8,128)(2,1)} collective-permute-done((bf16[2,256,1024]{2,1,0:T(8,128)(2,1)}, bf16[2,256,1024]{2,1,0:T(8,128)(2,1)}, u32[]{:S(2)}, u32[]{:S(2)}) %collective-permute-start.12) | collective-permute-done | bytes 1048608 | tf_op jit(solution)/shard_map/ppermute | solution.py:159
  660.1 4.1 fusion.15
  664.2 21.4 %reduce-scatter.15.cloned.1.call-done = bf16[144,768]{1,0:T(8,128)(2,1)} async-done(((bf16[576,768]{1,0:T(8,128)(2,1)}), bf16[144,768]{1,0:T(8,128)(2,1)}) %reduce-scatter.15.cloned.1.call-update) | async-done | bytes 221200 | tf_op jit(solution)/shard_map/reduce_scatter | solution.py:614
  692.4 3.6 fusion.27
  (333 shorter events, 149.3 us)
Async XLA Ops:
  7.2 20.0 %copy-start.36 = (bf16[32,1024]{1,0:T(8,128)(2,1)S(1)}, bf16[32,1024]{1,0:T(8,128)(2,1)}, u32[]{:S(2)}) copy-start(bf16[32,1024]{1,0:T(8,128)(2,1)} %param.32) | copy-start | bytes 196612
  7.2 35.8 %copy-start.10 = (bf16[2,256,1024]{2,1,0:T(8,128)(2,1)S(1)}, bf16[2,256,1024]{2,1,0:T(8,128)(2,1)}, u32[]{:S(2)}) copy-start(bf16[2,256,1024]{2,1,0:T(8,128)(2,1)} %param.22) | copy-start | bytes 3145732
  7.2 66.7 %all-gather.18.cloned.1.call-start = ((), (), s32[]{:S(2)}) async-start(), calls=%async_computation.18 | async-start | bytes 1880064 | tf_op jit(solution)/shard_map/all_gather | solution.py:414
  26.3 40.6 %copy-start.54 = (s32[2]{0:T(128)S(1)}, s32[2]{0:T(128)}, u32[]{:S(2)}) copy-start(s32[2]{0:T(128)} %param.23) | copy-start | bytes 28
  27.1 128.4 %all-gather.8.cloned.1.call-start = ((), (), s32[]{:S(2)}) async-start(), calls=%async_computation.10 | async-start | bytes 2359296 | tf_op jit(solution)/shard_map/all_gather | solution.py:430
  42.9 137.1 %all-gather.10.cloned.1.call-start = ((), (), s32[]{:S(2)}) async-start(), calls=%async_computation.11 | async-start | bytes 1585152 | tf_op jit(solution)/shard_map/all_gather | solution.py:440
  43.0 22.0 %collective-permute-start = (bf16[1,1,2,256,1024]{4,3,2,1,0:T(8,128)(2,1)S(1)}, bf16[1,1,2,256,1024]{4,3,2,1,0:T(8,128)(2,1)}, u32[]{:S(2)}, u32[]{:S(2)}) collective-permute-start(bf16[1,1,2,256,1024]{4,3,2,1,0:T(8,128)(2,1)S(1)} %bitcast.168), channel_id=1, source_target_pairs={{0,8},{4,12},{8,0},{12,4},{1,9},{5,13},{9,1},{13,5},{2,10},{6,14},... | collective-permute-start | bytes 3145736 | tf_op jit(solution)/shard_map/ppermute | solution.py:96
  66.9 25.5 %collective-permute-start.1 = (bf16[2,1,2,256,1024]{4,3,2,1,0:T(8,128)(2,1)S(1)}, bf16[2,1,2,256,1024]{4,3,2,1,0:T(8,128)(2,1)}, u32[]{:S(2)}, u32[]{:S(2)}) collective-permute-start(bf16[2,1,2,256,1024]{4,3,2,1,0:T(8,128)(2,1)S(1)} %maximum_select_fusion.1), channel_id=1, source_target_pairs={{0,4},{4,0},{8,12},{12,8},{1,5},{5,1},{9,13},{13,9},{2,6},{6,2},{1... | collective-permute-start | bytes 6291464 | tf_op jit(solution)/shard_map/ppermute | solution.py:96
  68.1 41.3 %copy-start.2 = (f32[1024,128]{1,0:T(8,128)}, f32[1024,128]{1,0:T(8,128)S(1)}, u32[]{:S(2)}) copy-start(f32[1024,128]{1,0:T(8,128)S(1)} %copy.86.sine_ref) | copy-start | bytes 1572868
  70.5 39.0 %copy-start.4 = (f32[1024,128]{1,0:T(8,128)}, f32[1024,128]{1,0:T(8,128)S(1)}, u32[]{:S(2)}) copy-start(f32[1024,128]{1,0:T(8,128)S(1)} %copy.85.cosine_ref) | copy-start | bytes 1572868
  80.2 28.0 %collective-permute-start.3 = (bf16[2,256,1024]{2,1,0:T(8,128)(2,1)}, bf16[2,256,1024]{2,1,0:T(8,128)(2,1)}, u32[]{:S(2)}, u32[]{:S(2)}) collective-permute-start(bf16[2,256,1024]{2,1,0:T(8,128)(2,1)} %get-tuple-element.35), channel_id=1, source_target_pairs={{1,0},{2,1},{3,2},{5,4},{6,5},{7,6},{9,8},{10,9},{11,10},{13,12},{... | collective-permute-start | bytes 3145736 | tf_op jit(solution)/shard_map/ppermute | solution.py:128
  81.5 27.9 %collective-permute-start.2 = (bf16[2,256,1024]{2,1,0:T(8,128)(2,1)}, bf16[2,256,1024]{2,1,0:T(8,128)(2,1)}, u32[]{:S(2)}, u32[]{:S(2)}) collective-permute-start(bf16[2,256,1024]{2,1,0:T(8,128)(2,1)} %get-tuple-element.35), channel_id=1, source_target_pairs={{0,1},{1,2},{2,3},{4,5},{5,6},{6,7},{8,9},{9,10},{10,11},{12,13},{... | collective-permute-start | bytes 3145736 | tf_op jit(solution)/shard_map/ppermute | solution.py:127
  136.4 18.1 %all-to-all-start.1 = ((bf16[4,2,256,256]{3,2,1,0:T(8,128)(2,1)}), bf16[4,2,256,256]{3,2,1,0:T(8,128)(2,1)S(1)}, u32[]{:S(2)}, u32[]{:S(2)}) async-start(bf16[4,2,256,256]{3,2,1,0:T(8,128)(2,1)} %attend_forward.1), calls=%async_computation.1 | async-start | bytes 2097152 | tf_op jit(solution)/shard_map/all_to_all | solution.py:469
  140.0 40.0 %all-gather.12.cloned.1.call-start = ((), (), s32[]{:S(2)}) async-start(), calls=%async_computation.12 | async-start | bytes 1585152 | tf_op jit(solution)/shard_map/all_gather | solution.py:441
  140.6 142.5 %all-gather.14.cloned.1.call-start = ((), (), s32[]{:S(2)}) async-start(), calls=%async_computation.13 | async-start | bytes 5242880 | tf_op jit(solution)/shard_map/all_gather | solution.py:77
  140.6 28.5 %collective-permute-start.6 = (bf16[2,256,1024]{2,1,0:T(8,128)(2,1)}, bf16[2,256,1024]{2,1,0:T(8,128)(2,1)}, u32[]{:S(2)}, u32[]{:S(2)}) collective-permute-start(bf16[2,256,1024]{2,1,0:T(8,128)(2,1)} %collective-permute-done.3), channel_id=1, source_target_pairs={{1,0},{2,1},{3,2},{5,4},{6,5},{7,6},{9,8},{10,9},{11,10},{13,12},{... | collective-permute-start | bytes 3145736 | tf_op jit(solution)/shard_map/ppermute | solution.py:128
  141.9 28.4 %collective-permute-start.4 = (bf16[2,256,1024]{2,1,0:T(8,128)(2,1)}, bf16[2,256,1024]{2,1,0:T(8,128)(2,1)}, u32[]{:S(2)}, u32[]{:S(2)}) collective-permute-start(bf16[2,256,1024]{2,1,0:T(8,128)(2,1)} %collective-permute-done.2), channel_id=1, source_target_pairs={{0,1},{1,2},{2,3},{4,5},{5,6},{6,7},{8,9},{9,10},{10,11},{12,13},{... | collective-permute-start | bytes 3145736 | tf_op jit(solution)/shard_map/ppermute | solution.py:127
  170.3 26.9 %collective-permute-start.5 = (bf16[2,256,1024]{2,1,0:T(8,128)(2,1)}, bf16[2,256,1024]{2,1,0:T(8,128)(2,1)}, u32[]{:S(2)}, u32[]{:S(2)}) collective-permute-start(bf16[2,256,1024]{2,1,0:T(8,128)(2,1)} %collective-permute-done.4), channel_id=1, source_target_pairs={{0,1},{1,2},{2,3},{4,5},{5,6},{6,7},{8,9},{9,10},{10,11},{12,13},{... | collective-permute-start | bytes 3145736 | tf_op jit(solution)/shard_map/ppermute | solution.py:127
  175.7 26.6 %collective-permute-start.7 = (bf16[2,256,1024]{2,1,0:T(8,128)(2,1)}, bf16[2,256,1024]{2,1,0:T(8,128)(2,1)}, u32[]{:S(2)}, u32[]{:S(2)}) collective-permute-start(bf16[2,256,1024]{2,1,0:T(8,128)(2,1)} %collective-permute-done.6), channel_id=1, source_target_pairs={{1,0},{2,1},{3,2},{5,4},{6,5},{7,6},{9,8},{10,9},{11,10},{13,12},{... | collective-permute-start | bytes 3145736 | tf_op jit(solution)/shard_map/ppermute | solution.py:128
  178.2 288.0 %copy-start.7 = (f32[2,256,1024]{2,1,0:T(8,128)}, f32[2,256,1024]{2,1,0:T(8,128)S(1)}, u32[]{:S(2)}) copy-start(f32[2,256,1024]{2,1,0:T(8,128)S(1)} %get-tuple-element.86) | copy-start | bytes 6291460
  178.2 24.9 %copy-start.46 = (bf16[684]{0:T(1024)(128)(2,1)S(1)}, bf16[684]{0:T(1024)(128)(2,1)}, u32[]{:S(2)}) copy-start(bf16[684]{0:T(1024)(128)(2,1)} %param.40) | copy-start | bytes 4108
  178.2 24.9 %copy-start.47 = (bf16[684]{0:T(1024)(128)(2,1)S(1)}, bf16[684]{0:T(1024)(128)(2,1)}, u32[]{:S(2)}) copy-start(bf16[684]{0:T(1024)(128)(2,1)} %param.37) | copy-start | bytes 4108
  178.2 24.9 %copy-start.48 = (bf16[684]{0:T(1024)(128)(2,1)S(1)}, bf16[684]{0:T(1024)(128)(2,1)}, u32[]{:S(2)}) copy-start(bf16[684]{0:T(1024)(128)(2,1)} %param.39) | copy-start | bytes 4108
  178.2 24.9 %copy-start.49 = (bf16[684]{0:T(1024)(128)(2,1)S(1)}, bf16[684]{0:T(1024)(128)(2,1)}, u32[]{:S(2)}) copy-start(bf16[684]{0:T(1024)(128)(2,1)} %param.41) | copy-start | bytes 4108
  202.3 113.0 %all-gather.16.cloned.1.call-start = ((), (), s32[]{:S(2)}) async-start(), calls=%async_computation.14 | async-start | bytes 1585152 | tf_op jit(solution)/shard_map/all_gather | solution.py:442
  202.9 170.7 %reduce-scatter.19.cloned.1.call-start = ((), (), s32[]{:S(2)}) async-start(), calls=%async_computation.19 | async-start | bytes 1769472
  336.7 126.8 %reduce-scatter.13.cloned.1.call-start = ((), (), s32[]{:S(2)}) async-start(), calls=%async_computation.15 | async-start | bytes 5242880 | tf_op jit(solution)/shard_map/reduce_scatter | solution.py:164
  386.6 268.3 %reduce-scatter.23.cloned.1.call-start = ((), (), s32[]{:S(2)}) async-start(), calls=%async_computation.21 | async-start | bytes 1769472
  472.3 19.5 %all-to-all-start.2 = ((bf16[4,2,256,256]{3,2,1,0:T(8,128)(2,1)}), bf16[4,2,256,256]{3,2,1,0:T(8,128)(2,1)S(1)}, u32[]{:S(2)}, u32[]{:S(2)}) async-start(bf16[4,2,256,256]{3,2,1,0:T(8,128)(2,1)} %bitcast.162), calls=%async_computation.3 | async-start | bytes 2097152 | tf_op jit(solution)/shard_map/all_to_all | solution.py:551
  475.9 180.9 %reduce-scatter.21.cloned.1.call-start = ((), (), s32[]{:S(2)}) async-start(), calls=%async_computation.20 | async-start | bytes 1769472
  484.0 174.6 %reduce-scatter.17.cloned.1.call-start = ((), (), s32[]{:S(2)}) async-start(), calls=%async_computation.17 | async-start | bytes 327680 | tf_op jit(solution)/shard_map/reduce_scatter | solution.py:631
  496.1 46.3 %copy-start.30 = (bf16[2,4,4,32,768]{4,3,2,1,0:T(8,128)(2,1)S(1)}, bf16[2,4,4,32,768]{4,3,2,1,0:T(8,128)(2,1)}, u32[]{:S(2)}) copy-start(bf16[2,4,4,32,768]{4,3,2,1,0:T(8,128)(2,1)} %copy-done.29) | copy-start | bytes 4718596
  547.7 24.4 %collective-permute-start.14 = (bf16[2,2,256,1024]{3,2,1,0:T(8,128)(2,1)}, bf16[2,2,256,1024]{3,2,1,0:T(8,128)(2,1)}, u32[]{:S(2)}, u32[]{:S(2)}) collective-permute-start(bf16[2,2,256,1024]{3,2,1,0:T(8,128)(2,1)} %dynamic-slice_bitcast_fusion), channel_id=1, source_target_pairs={{0,4},{4,0},{8,12},{12,8},{1,5},{5,1},{9,13},{13,9},{2,6},{6,2},{1... | collective-permute-start | bytes 6291464 | tf_op jit(solution)/shard_map/ppermute | solution.py:115
  557.7 25.8 %collective-permute-start.17 = (bf16[512,1024]{1,0:T(8,128)(2,1)}, bf16[512,1024]{1,0:T(8,128)(2,1)}, u32[]{:S(2)}, u32[]{:S(2)}) collective-permute-start(bf16[512,1024]{1,0:T(8,128)(2,1)} %dynamic-slice_bitcast_fusion.1), channel_id=1, source_target_pairs={{0,16},{16,0},{1,17},{17,1},{2,18},{18,2},{3,19},{19,3},{4,20},{20... | collective-permute-start | bytes 3145736 | tf_op jit(solution)/shard_map/ppermute | solution.py:115
  559.2 26.3 %collective-permute-start.8 = (bf16[2,256,1024]{2,1,0:T(8,128)(2,1)}, bf16[2,256,1024]{2,1,0:T(8,128)(2,1)}, u32[]{:S(2)}, u32[]{:S(2)}) collective-permute-start(bf16[2,256,1024]{2,1,0:T(8,128)(2,1)} %get-tuple-element.43), channel_id=1, source_target_pairs={{0,1},{1,2},{2,3},{4,5},{5,6},{6,7},{8,9},{9,10},{10,11},{12,13},{... | collective-permute-start | bytes 3145736 | tf_op jit(solution)/shard_map/ppermute | solution.py:159
  563.5 50.2 %collective-permute-start.11 = (bf16[2,256,1024]{2,1,0:T(8,128)(2,1)}, bf16[2,256,1024]{2,1,0:T(8,128)(2,1)}, u32[]{:S(2)}, u32[]{:S(2)}) collective-permute-start(bf16[2,256,1024]{2,1,0:T(8,128)(2,1)} %get-tuple-element.46), channel_id=1, source_target_pairs={{1,0},{2,1},{3,2},{5,4},{6,5},{7,6},{9,8},{10,9},{11,10},{13,12},{... | collective-permute-start | bytes 3145736 | tf_op jit(solution)/shard_map/ppermute | solution.py:159
  576.4 25.2 %collective-permute-start.15 = (bf16[2,256,1024]{2,1,0:T(8,128)(2,1)}, bf16[2,256,1024]{2,1,0:T(8,128)(2,1)}, u32[]{:S(2)}, u32[]{:S(2)}) collective-permute-start(bf16[2,256,1024]{2,1,0:T(8,128)(2,1)} %fusion.31), channel_id=1, source_target_pairs={{0,8},{4,12},{8,0},{12,4},{1,9},{5,13},{9,1},{13,5},{2,10},{6,14},... | collective-permute-start | bytes 3145736 | tf_op jit(solution)/shard_map/ppermute | solution.py:115
  585.2 9.1 %collective-permute-start.18 = (bf16[2,128,1024]{2,1,0:T(8,128)(2,1)S(1)}, bf16[2,128,1024]{2,1,0:T(8,128)(2,1)S(1)}, u32[]{:S(2)}, u32[]{:S(2)}) collective-permute-start(bf16[2,128,1024]{2,1,0:T(8,128)(2,1)S(1)} %dynamic-slice_bitcast_fusion.4), channel_id=1, source_target_pairs={{0,4},{4,0},{8,12},{12,8},{1,5},{5,1},{9,13},{13,9},{2,6},{6,2},{1... | collective-permute-start | bytes 1572872 | tf_op jit(solution)/shard_map/ppermute | solution.py:115
  588.6 26.6 %collective-permute-start.9 = (bf16[2,256,1024]{2,1,0:T(8,128)(2,1)}, bf16[2,256,1024]{2,1,0:T(8,128)(2,1)}, u32[]{:S(2)}, u32[]{:S(2)}) collective-permute-start(bf16[2,256,1024]{2,1,0:T(8,128)(2,1)} %fusion.21), channel_id=1, source_target_pairs={{0,1},{1,2},{2,3},{4,5},{5,6},{6,7},{8,9},{9,10},{10,11},{12,13},{... | collective-permute-start | bytes 3145736 | tf_op jit(solution)/shard_map/ppermute | solution.py:159
  611.4 20.8 %collective-permute-start.16 = (bf16[576,768]{1,0:T(8,128)(2,1)}, bf16[576,768]{1,0:T(8,128)(2,1)}, u32[]{:S(2)}, u32[]{:S(2)}) collective-permute-start(bf16[576,768]{1,0:T(8,128)(2,1)} %bitcast.163), channel_id=1, source_target_pairs={{0,16},{16,0},{1,17},{17,1},{2,18},{18,2},{3,19},{19,3},{4,20},{20... | collective-permute-start | bytes 2654216 | tf_op jit(solution)/shard_map/ppermute | solution.py:115
  612.0 8.4 %collective-permute-start.19 = (bf16[128,1024]{1,0:T(8,128)(2,1)S(1)}, bf16[128,1024]{1,0:T(8,128)(2,1)S(1)}, u32[]{:S(2)}, u32[]{:S(2)}) collective-permute-start(bf16[128,1024]{1,0:T(8,128)(2,1)S(1)} %fusion.33), channel_id=1, source_target_pairs={{0,8},{4,12},{8,0},{12,4},{1,9},{5,13},{9,1},{13,5},{2,10},{6,14},... | collective-permute-start | bytes 786440 | tf_op jit(solution)/shard_map/ppermute | solution.py:115
  619.1 30.7 %collective-permute-start.12 = (bf16[2,256,1024]{2,1,0:T(8,128)(2,1)}, bf16[2,256,1024]{2,1,0:T(8,128)(2,1)}, u32[]{:S(2)}, u32[]{:S(2)}) collective-permute-start(bf16[2,256,1024]{2,1,0:T(8,128)(2,1)} %get-tuple-element.47), channel_id=1, source_target_pairs={{1,0},{2,1},{3,2},{5,4},{6,5},{7,6},{9,8},{10,9},{11,10},{13,12},{... | collective-permute-start | bytes 3145736 | tf_op jit(solution)/shard_map/ppermute | solution.py:159
  621.2 64.5 %reduce-scatter.15.cloned.1.call-start = ((), (), s32[]{:S(2)}) async-start(), calls=%async_computation.16 | async-start | bytes 1105920 | tf_op jit(solution)/shard_map/reduce_scatter | solution.py:614
  634.5 19.6 %copy-start.33 = (bf16[684,128]{1,0:T(8,128)(2,1)S(1)}, bf16[684,128]{1,0:T(8,128)(2,1)}, u32[]{:S(2)}) copy-start(bf16[684,128]{1,0:T(8,128)(2,1)} %copy.100) | copy-start | bytes 525316
  634.5 25.6 %copy-start.8 = (f32[2,256,1024]{2,1,0:T(8,128)S(1)}, f32[2,256,1024]{2,1,0:T(8,128)}, u32[]{:S(2)}) copy-start(f32[2,256,1024]{2,1,0:T(8,128)} %copy-done.7) | copy-start | bytes 6291460
  634.5 56.2 %collective-permute-start.10 = (bf16[2,256,1024]{2,1,0:T(8,128)(2,1)}, bf16[2,256,1024]{2,1,0:T(8,128)(2,1)}, u32[]{:S(2)}, u32[]{:S(2)}) collective-permute-start(bf16[2,256,1024]{2,1,0:T(8,128)(2,1)} %get-tuple-element.45), channel_id=1, source_target_pairs={{0,1},{1,2},{2,3},{4,5},{5,6},{6,7},{8,9},{9,10},{10,11},{12,13},{... | collective-permute-start | bytes 3145736 | tf_op jit(solution)/shard_map/ppermute | solution.py:159
  652.8 39.7 %collective-permute-start.13 = (bf16[2,256,1024]{2,1,0:T(8,128)(2,1)}, bf16[2,256,1024]{2,1,0:T(8,128)(2,1)}, u32[]{:S(2)}, u32[]{:S(2)}) collective-permute-start(bf16[2,256,1024]{2,1,0:T(8,128)(2,1)} %fusion.20), channel_id=1, source_target_pairs={{1,0},{2,1},{3,2},{5,4},{6,5},{7,6},{9,8},{10,9},{11,10},{13,12},{... | collective-permute-start | bytes 3145736 | tf_op jit(solution)/shard_map/ppermute | solution.py:159
  687.3 9.2 %all-to-all-start.3 = ((bf16[4,36,768]{2,1,0:T(8,128)(2,1)}), bf16[4,36,768]{2,1,0:T(8,128)(2,1)S(1)}, u32[]{:S(2)}, u32[]{:S(2)}) async-start(bf16[4,36,768]{2,1,0:T(8,128)(2,1)} %all_to_all.18), calls=%async_computation.5 | async-start | bytes 491520 | tf_op jit(solution)/shard_map/all_to_all | solution.py:615
  (42 other events, 235.8 us)
Sparse Core Ops, SparseCore 0:
  27.2 45.7 all-gather.17
  74.9 26.2 all-gather.7
  103.1 25.0 all-gather.9
  142.4 28.0 all-gather.11
  202.4 80.6 all-gather.13
  284.9 23.5 all-gather.15
  336.9 36.7 reduce-scatter.18
  386.7 76.7 reduce-scatter.12
  466.9 38.8 reduce-scatter.22
  508.9 38.3 reduce-scatter.20
  621.3 26.0 reduce-scatter.16
  649.6 35.9 reduce-scatter.14
